TPU v7x, 32 devices: a whole 2x2x4 slice. The times are simulated.
32 devices in a mesh: dp: 4 (over y, x), expert: 8 (over z, core).
Axes of the slice: x: 2, y: 2, z: 4, core: 2. Of those that a mesh axis runs over, the one named last changes fastest.
Arguments:
- tokens: bfloat16 [4096, 2048], P(('dp', 'expert')), may hold values from -6 to 6
- teacher: bfloat16 [4096, 2048], P(('dp', 'expert')), may hold values from -6 to 6
- qkv_weight: bfloat16 [2048, 6144], P('dp'), may hold values from -0.125 to 0.125
- out_weight: bfloat16 [2048, 2048], P('dp'), may hold values from -1 to 1
- query_gain: float32 [128], replicated, may hold values from 0.5 to 1.5
- key_gain: float32 [128], replicated, may hold values from 0.5 to 1.5
- attn_gain: float32 [2048], replicated, may hold values from 0.5 to 1.5
- ffn_gain: float32 [2048], replicated, may hold values from 0.5 to 1.5
- router_weight: bfloat16 [2048, 16], replicated, may hold values from -0.0625 to 0.0625
- gate_up_weight: bfloat16 [16, 2048, 2048], P('expert', 'dp'), may hold values from -0.125 to 0.125
- down_weight: bfloat16 [16, 1024, 2048], P('expert', 'dp'), may hold values from -1.5 to 1.5
- deal: int32 [32], replicated, may hold values from 0 to 31, each once
- routes: int32 [4096, 8], P(('dp', 'expert')), may hold values from 0 to 15, all different within a row; in each aligned block of 128 rows (0 to 127, 128 to 255, ...) at most 128 rows name the same one
- counted: int32 [4096], P(('dp', 'expert')), may hold values from 0 to 1, as said below
- lengths: int32 [32, 4], P(('dp', 'expert')), may hold values from 1 to 64, 128 in all within a row
Outputs:
- output: bfloat16 [4096, 2048], P(('dp', 'expert'))
- mean_loss: float32 [], replicated
- d_tokens: float32 [4096, 2048], P(('dp', 'expert'))
- d_qkv_weight: float32 [2048, 6144], P(('dp', 'expert'))
- d_out_weight: float32 [2048, 2048], P(('dp', 'expert'))
- d_query_gain: float32 [128], replicated
- d_key_gain: float32 [128], replicated
- d_attn_gain: float32 [2048], replicated
- d_ffn_gain: float32 [2048], replicated
- d_router_weight: float32 [2048, 16], replicated
- d_gate_up_weight: float32 [16, 2048, 2048], P('expert', 'dp')
- d_down_weight: float32 [16, 1024, 2048], P('expert', 'dp')
Inputs may be any that keep to these rules, and one draw needn't show every extreme that they name: `routes`: each row names 8 different experts; among the 128 dealt rows of one device no expert is named more than 128 times, and in every draw some expert is named exactly 128 times on some device. Row d holds the lengths of the sequences that fill the block dealt to device d, in order; each row sums to 128 and its largest entry is exactly 64. `counted`: 1 marks a token whose error enters the loss. `deal`: each block number appears once.
All inputs are finite; a program needn't handle non-finite values.
Results may differ from a plain program's by a relative error of at most 0.017.
Values may be sent and summed in bfloat16 or wider, within the bound.
A program may use at most 320 MiB of HBM per device.

v0:
```python
import math

import jax
import jax.numpy as jnp
from jax import lax
from jax.sharding import PartitionSpec as P

H = 16
HD = 128
FFE = 1024


EPS = 1e-06
ROPE_BASE = 50000.0


def rms_scale(values):
    return lax.rsqrt(jnp.mean(values * values, axis=-1, keepdims=True) + EPS)


def rotate(values, cosine, sine_part):
    half_size = values.shape[-1] // 2
    first_half = values[..., :half_size]
    second_half = values[..., half_size:]
    return jnp.concatenate(
        [
            first_half * cosine - second_half * sine_part,
            second_half * cosine + first_half * sine_part,
        ],
        axis=-1,
    )


def unrotate(grad_in, cosine, sine_part):
    half_size = grad_in.shape[-1] // 2
    first_half = grad_in[..., :half_size]
    second_half = grad_in[..., half_size:]
    return jnp.concatenate(
        [
            first_half * cosine + second_half * sine_part,
            second_half * cosine - first_half * sine_part,
        ],
        axis=-1,
    )


def norm_back(grad_in, normed, scale_rows):
    return scale_rows * (grad_in - normed * jnp.mean(grad_in * normed, axis=-1, keepdims=True))


def outer_sum(left, right):
    return lax.dot_general(
        left, right, (((0,), (0,)), ((), ())), preferred_element_type=jnp.float32
    )


def right_dot(left, right):
    return lax.dot_general(
        left, right, (((1,), (1,)), ((), ())), preferred_element_type=jnp.float32
    )


def score_rows(query_low, key_low, same_seq, factor):
    scores = (
        jnp.einsum("thd,shd->hts", query_low, key_low, preferred_element_type=jnp.float32) * factor
    )
    return jnp.where(same_seq, scores, -1e30)


def slot_places(routes, experts, capacity):
    flat_ids = routes.reshape(-1)
    onehot = (flat_ids[:, None] == jnp.arange(experts, dtype=jnp.int32)[None, :]).astype(jnp.int32)
    before = jnp.cumsum(onehot, axis=0) - onehot
    return flat_ids * capacity + jnp.sum(before * onehot, axis=1)


def on_device(
    tokens,
    teacher,
    qkv_weight,
    out_weight,
    query_gain,
    key_gain,
    attn_gain,
    ffn_gain,
    router_weight,
    gate_up_weight,
    down_weight,
    deal,
    routes,
    counted,
    lengths,
):
    tok_rows, model_width = tokens.shape
    head_count = H
    head_size = HD
    hidden = FFE
    slot_count = routes.shape[1]
    experts = router_weight.shape[1]
    local_experts = gate_up_weight.shape[0]
    owners = lax.axis_size("expert")
    devices = lax.axis_size("dp") * owners
    stripe_rows = tok_rows // devices
    capacity = 2 * tok_rows * slot_count // experts
    factor = head_size ** (-0.5)
    given_pieces = (
        tokens.reshape(devices, stripe_rows, model_width)[deal],
        teacher.reshape(devices, stripe_rows, model_width)[deal],
    )
    dealt_tokens, dealt_teacher = (
        lax.all_to_all(given_pieces[0], ("dp", "expert"), split_axis=0, concat_axis=0, tiled=True),
        lax.all_to_all(given_pieces[1], ("dp", "expert"), split_axis=0, concat_axis=0, tiled=True),
    )
    dealt_tokens = dealt_tokens.reshape(tok_rows, model_width)
    dealt_teacher = dealt_teacher.reshape(tok_rows, model_width)
    qkv_full, out_full = (
        lax.all_gather(qkv_weight, "dp", axis=0, tiled=True),
        lax.all_gather(out_weight, "dp", axis=0, tiled=True),
    )
    gate_up_full, down_full = (
        lax.all_gather(gate_up_weight, "dp", axis=1, tiled=True),
        lax.all_gather(down_weight, "dp", axis=1, tiled=True),
    )
    lengths_row = lengths[0]
    seq_ends = jnp.cumsum(lengths_row)
    tok_index = jnp.arange(tok_rows, dtype=jnp.int32)
    passed = (tok_index[:, None] >= seq_ends[None, :]).astype(jnp.int32)
    segment = jnp.sum(passed, axis=1)
    seq_start = jnp.sum(passed * lengths_row[None, :], axis=1)
    inverse = jnp.exp(
        jnp.arange(head_size // 2, dtype=jnp.float32) * (-2.0 * math.log(ROPE_BASE) / head_size)
    )
    angles = (tok_index - seq_start).astype(jnp.float32)[:, None] * inverse[None, :]
    cosine = jnp.cos(angles)[:, None, :]
    sine_part = jnp.sin(angles)[:, None, :]
    same_seq = (segment[:, None] == segment[None, :])[None]
    tokens32 = dealt_tokens.astype(jnp.float32)
    attn_scale = rms_scale(tokens32)
    attn_normed = tokens32 * attn_scale
    attn_low = (attn_normed * attn_gain).astype(jnp.bfloat16)
    qkv = jnp.dot(attn_low, qkv_full, preferred_element_type=jnp.float32)
    queries = qkv[:, :model_width].reshape(tok_rows, head_count, head_size)
    keys_raw = qkv[:, model_width : 2 * model_width].reshape(tok_rows, head_count, head_size)
    values_low = (
        qkv[:, 2 * model_width :].reshape(tok_rows, head_count, head_size).astype(jnp.bfloat16)
    )
    query_scale = rms_scale(queries)
    query_normed = queries * query_scale
    query_low = rotate(query_normed * query_gain, cosine, sine_part).astype(jnp.bfloat16)
    key_scale = rms_scale(keys_raw)
    key_normed = keys_raw * key_scale
    key_low = rotate(key_normed * key_gain, cosine, sine_part).astype(jnp.bfloat16)
    scores = score_rows(query_low, key_low, same_seq, factor)
    row_max = jnp.max(scores, axis=-1, keepdims=True)
    weights = jnp.exp(scores - row_max)
    row_total = jnp.sum(weights, axis=-1, keepdims=True)
    probs_low = (weights / row_total).astype(jnp.bfloat16)
    mixed = jnp.einsum("hts,shd->thd", probs_low, values_low, preferred_element_type=jnp.float32)
    mixed_low = mixed.reshape(tok_rows, model_width).astype(jnp.bfloat16)
    residual = tokens32 + jnp.dot(mixed_low, out_full, preferred_element_type=jnp.float32)
    ffn_scale = rms_scale(residual)
    ffn_normed = residual * ffn_scale
    feed_low = (ffn_normed * ffn_gain).astype(jnp.bfloat16)
    logits = jnp.dot(feed_low, router_weight, preferred_element_type=jnp.float32)
    expert_table = (
        routes[:, :, None] == jnp.arange(experts, dtype=jnp.int32)[None, None, :]
    ).astype(jnp.float32)
    chosen = jnp.einsum("tke,te->tk", expert_table, logits, precision=lax.Precision.HIGHEST)
    gates = jax.nn.softmax(chosen, axis=-1)
    slot_place = slot_places(routes, experts, capacity)
    source_rows = jnp.repeat(feed_low, slot_count, axis=0)
    send = (
        jnp.zeros((experts * capacity, model_width), jnp.bfloat16).at[slot_place].set(source_rows)
    )
    send = send.reshape(owners, local_experts, capacity, model_width)
    arrived_rows = lax.all_to_all(send, "expert", split_axis=0, concat_axis=0, tiled=True)
    gate_up_rows = jnp.einsum(
        "sxcd,xdf->sxcf", arrived_rows, gate_up_full, preferred_element_type=jnp.float32
    )
    inner_low = (jax.nn.silu(gate_up_rows[..., :hidden]) * gate_up_rows[..., hidden:]).astype(
        jnp.bfloat16
    )
    produced = jnp.einsum(
        "sxcf,xfd->sxcd", inner_low, down_full, preferred_element_type=jnp.float32
    ).astype(jnp.bfloat16)
    produced, arrived, gate_up = (produced, arrived_rows, gate_up_rows)
    returned = lax.all_to_all(produced, "expert", split_axis=0, concat_axis=0, tiled=True)
    back_rows = (
        returned.reshape(experts * capacity, model_width)[slot_place]
        .reshape(tok_rows, slot_count, model_width)
        .astype(jnp.float32)
    )
    moe_sum = jnp.sum(gates[:, :, None] * back_rows, axis=1)
    result = residual + moe_sum
    output_low = result.astype(jnp.bfloat16)
    keep_mask = counted.astype(jnp.float32)
    error_rows = result - dealt_teacher.astype(jnp.float32)
    part_square = jnp.sum(keep_mask[:, None] * error_rows * error_rows)
    part_count = jnp.sum(keep_mask)
    total_square, total_count = lax.psum((part_square, part_count), ("dp", "expert"))
    valid_total = jnp.maximum(total_count, 1.0)
    mean_loss = total_square / (valid_total * model_width)
    grad_result = 2.0 * (tok_rows * devices) / valid_total * keep_mask[:, None] * error_rows
    gate_grad = jnp.sum(back_rows * grad_result[:, None, :], axis=2)
    slot_low = (
        (gates[:, :, None] * grad_result[:, None, :])
        .astype(jnp.bfloat16)
        .reshape(tok_rows * slot_count, model_width)
    )
    send_back = (
        jnp.zeros((experts * capacity, model_width), jnp.bfloat16).at[slot_place].set(slot_low)
    )
    send_back = send_back.reshape(owners, local_experts, capacity, model_width)
    grad_arrived = lax.all_to_all(send_back, "expert", split_axis=0, concat_axis=0, tiled=True)
    gate_part = gate_up[..., :hidden]
    up_part = gate_up[..., hidden:]
    sigmoid_gate = jax.nn.sigmoid(gate_part)
    silu_gate = jax.nn.silu(gate_part)
    inner_low = (silu_gate * up_part).astype(jnp.bfloat16)
    grad_inner = jnp.einsum(
        "sxcd,xfd->sxcf", grad_arrived, down_full, preferred_element_type=jnp.float32
    )
    grad_down = jnp.einsum(
        "sxcf,sxcd->xfd", inner_low, grad_arrived, preferred_element_type=jnp.float32
    )
    grad_gate = grad_inner * up_part * sigmoid_gate * (1.0 + gate_part * (1.0 - sigmoid_gate))
    grad_up = grad_inner * silu_gate
    grad_gate_up = jnp.concatenate([grad_gate, grad_up], axis=-1).astype(jnp.bfloat16)
    grad_gate_up_w = jnp.einsum(
        "sxcd,sxcf->xdf", arrived, grad_gate_up, preferred_element_type=jnp.float32
    )
    grad_entry = jnp.einsum(
        "sxcf,xdf->sxcd", grad_gate_up, gate_up_full, preferred_element_type=jnp.float32
    ).astype(jnp.bfloat16)
    grad_returned = lax.all_to_all(grad_entry, "expert", split_axis=0, concat_axis=0, tiled=True)
    grad_slots = (
        grad_returned.reshape(experts * capacity, model_width)[slot_place]
        .reshape(tok_rows, slot_count, model_width)
        .astype(jnp.float32)
    )
    grad_feed = jnp.sum(grad_slots, axis=1)
    grad_chosen = gates * (gate_grad - jnp.sum(gates * gate_grad, axis=1, keepdims=True))
    grad_logits = jnp.einsum(
        "tk,tke->te", grad_chosen, expert_table, precision=lax.Precision.HIGHEST
    )
    feed_wide = feed_low.astype(jnp.float32)
    grad_router = lax.dot_general(
        feed_wide,
        grad_logits,
        (((0,), (0,)), ((), ())),
        precision=lax.Precision.HIGHEST,
        preferred_element_type=jnp.float32,
    )
    grad_feed = grad_feed + lax.dot_general(
        grad_logits,
        router_weight.astype(jnp.float32),
        (((1,), (1,)), ((), ())),
        precision=lax.Precision.HIGHEST,
        preferred_element_type=jnp.float32,
    )
    grad_ffn_gain = jnp.sum(grad_feed * ffn_normed, axis=0)
    grad_resid = grad_result + norm_back(grad_feed * ffn_gain, ffn_normed, ffn_scale)
    grad_attn_low = grad_resid.astype(jnp.bfloat16)
    grad_out_w = outer_sum(mixed_low, grad_attn_low)
    out_grad_part = grad_out_w
    grad_mixed = (
        right_dot(grad_attn_low, out_full)
        .reshape(tok_rows, head_count, head_size)
        .astype(jnp.bfloat16)
    )
    scores = score_rows(query_low, key_low, same_seq, factor)
    probs = jnp.exp(scores - row_max) / row_total
    grad_probs = jnp.einsum(
        "thd,shd->hts", grad_mixed, values_low, preferred_element_type=jnp.float32
    )
    weighted = jnp.sum(probs * grad_probs, axis=-1, keepdims=True)
    grad_scores = (probs * (grad_probs - weighted)).astype(jnp.bfloat16)
    grad_value = jnp.einsum(
        "hts,thd->shd", probs.astype(jnp.bfloat16), grad_mixed, preferred_element_type=jnp.float32
    )
    grad_query = (
        jnp.einsum("hts,shd->thd", grad_scores, key_low, preferred_element_type=jnp.float32)
        * factor
    )
    grad_key = (
        jnp.einsum("hts,thd->shd", grad_scores, query_low, preferred_element_type=jnp.float32)
        * factor
    )
    grad_qn = unrotate(grad_query, cosine, sine_part)
    grad_query_gain = jnp.sum(grad_qn * query_normed, axis=(0, 1))
    grad_q = norm_back(grad_qn * query_gain, query_normed, query_scale)
    grad_kn = unrotate(grad_key, cosine, sine_part)
    grad_key_gain = jnp.sum(grad_kn * key_normed, axis=(0, 1))
    grad_k = norm_back(grad_kn * key_gain, key_normed, key_scale)
    grad_qkv = jnp.concatenate(
        [
            grad_q.reshape(tok_rows, model_width),
            grad_k.reshape(tok_rows, model_width),
            grad_value.reshape(tok_rows, model_width),
        ],
        axis=1,
    ).astype(jnp.bfloat16)
    grad_qkv_w = outer_sum(attn_low, grad_qkv)
    grad_normed = right_dot(grad_qkv, qkv_full)
    grad_attn_gain = jnp.sum(grad_normed * attn_normed, axis=0)
    grad_tokens = grad_resid + norm_back(grad_normed * attn_gain, attn_normed, attn_scale)
    qkv_grad_part, out_grad_part = (
        lax.psum_scatter(grad_qkv_w, ("dp", "expert"), scatter_dimension=0, tiled=True),
        lax.psum_scatter(out_grad_part, ("dp", "expert"), scatter_dimension=0, tiled=True),
    )
    gate_up_part, down_part = (
        lax.psum_scatter(
            grad_gate_up_w.astype(jnp.bfloat16), "dp", scatter_dimension=1, tiled=True
        ).astype(jnp.float32),
        lax.psum_scatter(
            grad_down.astype(jnp.bfloat16), "dp", scatter_dimension=1, tiled=True
        ).astype(jnp.float32),
    )
    small_sums = lax.psum(
        (grad_query_gain, grad_key_gain, grad_attn_gain, grad_ffn_gain, grad_router),
        ("dp", "expert"),
    )
    dealt_pieces = (
        output_low.astype(jnp.float32).reshape(devices, stripe_rows, model_width),
        grad_tokens.reshape(devices, stripe_rows, model_width),
    )
    back_output, back_grad = (
        lax.all_to_all(
            dealt_pieces[0].astype(jnp.bfloat16),
            ("dp", "expert"),
            split_axis=0,
            concat_axis=0,
            tiled=True,
        ).astype(jnp.float32),
        lax.all_to_all(
            dealt_pieces[1].astype(jnp.bfloat16),
            ("dp", "expert"),
            split_axis=0,
            concat_axis=0,
            tiled=True,
        ).astype(jnp.float32),
    )
    inverse_deal = (
        jnp.zeros((devices,), jnp.int32).at[deal].set(jnp.arange(devices, dtype=jnp.int32))
    )
    output = back_output[inverse_deal].reshape(tok_rows, model_width).astype(jnp.bfloat16)
    given_grad = back_grad[inverse_deal].reshape(tok_rows, model_width)
    return (
        output,
        mean_loss,
        given_grad,
        qkv_grad_part,
        out_grad_part,
        small_sums[0],
        small_sums[1],
        small_sums[2],
        small_sums[3],
        small_sums[4],
        gate_up_part,
        down_part,
    )


def solution(mesh):
    placed = (
        P(("dp", "expert"), None),
        P(("dp", "expert"), None),
        P("dp", None),
        P("dp", None),
        P(),
        P(),
        P(),
        P(),
        P(),
        P("expert", "dp", None),
        P("expert", "dp", None),
        P(),
        P(("dp", "expert"), None),
        P(("dp", "expert")),
        P(("dp", "expert"), None),
    )
    return jax.shard_map(
        on_device,
        mesh=mesh,
        in_specs=placed,
        out_specs=(
            P(("dp", "expert"), None),
            P(),
            P(("dp", "expert"), None),
            P(("dp", "expert"), None),
            P(("dp", "expert"), None),
            P(),
            P(),
            P(),
            P(),
            P(),
            P("expert", "dp", None),
            P("expert", "dp", None),
        ),
        check_vma=False,
    )
```

profile of v0, /device:TPU:0, one launch (start us, length us, event | category | flops | bytes accessed | tf_op | source)
XLA Modules:
  0.0 2070.3 jit_solution(10931470302391400939)
XLA Ops:
  9.7 1.8 gather_fusion
  11.5 7.3 all-to-all-start
  19.4 4.5 reduce-window.19
  25.0 10.1 all-to-all-done
  35.7 205.2 %all-gather.5.cloned.1.call-done = bf16[2048,6144]{1,0:T(8,128)(2,1)} async-done(((bf16[512,6144]{1,0:T(8,128)(2,1)}), bf16[2048,6144]{1,0:T(8,128)(2,1)}) %all-gather.5.cloned.1.call-update) | async-done | bytes 25165840 | tf_op jit(solution)/shard_map/all_gather | solution.py:117
  240.9 10.0 fusion.95
  251.0 1.6 copy-done.5
  252.6 1.5 slice_bitcast_fusion.3
  254.6 1.6 copy.262
  257.7 2.1 subtract_convert_fusion.1
  259.8 3.3 fusion.96
  263.1 2.9 convolution_convert_fusion.2
  266.0 64.3 %all-gather.7.cloned.1.call-done = bf16[2048,2048]{1,0:T(8,128)(2,1)} async-done(((bf16[512,2048]{1,0:T(8,128)(2,1)}), bf16[2048,2048]{1,0:T(8,128)(2,1)}) %all-gather.7.cloned.1.call-update) | async-done | bytes 8388624 | tf_op jit(solution)/shard_map/all_gather | solution.py:118
  330.3 4.8 multiply_reduce_fusion.7
  335.2 12.7 scatter_custom_fusion
  348.0 5.1 all-to-all-start.1
  353.9 1.8 gather_fusion.3
  355.6 181.3 %all-to-all-done.1 = bf16[8,2,128,2048]{3,2,1,0:T(8,128)(2,1)} async-done(((bf16[8,2,128,2048]{3,2,1,0:T(8,128)(2,1)}), bf16[8,2,128,2048]{3,2,1,0:T(8,128)(2,1)}, u32[]{:S(2)}, u32[]{:S(2)}) %all-to-all-start.1) | async-done | bytes 8388640 | tf_op jit(solution)/shard_map/all_to_all | solution.py:176
  537.0 3.1 all-to-all-start.4
  540.1 24.5 %fusion.22 = f32[8,2,128,2048]{3,2,0,1:T(8,128)} fusion(bf16[2,2048,2048]{2,1,0:T(8,128)(2,1)} %all-gather.9.cloned.1.call-done, bf16[8,2,128,2048]{3,2,1,0:T(8,128)(2,1)} %all-to-all-done.1), kind=kOutput, calls=%fused_computation.44 | convolution fusion | flops 17179869184 | bytes 41943040 | tf_op jit(solution)/shard_map/sxcd,xdf->sxcf/dot_general | solution.py:177
  564.6 8.5 multiply_convert_fusion
  573.2 11.1 all-gather.11.cloned.1.call-done
  584.3 15.1 convert_bitcast_fusion.1
  599.3 8.3 copy.211
  607.7 5.1 all-to-all-start.2
  613.4 202.4 %psum.50 = f32[]{:T(128)} all-reduce(f32[]{:T(128)} %convert_reduce_fusion.2), channel_id=1, replica_groups=mesh['dp'=4,'expert'=8] {'dp','expert'}, use_global_device_ids=true, to_apply=%region_20.21 | all-reduce | flops 1 | bytes 8 | tf_op jit(solution)/shard_map/psum | solution.py:200
  818.5 13.3 gather_fusion.1
  831.8 6.5 fusion.5
  839.6 12.0 scatter_custom_fusion.2
  851.6 187.6 %all_to_all.40 = bf16[8,2,128,2048]{3,2,1,0:T(8,128)(2,1)S(1)} all-to-all(bf16[8,2,128,2048]{3,2,1,0:T(8,128)(2,1)} %bitcast.226), channel_id=1, replica_groups=mesh['dp'=4,'expert'=8] {'expert'}, dimensions={0} | all-to-all | bytes 16777216 | tf_op jit(solution)/shard_map/all_to_all | solution.py:214
  1039.3 3.4 copy-done.17
  1042.6 13.3 bitcast_convert_fusion.1
  1056.0 19.7 fusion.9
  1075.7 24.6 %bitcast_convert_fusion = bf16[2,2048,2048]{2,1,0:T(8,128)(2,1)} fusion(bf16[8,2,128,2048]{3,2,1,0:T(8,128)(2,1)} %all-to-all-done.1, bf16[8,2,128,1024]{3,2,0,1:T(8,128)(2,1)} %get-tuple-element.27, bf16[8,2,128,1024]{3,2,0,1:T(8,128)(2,1)} %get-tuple-element.26), kind=kOutput, calls=%fused_computation.10 | convolution fusion | flops 17205035008 | bytes 33554432 | tf_op jit(solution)/shard_map/sxcd,sxcf->xdf/dot_general | solution.py:229
  1100.4 24.4 %convert_bitcast_fusion = bf16[8,2,128,2048]{3,2,0,1:T(8,128)(2,1)} fusion(bf16[2,2048,2048]{2,1,0:T(8,128)(2,1)} %all-gather.9.cloned.1.call-done, bf16[8,2,128,1024]{3,2,0,1:T(8,128)(2,1)} %get-tuple-element.27, bf16[8,2,128,1024]{3,2,0,1:T(8,128)(2,1)} %get-tuple-element.26), kind=kOutput, calls=%fused_computation.36 | convolution fusion | flops 17200840704 | bytes 33554432 | tf_op jit(solution)/shard_map/sxcf,xdf->sxcd/dot_general | solution.py:232
  1124.8 8.6 copy.213
  1133.5 5.1 all-to-all-start.6
  1138.7 3.2 fusion.6
  1143.9 178.8 %all-to-all-done.6 = bf16[8,2,128,2048]{3,2,1,0:T(8,128)(2,1)} async-done(((bf16[8,2,128,2048]{3,2,1,0:T(8,128)(2,1)}), bf16[8,2,128,2048]{3,2,1,0:T(8,128)(2,1)}, u32[]{:S(2)}, u32[]{:S(2)}) %all-to-all-start.6) | async-done | bytes 8388640 | tf_op jit(solution)/shard_map/all_to_all | solution.py:235
  1322.8 13.7 gather_fusion.4
  1336.5 5.1 convert_reduce_fusion
  1341.6 3.5 multiply_reduce_fusion
  1345.5 8.1 fusion.70
  1355.1 7.1 convolution_convert_fusion
  1362.2 2.0 copy.255
  1364.2 3.0 convolution_convert_fusion.1
  1367.2 2.1 copy.252
  1369.3 2.0 multiply_reduce_fusion.5
  1371.4 1.6 multiply_convert_fusion.1
  1375.0 3.0 multiply_reduce_fusion.3
  1379.5 5.2 fusion.54
  1384.8 20.9 %fusion.58 = f32[2048,6144]{1,0:T(8,128)} fusion(bf16[128,2048]{1,0:T(8,128)(2,1)} %copy.252, bf16[128,2048]{1,0:T(8,128)(2,1)} %get-tuple-element.29, bf16[128,2048]{1,0:T(8,128)(2,1)} %get-tuple-element.28, f32[128,2048]{1,0:T(8,128)S(1)} %copy-done.2, f32[2048]{0:T(1024)S(1)} %copy-done.37, f32[128]{0:T(128)S(1)} %copy-done.47), kind=kOutput, calls=%fused_computation.120 | convolution fusion | flops 3226730496 | bytes 52961792 | tf_op jit(solution)/shard_map/dot_general | solution.py:52
  1405.7 2.1 convert_element_type.171
  1407.8 4.9 all-to-all-start.3
  1412.7 14.2 multiply_reduce_fusion.1
  1426.9 1.5 add_convert_fusion
  1429.4 5.8 all-to-all-start.7
  1436.1 42.9 %all-reduce = (f32[]{:T(128)}, f32[128]{0:T(128)}, f32[128]{0:T(128)}, f32[2048]{0:T(1024)}, f32[2048]{0:T(1024)}) all-reduce(f32[]{:T(128)} %get-tuple-element.18, f32[128]{0:T(128)S(1)} %bitcast_reduce_fusion.1, f32[128]{0:T(128)S(1)} %bitcast_reduce_fusion, ...), channel_id=1, replica_groups=mesh['dp'=4,'expert'=8] {'dp','expert'}, use_global_device_ids=true, to_apply=%region_18.19 | all-reduce | flops 4353 | bytes 34824 | tf_op jit(solution)/shard_map/psum | solution.py:200
  1479.6 2.0 gather_fusion.2
  1485.2 4.2 convert_element_type.193
  1489.4 6.7 convert_element_type.191
  1496.1 130.4 %reduce-scatter.7.cloned.1.call-done = f32[64,2048]{1,0:T(8,128)} async-done(((f32[2048,2048]{1,0:T(8,128)}), f32[64,2048]{1,0:T(8,128)}) %reduce-scatter.7.cloned.1.call-update) | async-done | bytes 524304 | tf_op jit(solution)/shard_map/reduce_scatter | solution.py:309
  1626.4 434.4 %reduce-scatter.5.cloned.1.call-done = f32[64,6144]{1,0:T(8,128)} async-done(((f32[2048,6144]{1,0:T(8,128)}), f32[64,6144]{1,0:T(8,128)}) %reduce-scatter.5.cloned.1.call-update) | async-done | bytes 1572880 | tf_op jit(solution)/shard_map/reduce_scatter | solution.py:308
  2060.9 1.6 copy.314
  (244 shorter events, 24.1 us)
Async XLA Ops:
  7.2 809.5 %copy-start = (bf16[2048,16]{0,1:T(8,128)(2,1)S(1)}, bf16[2048,16]{0,1:T(8,128)(2,1)}, u32[]{:S(2)}) copy-start(bf16[2048,16]{0,1:T(8,128)(2,1)} %param.23) | copy-start | bytes 196612
  7.2 11.6 copy-start.49
  7.2 12.0 copy-start.64
  7.2 233.7 %copy-start.36 = (f32[2048]{0:T(1024)S(1)}, f32[2048]{0:T(1024)}, u32[]{:S(2)}) copy-start(f32[2048]{0:T(1024)} %param.21) | copy-start | bytes 24580
  7.2 233.7 %all-gather.5.cloned.1.call-start = ((), (), s32[]{:S(2)}) async-start(), calls=%async_computation.12 | async-start | bytes 31457280 | tf_op jit(solution)/shard_map/all_gather | solution.py:117
  8.0 322.3 %all-gather.7.cloned.1.call-start = ((), (), s32[]{:S(2)}) async-start(), calls=%async_computation.13 | async-start | bytes 10485760 | tf_op jit(solution)/shard_map/all_gather | solution.py:118
  8.7 531.4 %all-gather.9.cloned.1.call-start = ((), (), s32[]{:S(2)}) async-start(), calls=%async_computation.14 | async-start | bytes 20971520 | tf_op jit(solution)/shard_map/all_gather | solution.py:121
  9.7 25.8 %copy-start.63 = (s32[32]{0:T(128)}, s32[32]{0:T(128)S(1)}, u32[]{:S(2)}) copy-start(s32[32]{0:T(128)S(1)} %compare_select_fusion.2) | copy-start | bytes 388
  11.5 23.7 %all-to-all-start = ((bf16[32,4,2048]{2,1,0:T(4,128)(2,1)}), bf16[32,4,2048]{2,1,0:T(4,128)(2,1)S(1)}, u32[]{:S(2)}, u32[]{:S(2)}) async-start(bf16[32,4,2048]{2,1,0:T(4,128)(2,1)} %gather_fusion), calls=%async_computation | async-start | bytes 1048576 | tf_op jit(solution)/shard_map/all_to_all | solution.py:111
  18.9 798.1 %copy-start.32 = (s32[128,8]{1,0:T(8,128)}, s32[128,8]{1,0:T(8,128)S(1)}, u32[]{:S(2)}) copy-start(s32[128,8]{1,0:T(8,128)S(1)} %copy.204) | copy-start | bytes 12292
  24.7 238.4 %copy-start.50 = (pred[128,128]{0,1:T(8,128)(4,1)}, pred[128,128]{0,1:T(8,128)(4,1)S(1)}, u32[]{:S(2)}) copy-start(pred[128,128]{0,1:T(8,128)(4,1)S(1)} %broadcast_compare_fusion) | copy-start | bytes 49156
  25.0 232.6 %copy-start.28 = (f32[128,64]{1,0:T(8,128)}, f32[128,64]{1,0:T(8,128)S(1)}, u32[]{:S(2)}) copy-start(f32[128,64]{1,0:T(8,128)S(1)} %get-tuple-element.51) | copy-start | bytes 98308
  25.0 232.6 %copy-start.30 = (f32[128,64]{1,0:T(8,128)}, f32[128,64]{1,0:T(8,128)S(1)}, u32[]{:S(2)}) copy-start(f32[128,64]{1,0:T(8,128)S(1)} %get-tuple-element.52) | copy-start | bytes 98308
  35.6 205.3 %copy-start.46 = (f32[128]{0:T(128)}, f32[128]{0:T(128)S(1)}, u32[]{:S(2)}) copy-start(f32[128]{0:T(128)S(1)} %rsqrt.36) | copy-start | bytes 1540
  35.7 294.6 %copy-start.1 = (f32[128,2048]{1,0:T(8,128)}, f32[128,2048]{1,0:T(8,128)S(1)}, u32[]{:S(2)}) copy-start(f32[128,2048]{1,0:T(8,128)S(1)} %reshape.356) | copy-start | bytes 3145732
  254.0 5.7 copy-start.8
  254.0 5.7 copy-start.10
  263.1 71.9 %copy-start.53 = (f32[16,128]{1,0:T(8,128)}, f32[16,128]{1,0:T(8,128)S(1)}, u32[]{:S(2)}) copy-start(f32[16,128]{1,0:T(8,128)S(1)} %get-tuple-element.53) | copy-start | bytes 24580
  266.0 69.1 %copy-start.18 = (bf16[16,128,128]{2,1,0:T(8,128)(2,1)}, bf16[16,128,128]{2,1,0:T(8,128)(2,1)S(1)}, u32[]{:S(2)}) copy-start(bf16[16,128,128]{2,1,0:T(8,128)(2,1)S(1)} %convolution_convert_fusion.2) | copy-start | bytes 1572868
  335.0 503.3 %copy-start.3 = (f32[128,2048]{1,0:T(8,128)}, f32[128,2048]{1,0:T(8,128)S(1)}, u32[]{:S(2)}) copy-start(f32[128,2048]{1,0:T(8,128)S(1)} %get-tuple-element.56) | copy-start | bytes 3145732
  335.1 12.9 copy-start.61
  335.2 481.4 %copy-start.15 = (bf16[128,2048]{1,0:T(8,128)(2,1)}, bf16[128,2048]{1,0:T(8,128)(2,1)S(1)}, u32[]{:S(2)}) copy-start(bf16[128,2048]{1,0:T(8,128)(2,1)S(1)} %multiply_convert_fusion.2) | copy-start | bytes 1572868
  348.0 5.7 copy-start.35
  348.0 189.0 %all-to-all-start.1 = ((bf16[8,2,128,2048]{3,2,1,0:T(8,128)(2,1)}), bf16[8,2,128,2048]{3,2,1,0:T(8,128)(2,1)}, u32[]{:S(2)}, u32[]{:S(2)}) async-start(bf16[8,2,128,2048]{3,2,1,0:T(8,128)(2,1)} %bitcast.225), calls=%async_computation.1 | async-start | bytes 16777216 | tf_op jit(solution)/shard_map/all_to_all | solution.py:176
  353.1 231.2 %all-gather.11.cloned.1.call-start = ((), (), s32[]{:S(2)}) async-start(), calls=%async_computation.15 | async-start | bytes 10485760 | tf_op jit(solution)/shard_map/all_gather | solution.py:122
  537.0 70.7 %all-to-all-start.4 = ((bf16[32,4,2048]{2,1,0:T(4,128)(2,1)}), bf16[32,4,2048]{2,1,0:T(4,128)(2,1)S(1)}, u32[]{:S(2)}, u32[]{:S(2)}) async-start(bf16[32,4,2048]{2,1,0:T(4,128)(2,1)} %gather_fusion.3), calls=%async_computation.4 | async-start | bytes 1048576 | tf_op jit(solution)/shard_map/all_to_all | solution.py:112
  607.7 210.8 %all-to-all-start.2 = ((bf16[8,2,128,2048]{3,2,1,0:T(8,128)(2,1)}), bf16[8,2,128,2048]{3,2,1,0:T(8,128)(2,1)}, u32[]{:S(2)}, u32[]{:S(2)}) async-start(bf16[8,2,128,2048]{3,2,1,0:T(8,128)(2,1)} %copy.211), calls=%async_computation.2 | async-start | bytes 16777216 | tf_op jit(solution)/shard_map/all_to_all | solution.py:187
  612.8 872.4 %reduce-scatter.11.cloned.1.call-start = ((), (), s32[]{:S(2)}) async-start(), calls=%async_computation.20 | async-start | bytes 10485760 | tf_op jit(solution)/shard_map/reduce_scatter | solution.py:315
  816.6 15.2 copy-start.44
  816.7 21.6 %copy-start.12 = (f32[128,2048]{1,0:T(8,128)}, f32[128,2048]{1,0:T(8,128)S(1)}, u32[]{:S(2)}) copy-start(f32[128,2048]{1,0:T(8,128)S(1)} %reshape.358) | copy-start | bytes 3145732
  817.6 14.1 copy-start.26
  818.2 13.5 copy-start.55
  839.6 199.7 %copy-start.6 = (f32[128,2048]{1,0:T(8,128)}, f32[128,2048]{1,0:T(8,128)S(1)}, u32[]{:S(2)}) copy-start(f32[128,2048]{1,0:T(8,128)S(1)} %broadcast_multiply_fusion) | copy-start | bytes 3145732
  1056.0 433.4 %reduce-scatter.9.cloned.1.call-start = ((), (), s32[]{:S(2)}) async-start(), calls=%async_computation.19 | async-start | bytes 20971520 | tf_op jit(solution)/shard_map/reduce_scatter | solution.py:312
  1133.4 5.2 copy-start.7
  1133.4 8.4 copy-start.27
  1133.4 8.4 copy-start.52
  1133.5 8.4 copy-start.56
  1133.5 8.7 copy-start.33
  1133.5 9.4 copy-start.16
  1133.5 189.3 %copy-start.45 = (s32[1024]{0:T(1024)S(1)}, s32[1024]{0:T(1024)}, u32[]{:S(2)}) copy-start(s32[1024]{0:T(1024)} %copy-done.44) | copy-start | bytes 12292
  1133.5 189.3 %all-to-all-start.6 = ((bf16[8,2,128,2048]{3,2,1,0:T(8,128)(2,1)}), bf16[8,2,128,2048]{3,2,1,0:T(8,128)(2,1)}, u32[]{:S(2)}, u32[]{:S(2)}) async-start(bf16[8,2,128,2048]{3,2,1,0:T(8,128)(2,1)} %copy.213), calls=%async_computation.6 | async-start | bytes 16777216 | tf_op jit(solution)/shard_map/all_to_all | solution.py:235
  1138.6 357.5 %all-reduce.3.cloned.1.call-start = ((), (), s32[]{:S(2)}) async-start(), calls=%async_computation.18 | async-start | bytes 262144 | tf_op jit(solution)/shard_map/psum | solution.py:319
  1143.9 482.5 %reduce-scatter.7.cloned.1.call-start = ((), (), s32[]{:S(2)}) async-start(), calls=%async_computation.17 | async-start | bytes 17301504 | tf_op jit(solution)/shard_map/reduce_scatter | solution.py:309
  1322.8 18.8 copy-start.4
  1322.8 18.8 copy-start.13
  1322.8 18.8 copy-start.43
  1322.8 18.8 copy-start.62
  1336.5 9.0 copy-start.19
  1353.7 10.6 copy-start.22
  1353.7 10.6 copy-start.23
  1353.7 10.5 copy-start.24
  1353.7 10.5 copy-start.25
  1353.7 10.5 copy-start.54
  1353.7 707.2 %reduce-scatter.5.cloned.1.call-start = ((), (), s32[]{:S(2)}) async-start(), calls=%async_computation.16 | async-start | bytes 51904512 | tf_op jit(solution)/shard_map/reduce_scatter | solution.py:308
  1367.2 6.7 copy-start.29
  1367.2 6.8 copy-start.31
  1378.0 6.8 copy-start.2
  1378.0 6.8 copy-start.37
  1378.0 6.8 copy-start.47
  1405.6 7.0 copy-start.20
  1405.6 7.1 copy-start.21
  1407.8 21.6 %all-to-all-start.3 = ((bf16[32,4,2048]{2,1,0:T(4,128)(2,1)}), bf16[32,4,2048]{2,1,0:T(4,128)(2,1)}, u32[]{:S(2)}, u32[]{:S(2)}) async-start(bf16[32,4,2048]{2,1,0:T(4,128)(2,1)} %convert_element_type.171), calls=%async_computation.3 | async-start | bytes 1048576 | tf_op jit(solution)/shard_map/all_to_all | solution.py:328
  1429.4 53.2 %all-to-all-start.7 = ((bf16[32,4,2048]{2,1,0:T(4,128)(2,1)}), bf16[32,4,2048]{2,1,0:T(4,128)(2,1)S(1)}, u32[]{:S(2)}, u32[]{:S(2)}) async-start(bf16[32,4,2048]{2,1,0:T(4,128)(2,1)} %convert_element_type.188), calls=%async_computation.7 | async-start | bytes 1048576 | tf_op jit(solution)/shard_map/all_to_all | solution.py:335
  (20 other events, 52.4 us)
Sparse Core Ops, SparseCore 0:
  9.9 230.9 all-gather.4
  242.7 87.4 all-gather.6
  332.1 157.2 all-gather.8
  491.1 93.0 all-gather.10
  1056.1 86.1 reduce-scatter.10
  1145.3 153.7 reduce-scatter.8
  1305.1 126.9 all-reduce.2
  1435.0 191.3 reduce-scatter.6
  1633.4 427.3 reduce-scatter.4
where the time goes:
time: 2080 us; the launch traced here: 2070 us
  waiting for transfers between devices  1220 us (59%)
  blocking collectives  433 us (21%)
  matrix products  205 us (10%)
  local copies, waits for them, and re-layouts  89.8 us (4%)
  other arithmetic  69.9 us (3%)
  starting transfers between devices  36.7 us (2%)
    reduce_scatter x1, waiting for transfers between devices, on_device(): lax.psum_scatter(grad_qkv_w, ('dp', 'expert'), scatter_dimension=0, tiled...  434 us
    psum x2, blocking collectives, on_device(): lax.psum((part_square, part_count), ('dp', 'expert'))  245 us
    all_gather x1, waiting for transfers between devices, on_device(): lax.all_gather(qkv_weight, 'dp', axis=0, tiled=True)  205 us
    all_to_all x1, blocking collectives, on_device(): lax.all_to_all(send_back, 'expert', split_axis=0, concat_axis=0, tiled=True)  188 us
    all_to_all x1, waiting for transfers between devices, on_device(): lax.all_to_all(send, 'expert', split_axis=0, concat_axis=0, tiled=True)  181 us
    all_to_all x1, waiting for transfers between devices, on_device(): lax.all_to_all(grad_entry, 'expert', split_axis=0, concat_axis=0, tiled=T...  179 us
    reduce_scatter x1, waiting for transfers between devices, on_device(): lax.psum_scatter(out_grad_part, ('dp', 'expert'), scatter_dimension=0, ti...  130 us
    all_gather x1, waiting for transfers between devices, on_device(): lax.all_gather(out_weight, 'dp', axis=0, tiled=True)  64.3 us
  transfers between devices with their start and end apart: 16, of which 8 were waited for; matrix products, arithmetic and copies ran while one was open for 15% of the time, Pallas kernels for 0%

commit v1 on v0

v1 whole, which is shorter than its diff:
```python
import math

import jax
import jax.numpy as jnp
from jax import lax
from jax.sharding import PartitionSpec as P

HD = 128
EPS = 1e-06
ROPE_BASE = 50000.0
BOTH = ("dp", "expert")


def rms_scale(values):
    return lax.rsqrt(jnp.mean(values * values, axis=-1, keepdims=True) + EPS)


def rotate(values, cosine, sine_part):
    half = values.shape[-1] // 2
    a, b = values[..., :half], values[..., half:]
    return jnp.concatenate([a * cosine - b * sine_part, b * cosine + a * sine_part], axis=-1)


def norm_back(grad_in, normed, scale_rows):
    return scale_rows * (grad_in - normed * jnp.mean(grad_in * normed, axis=-1, keepdims=True))


def dotf(left, right, dims):
    return lax.dot_general(left, right, (dims, ((), ())), preferred_element_type=jnp.float32)


def swap(pieces, axes):
    return lax.all_to_all(pieces, axes, split_axis=0, concat_axis=0, tiled=True)


def spread(block, axes, count):
    return swap(jnp.broadcast_to(block[None], (count, *block.shape)), axes)


def sum_small(values, devices):
    flat = jnp.concatenate([v.reshape(-1) for v in values])
    size = flat.shape[0]
    chunk = -(-size // (devices * 128)) * 128
    flat = jnp.pad(flat, (0, devices * chunk - size)).reshape(devices, chunk)
    total = jnp.sum(swap(flat, BOTH), axis=0)
    total = spread(total, BOTH, devices).reshape(-1)
    out, at = [], 0
    for v in values:
        out.append(total[at : at + v.size].reshape(v.shape))
        at += v.size
    return out


def on_device(
    tokens,
    teacher,
    qkv_weight,
    out_weight,
    query_gain,
    key_gain,
    attn_gain,
    ffn_gain,
    router_weight,
    gate_up_weight,
    down_weight,
    deal,
    routes,
    counted,
    lengths,
):
    bf16 = jnp.bfloat16
    f32 = jnp.float32
    rows, width = tokens.shape
    slots = routes.shape[1]
    experts = router_weight.shape[1]
    local = gate_up_weight.shape[0]
    hidden = gate_up_weight.shape[2] // 2
    owners = lax.axis_size("expert")
    dps = lax.axis_size("dp")
    devices = dps * owners
    stripe = rows // devices
    my_dp = lax.axis_index("dp")
    my_ex = lax.axis_index("expert")
    part = width // dps
    heads = part // HD
    group = dps * rows
    factor = HD ** (-0.5)

    lanes = 128
    packed = jnp.concatenate(
        [
            routes.reshape(-1),
            counted,
            jnp.pad(lengths[0], (0, lanes - lengths.shape[1])),
        ]
    )
    packed = spread(packed, BOTH, devices)
    packed = packed.reshape(dps, owners, -1)
    total_count = jnp.sum(packed[:, :, rows * slots : rows * slots + rows]).astype(f32)
    valid_total = jnp.maximum(total_count, 1.0)
    group_routes = lax.dynamic_index_in_dim(packed, my_dp, 0, keepdims=False)
    group_routes = group_routes[:, : rows * slots].reshape(owners * rows, slots)
    group_lengths = lax.dynamic_index_in_dim(packed, my_ex, 1, keepdims=False)
    group_lengths = group_lengths[:, rows * slots + rows :][:, : lengths.shape[1]]

    dealt_tokens = swap(tokens.reshape(devices, stripe, width)[deal], BOTH).reshape(rows, width)
    dealt_teacher = swap(teacher.reshape(devices, stripe, width)[deal], BOTH).reshape(rows, width)

    gate_up = []
    for e in range(local):
        gate_up.append(lax.all_gather(gate_up_weight[e], "dp", axis=0, tiled=True))
    down = lax.all_gather(down_weight, "dp", axis=1, tiled=True)
    down = down.reshape(local * hidden, width)

    ends = jnp.cumsum(group_lengths, axis=1)
    index = jnp.arange(rows, dtype=jnp.int32)
    passed = (index[None, :, None] >= ends[:, None, :]).astype(jnp.int32)
    segment = jnp.sum(passed, axis=2)
    start = jnp.sum(passed * group_lengths[:, None, :], axis=2)
    inverse = jnp.exp(
        jnp.arange(HD // 2, dtype=f32) * (-2.0 * math.log(ROPE_BASE) / HD)
    )
    angles = (index[None, :] - start).astype(f32)[:, :, None] * inverse
    cosine = jnp.cos(angles)[:, :, None, :]
    sine_part = jnp.sin(angles)[:, :, None, :]
    same = (segment[:, :, None] == segment[:, None, :])[:, None]

    weight_parts = lax.optimization_barrier(
        jnp.stack(
            [
                jnp.concatenate(
                    [
                        qkv_weight[:, g * width + d * part : g * width + (d + 1) * part]
                        for g in range(3)
                    ],
                    axis=1,
                )
                for d in range(dps)
            ]
        )
    )
    tokens32 = dealt_tokens.astype(f32)
    attn_scale = rms_scale(tokens32)
    attn_normed = tokens32 * attn_scale
    attn_low = (attn_normed * attn_gain).astype(bf16)
    attn_cols = swap(attn_low.reshape(rows, dps, part).transpose(1, 0, 2), "dp")
    attn_cols = attn_cols.reshape(group, part)
    qkv = jnp.einsum("tk,dkc->dtc", attn_cols, weight_parts, preferred_element_type=f32)
    qkv = jnp.sum(swap(qkv.astype(bf16), "dp").astype(f32), axis=0)
    queries, keys, values_low = (
        qkv[:, g * part : (g + 1) * part].reshape(dps, rows, heads, HD) for g in range(3)
    )
    values_low = values_low.astype(bf16)
    query_scale = rms_scale(queries)
    query_normed = queries * query_scale
    query_low = rotate(query_normed * query_gain, cosine, sine_part).astype(bf16)
    key_scale = rms_scale(keys)
    key_normed = keys * key_scale
    key_low = rotate(key_normed * key_gain, cosine, sine_part).astype(bf16)
    scores = (
        jnp.einsum("bthd,bshd->bhts", query_low, key_low, preferred_element_type=f32) * factor
    )
    scores = jnp.where(same, scores, -1e30)
    row_max = jnp.max(scores, axis=-1, keepdims=True)
    weights = jnp.exp(scores - row_max)
    probs = weights / jnp.sum(weights, axis=-1, keepdims=True)
    probs_low = probs.astype(bf16)
    mixed = jnp.einsum("bhts,bshd->bthd", probs_low, values_low, preferred_element_type=f32)
    mixed_low = mixed.reshape(group, part).astype(bf16)
    attn_out = dotf(mixed_low, out_weight, ((1,), (0,)))
    attn_out = swap(attn_out.astype(bf16).reshape(dps, rows, width), "dp")
    residual = tokens32 + jnp.sum(attn_out.astype(f32), axis=0)

    ffn_scale = rms_scale(residual)
    ffn_normed = residual * ffn_scale
    feed_low = (ffn_normed * ffn_gain).astype(bf16)
    feed = lax.all_gather(feed_low, "expert", axis=0, tiled=True)
    logits = dotf(feed, router_weight, ((1,), (0,)))
    table = group_routes[:, :, None] == jnp.arange(experts, dtype=jnp.int32)
    named = jnp.any(table, axis=1)
    masked = jnp.where(named, logits, -jnp.inf)
    gates = jnp.exp(masked - jnp.max(masked, axis=1, keepdims=True))
    gates = gates / jnp.sum(gates, axis=1, keepdims=True)
    own_gates = lax.dynamic_slice_in_dim(gates, my_ex * local, local, axis=1)
    my_gates = lax.dynamic_slice_in_dim(gates, my_ex * rows, rows, axis=0)
    gate_rows, up_rows, inner = [], [], []
    for e in range(local):
        gu = dotf(feed, gate_up[e], ((1,), (0,)))
        g, u = gu[:, :hidden], gu[:, hidden:]
        gate_rows.append(g)
        up_rows.append(u)
        inner.append((jax.nn.silu(g) * u * own_gates[:, e : e + 1]).astype(bf16))
    inner = jnp.concatenate(inner, axis=1)
    moe = dotf(inner, down, ((1,), (0,)))
    moe = lax.psum_scatter(moe.astype(bf16), "expert", scatter_dimension=0, tiled=True)
    result = residual + moe.astype(f32)

    keep = counted.astype(f32)[:, None]
    error_rows = result - dealt_teacher.astype(f32)
    part_square = jnp.sum(keep * error_rows * error_rows)
    grad_result = (2.0 * (rows * devices) / valid_total) * keep * error_rows

    grad_rows = lax.all_gather(grad_result.astype(bf16), "expert", axis=0, tiled=True)
    grad_feed = 0.0
    gate_grads, grad_gate_up_w = [], []
    grad_inner_raw = dotf(grad_rows, down, ((1,), (1,)))
    grad_down_w = dotf(inner, grad_rows, ((0,), (0,)))
    for e in range(local):
        g, u = gate_rows[e], up_rows[e]
        sg = jax.nn.sigmoid(g)
        silu = g * sg
        raw = grad_inner_raw[:, e * hidden : (e + 1) * hidden]
        gate_grads.append(jnp.sum(raw * (silu * u), axis=1))
        grad_inner = raw * own_gates[:, e : e + 1]
        grad_g = grad_inner * u * sg * (1.0 + g * (1.0 - sg))
        grad_u = grad_inner * silu
        grad_gu = jnp.concatenate([grad_g, grad_u], axis=1).astype(bf16)
        grad_gate_up_w.append(dotf(feed, grad_gu, ((0,), (0,))))
        grad_feed = grad_feed + dotf(grad_gu, gate_up[e], ((1,), (1,)))
    grad_feed = lax.psum_scatter(
        grad_feed.astype(bf16), "expert", scatter_dimension=0, tiled=True
    ).astype(f32)
    gate_grad = swap(
        jnp.stack(gate_grads, axis=0).reshape(local, owners, rows).transpose(1, 0, 2), "expert"
    )
    gate_grad = gate_grad.reshape(experts, rows).T
    grad_logits = my_gates * (gate_grad - jnp.sum(my_gates * gate_grad, axis=1, keepdims=True))
    grad_router = lax.dot_general(
        feed_low.astype(f32),
        grad_logits,
        (((0,), (0,)), ((), ())),
        precision=lax.Precision.HIGHEST,
        preferred_element_type=f32,
    )
    grad_feed = grad_feed + lax.dot_general(
        grad_logits,
        router_weight.astype(f32),
        (((1,), (1,)), ((), ())),
        precision=lax.Precision.HIGHEST,
        preferred_element_type=f32,
    )
    grad_ffn_gain = jnp.sum(grad_feed * ffn_normed, axis=0)
    grad_resid = grad_result + norm_back(grad_feed * ffn_gain, ffn_normed, ffn_scale)

    early = sum_small((part_square, grad_ffn_gain, grad_router), devices)
    grad_attn = spread(grad_resid.astype(bf16), "dp", dps).reshape(group, width)
    grad_out_w = dotf(mixed_low, grad_attn, ((0,), (0,)))
    grad_mixed = dotf(grad_attn, out_weight, ((1,), (1,)))
    grad_mixed = grad_mixed.reshape(dps, rows, heads, HD).astype(bf16)
    grad_probs = jnp.einsum("bthd,bshd->bhts", grad_mixed, values_low, preferred_element_type=f32)
    weighted = jnp.sum(probs * grad_probs, axis=-1, keepdims=True)
    grad_scores = (probs * (grad_probs - weighted)).astype(bf16)
    grad_value = jnp.einsum("bhts,bthd->bshd", probs_low, grad_mixed, preferred_element_type=f32)
    grad_query = (
        jnp.einsum("bhts,bshd->bthd", grad_scores, key_low, preferred_element_type=f32) * factor
    )
    grad_key = (
        jnp.einsum("bhts,bthd->bshd", grad_scores, query_low, preferred_element_type=f32) * factor
    )
    grad_qn = rotate(grad_query, cosine, -sine_part)
    grad_query_gain = jnp.sum(grad_qn * query_normed, axis=(0, 1, 2))
    grad_q = norm_back(grad_qn * query_gain, query_normed, query_scale)
    grad_kn = rotate(grad_key, cosine, -sine_part)
    grad_key_gain = jnp.sum(grad_kn * key_normed, axis=(0, 1, 2))
    grad_k = norm_back(grad_kn * key_gain, key_normed, key_scale)
    grad_qkv = jnp.concatenate(
        [
            grad_q.reshape(group, part).astype(bf16),
            grad_k.reshape(group, part).astype(bf16),
            grad_value.reshape(group, part).astype(bf16),
        ],
        axis=1,
    )
    grad_qkv = spread(grad_qkv, "dp", dps)
    grad_qkv_w = [dotf(attn_cols, grad_qkv[d], ((0,), (0,))).astype(bf16) for d in range(dps)]
    grad_qkv_w = jnp.concatenate(
        [grad_qkv_w[d][:, g * part : (g + 1) * part] for g in range(3) for d in range(dps)], axis=1
    )
    grad_normed = jnp.einsum("dtc,dkc->tk", grad_qkv, weight_parts, preferred_element_type=f32)
    grad_normed = swap(grad_normed.astype(bf16).reshape(dps, rows, part), "dp")
    grad_normed = grad_normed.transpose(1, 0, 2).reshape(rows, width).astype(f32)
    grad_attn_gain = jnp.sum(grad_normed * attn_normed, axis=0)
    grad_tokens = grad_resid + norm_back(grad_normed * attn_gain, attn_normed, attn_scale)

    qkv_out = lax.psum_scatter(
        grad_qkv_w, "expert", scatter_dimension=0, tiled=True
    ).astype(f32)
    out_out = lax.psum_scatter(
        grad_out_w.astype(bf16), "expert", scatter_dimension=0, tiled=True
    ).astype(f32)
    gate_up_out = jnp.stack(
        [
            lax.psum_scatter(w.astype(bf16), "dp", scatter_dimension=0, tiled=True).astype(f32)
            for w in grad_gate_up_w
        ]
    )
    down_out = lax.psum_scatter(
        grad_down_w.astype(bf16).reshape(local, hidden, width),
        "dp",
        scatter_dimension=1,
        tiled=True,
    ).astype(f32)
    late = sum_small((grad_query_gain, grad_key_gain, grad_attn_gain), devices)
    mean_loss = early[0] / (valid_total * width)

    inverse_deal = (
        jnp.zeros((devices,), jnp.int32).at[deal].set(jnp.arange(devices, dtype=jnp.int32))
    )
    back_output = swap(result.astype(bf16).reshape(devices, stripe, width), BOTH)
    back_grad = swap(grad_tokens.astype(bf16).reshape(devices, stripe, width), BOTH)
    output = back_output[inverse_deal].reshape(rows, width)
    given_grad = back_grad[inverse_deal].reshape(rows, width).astype(f32)
    return (
        output,
        mean_loss,
        given_grad,
        qkv_out,
        out_out,
        late[0],
        late[1],
        late[2],
        early[1],
        early[2],
        gate_up_out,
        down_out,
    )


def solution(mesh):
    placed = (
        P(BOTH, None),
        P(BOTH, None),
        P("dp", None),
        P("dp", None),
        P(),
        P(),
        P(),
        P(),
        P(),
        P("expert", "dp", None),
        P("expert", "dp", None),
        P(),
        P(BOTH, None),
        P(BOTH),
        P(BOTH, None),
    )
    return jax.shard_map(
        on_device,
        mesh=mesh,
        in_specs=placed,
        out_specs=(
            P(BOTH, None),
            P(),
            P(BOTH, None),
            P(BOTH, None),
            P(BOTH, None),
            P(),
            P(),
            P(),
            P(),
            P(),
            P("expert", "dp", None),
            P("expert", "dp", None),
        ),
        check_vma=False,
    )
```

time: 2080 us -> 1270 us (0.61)
  waiting for transfers between devices: 1220 us -> 682 us
  blocking collectives: 433 us -> 135 us
  matrix products: 205 us -> 176 us
  starting transfers between devices: 36.7 us -> 57.6 us
    reduce_scatter x4 -> x7, waiting for transfers between devices: 565 us -> 193 us  [the longest x1 65.8 us: on_device(): lax.psum_scatter(grad_qkv_w, 'expert', scatter_dimension=0, tiled=True)]
    psum x2 -> x0, blocking collectives: 245 us -> none  [on_device(): lax.psum((part_square, part_count), ('dp', 'expert'))]
    all_to_all x7 -> x14, waiting for transfers between devices: 370 us -> 174 us  [swap(): return lax.all_to_all(pieces, axes, split_axis=0, concat_axis=0, tiled=True)]
    all_to_all x1 -> x2, blocking collectives: 188 us -> 135 us  [swap(): return lax.all_to_all(pieces, axes, split_axis=0, concat_axis=0, tiled=True)]
    all_gather x4 -> x5, waiting for transfers between devices: 281 us -> 314 us  [the longest x2 156 us: on_device(): gate_up.append(lax.all_gather(gate_up_weight[e], 'dp', axis=0, tiled=True))]
    dot_general x22 -> x26, matrix products: 202 us -> 173 us  [the longest x17 141 us: dotf(): lax.dot_general(left, right, (dims, ((), ())), preferred_element_type=jnp...]
    gather x6 -> x4, local copies, waits for them, and re-layouts: 33.7 us -> 7.56 us  [the longest x1 2.03 us: on_device(): output = back_output[inverse_deal].reshape(rows, width)]
    all_to_all x7 -> x14, starting transfers between devices: 36.4 us -> 56.3 us  [swap(): return lax.all_to_all(pieces, axes, split_axis=0, concat_axis=0, tiled=True)]
  transfers between devices with their start and end apart: 16 -> 26, of which waited for: 8 -> 22; matrix products, arithmetic and copies ran while one was open for 15% -> 17% of each run, Pallas kernels for 0% -> 0%
where the time goes in v1:
time: 1270 us; the launch traced here: 1260 us
  waiting for transfers between devices  682 us (54%)
  matrix products  176 us (14%)
  blocking collectives  135 us (11%)
  local copies, waits for them, and re-layouts  107 us (8%)
  other arithmetic  89.9 us (7%)
  starting transfers between devices  57.6 us (5%)
  between operations  17.9 us (1%)
    all_to_all x14, waiting for transfers between devices, swap(): return lax.all_to_all(pieces, axes, split_axis=0, concat_axis=0, tiled=True)  174 us
    all_gather x2, waiting for transfers between devices, on_device(): gate_up.append(lax.all_gather(gate_up_weight[e], 'dp', axis=0, tiled=True))  156 us
    dot_general x17, matrix products, dotf(): lax.dot_general(left, right, (dims, ((), ())), preferred_element_type=jnp...  141 us
    all_to_all x2, blocking collectives, swap(): return lax.all_to_all(pieces, axes, split_axis=0, concat_axis=0, tiled=True)  135 us
    all_gather x1, waiting for transfers between devices, on_device(): down = lax.all_gather(down_weight, 'dp', axis=1, tiled=True)  71 us
    reduce_scatter x1, waiting for transfers between devices, on_device(): lax.psum_scatter(grad_qkv_w, 'expert', scatter_dimension=0, tiled=True)  65.8 us
    reduce_scatter x2, waiting for transfers between devices, on_device(): lax.psum_scatter(w.astype(bf16), 'dp', scatter_dimension=0, tiled=True)  63.3 us
    all_to_all x14, starting transfers between devices, swap(): return lax.all_to_all(pieces, axes, split_axis=0, concat_axis=0, tiled=True)  56.3 us
  transfers between devices with their start and end apart: 26, of which 22 were waited for; matrix products, arithmetic and copies ran while one was open for 17% of the time, Pallas kernels for 0%

profile of v1, /device:TPU:0, one launch (start us, length us, event | category | flops | bytes accessed | tf_op | source)
XLA Modules:
  0.0 1264.8 jit_solution(10080936199549267716)
XLA Ops:
  11.5 7.3 all-to-all-start
  19.6 3.2 fusion.68
  26.4 8.7 all-to-all-done
  39.4 3.5 all-to-all-start.1
  42.9 6.6 pad_maximum_fusion
  54.8 8.2 convert_bitcast_fusion
  63.4 5.4 all-to-all-start.2
  71.8 67.8 %all-to-all-done.2 = bf16[4,512,1536]{1,2,0:T(8,128)(2,1)} async-done(((bf16[4,512,1536]{1,2,0:T(8,128)(2,1)}), bf16[4,512,1536]{1,2,0:T(8,128)(2,1)}, u32[]{:S(2)}, u32[]{:S(2)}) %all-to-all-start.2) | async-done | bytes 6291488 | tf_op jit(solution)/shard_map/all_to_all | solution.py:33
  139.6 4.1 convert_reduce_fusion
  178.8 3.4 fusion.71
  182.2 3.4 fusion.24
  187.7 3.6 convolution_convert_fusion.9
  191.3 4.5 all-to-all-start.4
  196.9 23.9 %all-to-all-done.4 = bf16[4,128,2048]{2,1,0:T(8,128)(2,1)} async-done(((bf16[4,128,2048]{2,1,0:T(8,128)(2,1)}), bf16[4,128,2048]{2,1,0:T(8,128)(2,1)}, u32[]{:S(2)}, u32[]{:S(2)}) %all-to-all-start.4) | async-done | bytes 2097184 | tf_op jit(solution)/shard_map/all_to_all | solution.py:33
  220.8 3.0 convert_reduce_fusion.1
  228.1 2.9 multiply_convert_fusion.7
  231.1 4.8 fusion.69
  238.7 38.7 %all-gather.8.cloned.1.call-done = bf16[1024,2048]{1,0:T(8,128)(2,1)} async-done(((bf16[128,2048]{1,0:T(8,128)(2,1)}), bf16[1024,2048]{1,0:T(8,128)(2,1)}) %all-gather.8.cloned.1.call-update) | async-done | bytes 4194320 | tf_op jit(solution)/shard_map/all_gather | solution.py:177
  277.4 3.4 fusion.72
  280.9 85.2 %all-gather.14.cloned.1.call-done = bf16[1,2048,2048]{2,1,0:T(8,128)(2,1)} async-done(((bf16[1,512,2048]{2,1,0:T(8,128)(2,1)}), bf16[1,2048,2048]{2,1,0:T(8,128)(2,1)}) %all-gather.14.cloned.1.call-update) | async-done | bytes 8388624 | tf_op jit(solution)/shard_map/all_gather | solution.py:111
  366.1 12.7 %fusion.7 = f32[1024,2048]{1,0:T(8,128)S(1)} fusion(bf16[1024,2048]{1,0:T(8,128)(2,1)} %all-gather.8.cloned.1.call-done, bf16[1,2048,2048]{2,1,0:T(8,128)(2,1)} %all-gather.14.cloned.1.call-done), kind=kOutput, calls=%fused_computation.13 | convolution fusion | flops 8589934592 | bytes 20971520 | tf_op jit(solution)/shard_map/dot_general | solution.py:29
  378.8 3.4 copy-done.1
  384.7 70.8 %all-gather.16.cloned.1.call-done = bf16[1,2048,2048]{2,1,0:T(8,128)(2,1)} async-done(((bf16[1,512,2048]{2,1,0:T(8,128)(2,1)}), bf16[1,2048,2048]{2,1,0:T(8,128)(2,1)}) %all-gather.16.cloned.1.call-update) | async-done | bytes 8388624 | tf_op jit(solution)/shard_map/all_gather | solution.py:111
  455.5 12.5 fusion.3
  468.0 3.2 copy-done.2
  473.7 71.0 %all-gather.10.cloned.1.call-done = bf16[2,1024,2048]{2,1,0:T(8,128)(2,1)} async-done(((bf16[2,256,2048]{2,1,0:T(8,128)(2,1)}), bf16[2,1024,2048]{2,1,0:T(8,128)(2,1)}) %all-gather.10.cloned.1.call-update) | async-done | bytes 8388624 | tf_op jit(solution)/shard_map/all_gather | solution.py:112
  544.7 14.4 %convolution_convert_fusion.3 = bf16[1024,2048]{1,0:T(8,128)(2,1)} fusion(bf16[2048,2048]{1,0:T(8,128)(2,1)} %bitcast.275, bf16[1024,1024]{1,0:T(8,128)(2,1)} %multiply_convert_fusion.4, bf16[1024,1024]{1,0:T(8,128)(2,1)} %multiply_convert_fusion.5), kind=kOutput, calls=%fused_computation.42 | convolution fusion | flops 8600420352 | bytes 16777216 | tf_op jit(solution)/shard_map/dot_general | solution.py:29
  562.0 4.7 all-to-all-start.6
  569.3 22.6 %all-to-all-done.6 = bf16[32,4,2048]{2,1,0:T(4,128)(2,1)} async-done(((bf16[32,4,2048]{2,1,0:T(4,128)(2,1)}), bf16[32,4,2048]{2,1,0:T(4,128)(2,1)}, u32[]{:S(2)}, u32[]{:S(2)}) %all-to-all-start.6) | async-done | bytes 524320 | tf_op jit(solution)/shard_map/all_to_all | solution.py:33
  593.0 24.6 %reduce-scatter.8.cloned.1.call-done = bf16[128,2048]{1,0:T(8,128)(2,1)} async-done(((bf16[1024,2048]{1,0:T(8,128)(2,1)}), bf16[128,2048]{1,0:T(8,128)(2,1)}) %reduce-scatter.8.cloned.1.call-update) | async-done | bytes 524304 | tf_op jit(solution)/shard_map/reduce_scatter | solution.py:195
  620.0 47.9 %all-gather.12.cloned.1.call-done = bf16[1024,2048]{1,0:T(8,128)(2,1)} async-done(((bf16[128,2048]{1,0:T(8,128)(2,1)}), bf16[1024,2048]{1,0:T(8,128)(2,1)}) %all-gather.12.cloned.1.call-update) | async-done | bytes 4194320 | tf_op jit(solution)/shard_map/all_gather | solution.py:203
  667.9 12.6 fusion.73
  680.5 9.6 multiply_reduce_fusion.1
  690.1 15.5 %fusion.1 = f32[1024,2048]{1,0:T(8,128)} fusion(bf16[1,2048,2048]{2,1,0:T(8,128)(2,1)} %all-gather.16.cloned.1.call-done, bf16[1024,1024]{1,0:T(8,128)(2,1)S(1)} %get-tuple-element.119, bf16[1024,1024]{1,0:T(8,128)(2,1)S(1)} %get-tuple-element.120), kind=kOutput, calls=%fused_computation.7 | convolution fusion | flops 8598323200 | bytes 20971520 | tf_op jit(solution)/shard_map/dot_general | solution.py:29
  705.6 14.7 %add_convert_fusion = bf16[1024,2048]{1,0:T(8,128)(2,1)} fusion(f32[1024,2048]{1,0:T(8,128)} %fusion.1, bf16[1,2048,2048]{2,1,0:T(8,128)(2,1)} %all-gather.14.cloned.1.call-done, bf16[1024,1024]{1,0:T(8,128)(2,1)S(1)} %get-tuple-element.121, bf16[1024,1024]{1,0:T(8,128)(2,1)} %get-tuple-element.122), kind=kOutput, calls=%fused_computation.15 | convolution fusion | flops 8602517504 | bytes 25165824 | tf_op jit(solution)/shard_map/dot_general | solution.py:29
  721.0 3.3 all-to-all-start.7
  724.4 5.5 all-to-all-done.7
  729.9 39.6 %reduce-scatter.10.cloned.1.call-done = bf16[128,2048]{1,0:T(8,128)(2,1)} async-done(((bf16[1024,2048]{1,0:T(8,128)(2,1)}), bf16[128,2048]{1,0:T(8,128)(2,1)}) %reduce-scatter.10.cloned.1.call-update) | async-done | bytes 524304 | tf_op jit(solution)/shard_map/reduce_scatter | solution.py:220
  769.5 3.3 multiply_reduce_fusion.7
  774.7 26.8 %all_to_all.91 = bf16[4,128,2048]{2,1,0:T(8,128)(2,1)S(1)} all-to-all(bf16[4,128,2048]{2,1,0:T(8,128)(2,1)S(1)} %broadcast_in_dim.36), channel_id=1, replica_groups=mesh['dp'=4,'expert'=8] {'dp'}, dimensions={0} | all-to-all | bytes 4194304 | tf_op jit(solution)/shard_map/all_to_all | solution.py:33
  802.8 2.7 convolution_convert_fusion.8
  805.5 14.1 %convolution_convert_fusion = bf16[2048,2048]{1,0:T(8,128)(2,1)} fusion(bf16[1024,2048]{1,0:T(8,128)(2,1)} %all-gather.12.cloned.1.call-done, bf16[1024,1024]{1,0:T(8,128)(2,1)} %multiply_convert_fusion.4, bf16[1024,1024]{1,0:T(8,128)(2,1)} %multiply_convert_fusion.5), kind=kOutput, calls=%fused_computation.16 | convolution fusion | flops 8602517504 | bytes 16777216 | tf_op jit(solution)/shard_map/dot_general | solution.py:29
  819.7 14.2 %convolution_convert_fusion.2 = bf16[2048,2048]{1,0:T(8,128)(2,1)} fusion(bf16[1024,2048]{1,0:T(8,128)(2,1)} %all-gather.8.cloned.1.call-done, bf16[1024,1024]{1,0:T(8,128)(2,1)} %copy-done.24, bf16[1024,1024]{1,0:T(8,128)(2,1)} %get-tuple-element.122), kind=kOutput, calls=%fused_computation.18 | convolution fusion | flops 8602517504 | bytes 16777216 | tf_op jit(solution)/shard_map/dot_general | solution.py:29
  834.0 14.1 %convolution_convert_fusion.1 = bf16[2048,2048]{1,0:T(8,128)(2,1)} fusion(bf16[1024,2048]{1,0:T(8,128)(2,1)} %all-gather.8.cloned.1.call-done, bf16[1024,1024]{1,0:T(8,128)(2,1)} %copy-done.22, bf16[1024,1024]{1,0:T(8,128)(2,1)} %copy-done.23), kind=kOutput, calls=%fused_computation.17 | convolution fusion | flops 8602517504 | bytes 16777216 | tf_op jit(solution)/shard_map/dot_general | solution.py:29
  848.9 3.1 fusion.21
  860.8 3.2 multiply_reduce_fusion.5
  865.6 3.8 fusion.25
  878.3 107.7 %all_to_all.92 = bf16[4,512,1536]{2,1,0:T(8,128)(2,1)S(1)} all-to-all(bf16[4,512,1536]{2,1,0:T(8,128)(2,1)S(1)} %broadcast_in_dim.38), channel_id=1, replica_groups=mesh['dp'=4,'expert'=8] {'dp'}, dimensions={0} | all-to-all | bytes 12582912 | tf_op jit(solution)/shard_map/all_to_all | solution.py:33
  1005.8 4.0 all-to-all-start.8
  1009.8 9.2 fusion.20
  1019.1 4.2 all-to-all-start.12
  1023.4 14.8 %all-to-all-done.12 = bf16[4,128,512]{2,1,0:T(8,128)(2,1)} async-done(((bf16[4,128,512]{2,1,0:T(8,128)(2,1)}), bf16[4,128,512]{2,1,0:T(8,128)(2,1)}, u32[]{:S(2)}, u32[]{:S(2)}) %all-to-all-start.12) | async-done | bytes 524320 | tf_op jit(solution)/shard_map/all_to_all | solution.py:33
  1038.9 4.8 all-to-all-start.9
  1045.9 6.1 all-to-all-done.9
  1056.6 5.1 all-to-all-done.14
  1061.7 3.3 all-to-all-start.5
  1072.3 9.0 all-to-all-done.5
  1084.5 2.7 add_convert_fusion.1
  1091.6 3.5 all-to-all-start.13
  1105.3 6.2 all-to-all-done.13
  1114.6 4.4 convert_element_type.256
  1119.0 63.3 %reduce-scatter.18.cloned.1.call-done = bf16[512,2048]{1,0:T(8,128)(2,1)} async-done(((bf16[2048,2048]{1,0:T(8,128)(2,1)}), bf16[512,2048]{1,0:T(8,128)(2,1)}) %reduce-scatter.18.cloned.1.call-update) | async-done | bytes 2097168 | tf_op jit(solution)/shard_map/reduce_scatter | solution.py:293
  1182.3 6.2 maximum_convert_fusion
  1188.4 65.8 %reduce-scatter.12.cloned.1.call-done = bf16[64,6144]{1,0:T(8,128)(2,1)} async-done(((bf16[512,6144]{1,0:T(8,128)(2,1)}), bf16[64,6144]{1,0:T(8,128)(2,1)}) %reduce-scatter.12.cloned.1.call-update) | async-done | bytes 786448 | tf_op jit(solution)/shard_map/reduce_scatter | solution.py:285
  (296 shorter events, 161.2 us)
Async XLA Ops:
  7.2 180.5 %copy-start = (bf16[512,2048]{1,0:T(8,128)(2,1)S(1)}, bf16[512,2048]{1,0:T(8,128)(2,1)}, u32[]{:S(2)}) copy-start(bf16[512,2048]{1,0:T(8,128)(2,1)} %param.18) | copy-start | bytes 6291460
  11.5 23.6 %all-to-all-start = ((bf16[32,4,2048]{2,1,0:T(4,128)(2,1)}), bf16[32,4,2048]{2,1,0:T(4,128)(2,1)S(1)}, u32[]{:S(2)}, u32[]{:S(2)}) async-start(bf16[32,4,2048]{2,1,0:T(4,128)(2,1)} %gather_fusion), calls=%async_computation | async-start | bytes 1048576 | tf_op jit(solution)/shard_map/all_to_all | solution.py:33
  19.5 17.4 %copy-start.40 = (f32[4,512]{1,0:T(4,128)}, f32[4,512]{1,0:T(4,128)S(1)}, u32[]{:S(2)}) copy-start(f32[4,512]{1,0:T(4,128)S(1)} %mul.535) | copy-start | bytes 24580
  35.5 7.3 copy-start.46
  39.4 12.0 all-to-all-start.1
  42.9 6.6 copy-start.52
  42.9 6.8 copy-start.54
  42.9 6.8 copy-start.55
  51.4 11.6 copy-start.29
  52.2 11.1 all-to-all-start.3
  63.4 76.2 %all-to-all-start.2 = ((bf16[4,512,1536]{1,2,0:T(8,128)(2,1)}), bf16[4,512,1536]{1,2,0:T(8,128)(2,1)}, u32[]{:S(2)}, u32[]{:S(2)}) async-start(bf16[4,512,1536]{1,2,0:T(8,128)(2,1)} %convert_bitcast_fusion), calls=%async_computation.2 | async-start | bytes 12582912 | tf_op jit(solution)/shard_map/all_to_all | solution.py:33
  70.0 112.2 %copy-start.42 = (pred[4,128,128]{1,2,0:T(8,128)(4,1)}, pred[4,128,128]{1,2,0:T(8,128)(4,1)S(1)}, u32[]{:S(2)}) copy-start(pred[4,128,128]{1,2,0:T(8,128)(4,1)S(1)} %broadcast_compare_fusion) | copy-start | bytes 196612
  71.8 105.1 %copy-start.14 = (f32[4,128,64]{2,1,0:T(8,128)}, f32[4,128,64]{2,1,0:T(8,128)S(1)}, u32[]{:S(2)}) copy-start(f32[4,128,64]{2,1,0:T(8,128)S(1)} %get-tuple-element.160) | copy-start | bytes 393220
  159.5 14.2 %copy-start.48 = (f32[128]{0:T(128)S(1)}, f32[128]{0:T(128)}, u32[]{:S(2)}) copy-start(f32[128]{0:T(128)} %param.20) | copy-start | bytes 1540
  162.0 13.3 %copy-start.50 = (f32[128]{0:T(128)S(1)}, f32[128]{0:T(128)}, u32[]{:S(2)}) copy-start(f32[128]{0:T(128)} %param.19) | copy-start | bytes 1540
  167.0 11.8 copy-start.37
  170.6 8.2 copy-start.35
  173.7 3.2 copy-start.27
  178.8 6.8 copy-start.17
  182.2 9.1 copy-start.44
  191.3 29.5 %all-to-all-start.4 = ((bf16[4,128,2048]{2,1,0:T(8,128)(2,1)}), bf16[4,128,2048]{2,1,0:T(8,128)(2,1)}, u32[]{:S(2)}, u32[]{:S(2)}) async-start(bf16[4,128,2048]{2,1,0:T(8,128)(2,1)} %bitcast.241), calls=%async_computation.4 | async-start | bytes 4194304 | tf_op jit(solution)/shard_map/all_to_all | solution.py:33
  195.8 32.3 %copy-start.39 = (f32[2048]{0:T(1024)S(1)}, f32[2048]{0:T(1024)}, u32[]{:S(2)}) copy-start(f32[2048]{0:T(1024)} %param.22) | copy-start | bytes 24580
  195.8 81.5 %all-gather.8.cloned.1.call-start = ((), (), s32[]{:S(2)}) async-start(), calls=%async_computation.23 | async-start | bytes 4718592 | tf_op jit(solution)/shard_map/all_gather | solution.py:177
  231.1 135.1 %all-gather.14.cloned.1.call-start = ((), (), s32[]{:S(2)}) async-start(), calls=%async_computation.33 | async-start | bytes 10485760 | tf_op jit(solution)/shard_map/all_gather | solution.py:111
  235.9 41.5 %copy-start.34 = (bf16[2048,16]{0,1:T(8,128)(2,1)S(1)}, bf16[2048,16]{0,1:T(8,128)(2,1)}, u32[]{:S(2)}) copy-start(bf16[2048,16]{0,1:T(8,128)(2,1)} %param.23) | copy-start | bytes 196612
  235.9 219.5 %all-gather.16.cloned.1.call-start = ((), (), s32[]{:S(2)}) async-start(), calls=%async_computation.34 | async-start | bytes 10485760 | tf_op jit(solution)/shard_map/all_gather | solution.py:111
  236.7 308.0 %all-gather.10.cloned.1.call-start = ((), (), s32[]{:S(2)}) async-start(), calls=%async_computation.24 | async-start | bytes 10485760 | tf_op jit(solution)/shard_map/all_gather | solution.py:112
  237.3 380.3 %reduce-scatter.8.cloned.1.call-start = ((), (), s32[]{:S(2)}) async-start(), calls=%async_computation.25 | async-start | bytes 4718592 | tf_op jit(solution)/shard_map/reduce_scatter | solution.py:195
  378.8 3.4 copy-start.1
  467.9 3.2 copy-start.2
  562.0 29.8 %all-to-all-start.6 = ((bf16[32,4,2048]{2,1,0:T(4,128)(2,1)}), bf16[32,4,2048]{2,1,0:T(4,128)(2,1)}, u32[]{:S(2)}, u32[]{:S(2)}) async-start(bf16[32,4,2048]{2,1,0:T(4,128)(2,1)} %gather_fusion.2), calls=%async_computation.7 | async-start | bytes 1048576 | tf_op jit(solution)/shard_map/all_to_all | solution.py:33
  566.8 101.2 %all-gather.12.cloned.1.call-start = ((), (), s32[]{:S(2)}) async-start(), calls=%async_computation.26 | async-start | bytes 4718592 | tf_op jit(solution)/shard_map/all_gather | solution.py:203
  620.0 149.5 %reduce-scatter.10.cloned.1.call-start = ((), (), s32[]{:S(2)}) async-start(), calls=%async_computation.27 | async-start | bytes 4718592 | tf_op jit(solution)/shard_map/reduce_scatter | solution.py:220
  690.1 15.5 %copy-start.22 = (bf16[1024,1024]{1,0:T(8,128)(2,1)}, bf16[1024,1024]{1,0:T(8,128)(2,1)S(1)}, u32[]{:S(2)}) copy-start(bf16[1024,1024]{1,0:T(8,128)(2,1)S(1)} %get-tuple-element.119) | copy-start | bytes 6291460
  690.1 15.5 %copy-start.23 = (bf16[1024,1024]{1,0:T(8,128)(2,1)}, bf16[1024,1024]{1,0:T(8,128)(2,1)S(1)}, u32[]{:S(2)}) copy-start(bf16[1024,1024]{1,0:T(8,128)(2,1)S(1)} %get-tuple-element.120) | copy-start | bytes 6291460
  690.1 15.5 %copy-start.24 = (bf16[1024,1024]{1,0:T(8,128)(2,1)}, bf16[1024,1024]{1,0:T(8,128)(2,1)S(1)}, u32[]{:S(2)}) copy-start(bf16[1024,1024]{1,0:T(8,128)(2,1)S(1)} %get-tuple-element.121) | copy-start | bytes 6291460
  721.0 8.9 all-to-all-start.7
  724.3 378.1 %reduce-scatter.14.cloned.1.call-start = ((), (), s32[]{:S(2)}) async-start(), calls=%async_computation.29 | async-start | bytes 2359296 | tf_op jit(solution)/shard_map/reduce_scatter | solution.py:288
  769.4 3.3 copy-start.5
  769.4 3.3 copy-start.11
  774.4 28.4 %copy-start.32 = (bf16[4,128,4,128]{3,2,1,0:T(4,128)(2,1)S(1)}, bf16[4,128,4,128]{3,2,1,0:T(4,128)(2,1)}, u32[]{:S(2)}) copy-start(bf16[4,128,4,128]{3,2,1,0:T(4,128)(2,1)} %copy.302) | copy-start | bytes 1572868
  805.5 309.1 %reduce-scatter.20.cloned.1.call-start = ((), (), s32[]{:S(2)}) async-start(), calls=%async_computation.32 | async-start | bytes 10485760 | tf_op jit(solution)/shard_map/reduce_scatter | solution.py:297
  819.7 299.3 %reduce-scatter.16.cloned.1.call-start = ((), (), s32[]{:S(2)}) async-start(), calls=%async_computation.30 | async-start | bytes 10485760 | tf_op jit(solution)/shard_map/reduce_scatter | solution.py:293
  834.0 348.3 %reduce-scatter.18.cloned.1.call-start = ((), (), s32[]{:S(2)}) async-start(), calls=%async_computation.31 | async-start | bytes 10485760 | tf_op jit(solution)/shard_map/reduce_scatter | solution.py:293
  848.2 3.9 copy-start.25
  848.2 3.9 copy-start.45
  848.2 406.0 %reduce-scatter.12.cloned.1.call-start = ((), (), s32[]{:S(2)}) async-start(), calls=%async_computation.28 | async-start | bytes 7077888 | tf_op jit(solution)/shard_map/reduce_scatter | solution.py:285
  848.8 3.2 copy-start.31
  856.6 4.2 copy-start.6
  869.5 2.3 copy-start.13
  878.3 107.7 %copy-start.30 = (bf16[4,128,512]{2,1,0:T(8,128)(2,1)S(1)}, bf16[4,128,512]{2,1,0:T(8,128)(2,1)}, u32[]{:S(2)}) copy-start(bf16[4,128,512]{2,1,0:T(8,128)(2,1)} %copy-done.29) | copy-start | bytes 1572868
  986.1 6.2 copy-start.10
  1005.8 13.3 %all-to-all-start.8 = ((f32[32,1,1152]{2,1,0:T(1,128)}), f32[32,1,1152]{2,1,0:T(1,128)S(1)}, u32[]{:S(2)}, u32[]{:S(2)}) async-start(f32[32,1,1152]{2,1,0:T(1,128)} %bitcast.24), calls=%async_computation.10 | async-start | bytes 294912 | tf_op jit(solution)/shard_map/all_to_all | solution.py:33
  1009.8 33.9 %copy-start.8 = (f32[128,4,512]{2,1,0:T(4,128)S(1)}, f32[128,4,512]{2,1,0:T(4,128)}, u32[]{:S(2)}) copy-start(f32[128,4,512]{2,1,0:T(4,128)} %reshape.333) | copy-start | bytes 3145732
  1009.8 33.9 %copy-start.41 = (f32[4,512]{1,0:T(4,128)S(1)}, f32[4,512]{1,0:T(4,128)}, u32[]{:S(2)}) copy-start(f32[4,512]{1,0:T(4,128)} %copy-done.40) | copy-start | bytes 24580
  1009.8 33.9 %copy-start.47 = (f32[128]{0:T(128)S(1)}, f32[128]{0:T(128)}, u32[]{:S(2)}) copy-start(f32[128]{0:T(128)} %copy-done.46) | copy-start | bytes 1540
  1019.1 19.1 %all-to-all-start.12 = ((bf16[4,128,512]{2,1,0:T(8,128)(2,1)}), bf16[4,128,512]{2,1,0:T(8,128)(2,1)}, u32[]{:S(2)}, u32[]{:S(2)}) async-start(bf16[4,128,512]{2,1,0:T(8,128)(2,1)} %bitcast.256), calls=%async_computation.14 | async-start | bytes 1048576 | tf_op jit(solution)/shard_map/all_to_all | solution.py:33
  1038.9 13.2 %all-to-all-start.9 = ((f32[32,1,1152]{2,1,0:T(1,128)}), f32[32,1,1152]{2,1,0:T(1,128)S(1)}, u32[]{:S(2)}, u32[]{:S(2)}) async-start(f32[32,1,1152]{2,1,0:T(1,128)} %broadcast_in_dim.35), calls=%async_computation.11 | async-start | bytes 294912 | tf_op jit(solution)/shard_map/all_to_all | solution.py:33
  1045.3 39.3 %copy-start.9 = (f32[128,2048]{1,0:T(8,128)S(1)}, f32[128,2048]{1,0:T(8,128)}, u32[]{:S(2)}) copy-start(f32[128,2048]{1,0:T(8,128)} %reshape.332) | copy-start | bytes 3145732
  1045.3 39.3 %copy-start.43 = (f32[2048]{0:T(1024)S(1)}, f32[2048]{0:T(1024)}, u32[]{:S(2)}) copy-start(f32[2048]{0:T(1024)} %param.21) | copy-start | bytes 24580
  1052.0 9.7 all-to-all-start.14
  1061.7 19.7 %all-to-all-start.5 = ((bf16[32,4,2048]{2,1,0:T(4,128)(2,1)}), bf16[32,4,2048]{2,1,0:T(4,128)(2,1)}, u32[]{:S(2)}, u32[]{:S(2)}) async-start(bf16[32,4,2048]{2,1,0:T(4,128)(2,1)} %reshape.319), calls=%async_computation.6 | async-start | bytes 1048576 | tf_op jit(solution)/shard_map/all_to_all | solution.py:33
  1082.0 9.6 all-to-all-start.15
  1091.6 19.9 %all-to-all-start.13 = ((bf16[32,4,2048]{2,1,0:T(4,128)(2,1)}), bf16[32,4,2048]{2,1,0:T(4,128)(2,1)}, u32[]{:S(2)}, u32[]{:S(2)}) async-start(bf16[32,4,2048]{2,1,0:T(4,128)(2,1)} %reshape.328), calls=%async_computation.15 | async-start | bytes 1048576 | tf_op jit(solution)/shard_map/all_to_all | solution.py:33
  (19 other events, 26.1 us)
Sparse Core Ops, SparseCore 0:
  231.2 46.1 all-gather.7
  279.8 86.2 all-gather.13
  368.0 87.4 all-gather.15
  457.2 87.4 all-gather.9
  559.2 58.3 reduce-scatter.7
  620.1 47.7 all-gather.11
  720.5 48.9 reduce-scatter.9
  805.6 35.0 reduce-scatter.13
  843.7 142.6 reduce-scatter.19
  989.3 101.4 reduce-scatter.15
  1094.4 87.7 reduce-scatter.17
  1184.4 69.7 reduce-scatter.11

commit v2 on v1

--- a/solution.py
+++ b/solution.py
@@ -1,14 +1,18 @@
+import functools
 import math
 
 import jax
 import jax.numpy as jnp
 from jax import lax
+from jax.experimental import pallas as pl
+from jax.experimental.pallas import tpu as pltpu
 from jax.sharding import PartitionSpec as P
 
 HD = 128
 EPS = 1e-06
 ROPE_BASE = 50000.0
 BOTH = ("dp", "expert")
+LIMIT = 60 * 1024 * 1024
 
 
 def rms_scale(values):
@@ -35,6 +39,248 @@
 
 def spread(block, axes, count):
     return swap(jnp.broadcast_to(block[None], (count, *block.shape)), axes)
+
+
+def neighbour(index):
+    return {"expert": index}
+
+
+def meet_neighbours(me, count):
+    barrier = pltpu.get_barrier_semaphore()
+
+    @pl.when(me > 0)
+    def _():
+        pl.semaphore_signal(
+            barrier, inc=1, device_id=neighbour(me - 1), device_id_type=pl.DeviceIdType.MESH
+        )
+
+    @pl.when(me < count - 1)
+    def _():
+        pl.semaphore_signal(
+            barrier, inc=1, device_id=neighbour(me + 1), device_id_type=pl.DeviceIdType.MESH
+        )
+
+    ends = ((me == 0) | (me == count - 1)).astype(jnp.int32)
+    pl.semaphore_wait(barrier, 2 - ends)
+
+
+def remote(source, target, send, receive, index):
+    return pltpu.make_async_remote_copy(
+        src_ref=source,
+        dst_ref=target,
+        send_sem=send,
+        recv_sem=receive,
+        device_id=neighbour(index),
+        device_id_type=pl.DeviceIdType.MESH,
+    )
+
+
+def gather_kernel(count, block, out, send_right, send_left, receive):
+    me = lax.axis_index("expert")
+    meet_neighbours(me, count)
+
+    @pl.when(me < count - 1)
+    def _():
+        remote(block, out.at[me], send_right.at[me], receive.at[me], me + 1).start()
+
+    @pl.when(me > 0)
+    def _():
+        remote(block, out.at[me], send_left.at[me], receive.at[me], me - 1).start()
+
+    out[me] = block[...]
+
+    def step(s, carry):
+        low, high = me - s, me + s
+
+        @pl.when(low >= 0)
+        def _():
+            remote(out.at[low], out.at[low], send_right.at[low], receive.at[low], me).wait_recv()
+
+            @pl.when(me < count - 1)
+            def _():
+                remote(
+                    out.at[low], out.at[low], send_right.at[low], receive.at[low], me + 1
+                ).start()
+
+        @pl.when(high < count)
+        def _():
+            remote(out.at[high], out.at[high], send_left.at[high], receive.at[high], me).wait_recv()
+
+            @pl.when(me > 0)
+            def _():
+                remote(
+                    out.at[high], out.at[high], send_left.at[high], receive.at[high], me - 1
+                ).start()
+
+        return carry
+
+    lax.fori_loop(1, count, step, 0)
+
+    def drain(b, carry):
+        @pl.when((b <= me) & (me < count - 1))
+        def _():
+            remote(block, out.at[b], send_right.at[b], receive.at[b], me + 1).wait_send()
+
+        @pl.when((b >= me) & (me > 0))
+        def _():
+            remote(block, out.at[b], send_left.at[b], receive.at[b], me - 1).wait_send()
+
+        return carry
+
+    lax.fori_loop(0, count, drain, 0)
+
+
+def gather_rows(block, number):
+    count = lax.axis_size("expert")
+    out = pl.pallas_call(
+        functools.partial(gather_kernel, count),
+        out_shape=jax.ShapeDtypeStruct((count, *block.shape), block.dtype),
+        in_specs=[pl.BlockSpec(memory_space=pltpu.VMEM)],
+        out_specs=pl.BlockSpec(memory_space=pltpu.VMEM),
+        scratch_shapes=[pltpu.SemaphoreType.DMA((count,))] * 3,
+        compiler_params=pltpu.CompilerParams(
+            collective_id=number, has_side_effects=True, vmem_limit_bytes=LIMIT
+        ),
+        cost_estimate=pl.CostEstimate(
+            flops=0, bytes_accessed=30 * count * block.size, transcendentals=0
+        ),
+    )(block)
+    return out.reshape(count * block.shape[0], *block.shape[1:])
+
+
+def add_rows(left, right, out):
+    rows = out.shape[0]
+    step = 16
+
+    def body(r, carry):
+        at = pl.ds(pl.multiple_of(r * step, step), step)
+        out[at] = (left[at].astype(jnp.float32) + right[at].astype(jnp.float32)).astype(out.dtype)
+        return carry
+
+    lax.fori_loop(0, rows // step, body, 0)
+
+
+def reduce_kernel(
+    count, parts, out, right_sums, left_sums, send_right, send_left, receive_right, receive_left
+):
+    me = lax.axis_index("expert")
+    meet_neighbours(me, count)
+
+    def step(t, carry):
+        high = count - 1 - (t - me)
+
+        @pl.when((t >= me) & (high > me))
+        def _():
+            @pl.when(me == 0)
+            def _():
+                remote(
+                    parts.at[high],
+                    right_sums.at[high],
+                    send_right.at[high],
+                    receive_right.at[high],
+                    me + 1,
+                ).start()
+
+            @pl.when(me > 0)
+            def _():
+                move = remote(
+                    right_sums.at[high],
+                    right_sums.at[high],
+                    send_right.at[high],
+                    receive_right.at[high],
+                    me + 1,
+                )
+                move.wait_recv()
+                add_rows(right_sums.at[high], parts.at[high], right_sums.at[high])
+                move.start()
+
+        low = t - (count - 1 - me)
+
+        @pl.when((low >= 0) & (low < me))
+        def _():
+            @pl.when(me == count - 1)
+            def _():
+                remote(
+                    parts.at[low],
+                    left_sums.at[low],
+                    send_left.at[low],
+                    receive_left.at[low],
+                    me - 1,
+                ).start()
+
+            @pl.when(me < count - 1)
+            def _():
+                move = remote(
+                    left_sums.at[low],
+                    left_sums.at[low],
+                    send_left.at[low],
+                    receive_left.at[low],
+                    me - 1,
+                )
+                move.wait_recv()
+                add_rows(left_sums.at[low], parts.at[low], left_sums.at[low])
+                move.start()
+
+        return carry
+
+    lax.fori_loop(0, count - 1, step, 0)
+
+    @pl.when(me == 0)
+    def _():
+        remote(
+            left_sums.at[me], left_sums.at[me], send_left.at[me], receive_left.at[me], me
+        ).wait_recv()
+        add_rows(parts.at[me], left_sums.at[me], out)
+
+    @pl.when(me > 0)
+    def _():
+        remote(
+            right_sums.at[me], right_sums.at[me], send_right.at[me], receive_right.at[me], me
+        ).wait_recv()
+        add_rows(parts.at[me], right_sums.at[me], out)
+
+        @pl.when(me < count - 1)
+        def _():
+            remote(
+                left_sums.at[me], left_sums.at[me], send_left.at[me], receive_left.at[me], me
+            ).wait_recv()
+            add_rows(out, left_sums.at[me], out)
+
+    def drain(b, carry):
+        @pl.when(b > me)
+        def _():
+            remote(
+                parts.at[b], right_sums.at[b], send_right.at[b], receive_right.at[b], me
+            ).wait_send()
+
+        @pl.when(b < me)
+        def _():
+            remote(
+                parts.at[b], left_sums.at[b], send_left.at[b], receive_left.at[b], me
+            ).wait_send()
+
+        return carry
+
+    lax.fori_loop(0, count, drain, 0)
+
+
+def reduce_rows(parts, number):
+    count = lax.axis_size("expert")
+    parts = parts.reshape(count, -1, parts.shape[-1])
+    return pl.pallas_call(
+        functools.partial(reduce_kernel, count),
+        out_shape=jax.ShapeDtypeStruct(parts.shape[1:], jnp.float32),
+        in_specs=[pl.BlockSpec(memory_space=pltpu.VMEM)],
+        out_specs=pl.BlockSpec(memory_space=pltpu.VMEM),
+        scratch_shapes=[pltpu.VMEM(parts.shape, parts.dtype)] * 2
+        + [pltpu.SemaphoreType.DMA((count,))] * 4,
+        compiler_params=pltpu.CompilerParams(
+            collective_id=number, has_side_effects=True, vmem_limit_bytes=LIMIT
+        ),
+        cost_estimate=pl.CostEstimate(
+            flops=0, bytes_accessed=30 * parts.size, transcendentals=0
+        ),
+    )(parts)
 
 
 def sum_small(values, devices):
@@ -82,6 +328,7 @@
     my_dp = lax.axis_index("dp")
     my_ex = lax.axis_index("expert")
     part = width // dps
+    piece = part // owners
     heads = part // HD
     group = dps * rows
     factor = HD ** (-0.5)
@@ -103,7 +350,8 @@
     group_lengths = lax.dynamic_index_in_dim(packed, my_ex, 1, keepdims=False)
     group_lengths = group_lengths[:, rows * slots + rows :][:, : lengths.shape[1]]
 
-    dealt_tokens = swap(tokens.reshape(devices, stripe, width)[deal], BOTH).reshape(rows, width)
+    dealt_tokens = swap(tokens.reshape(devices, stripe, width)[deal], BOTH)
+    dealt_tokens = dealt_tokens.reshape(rows, width)
     dealt_teacher = swap(teacher.reshape(devices, stripe, width)[deal], BOTH).reshape(rows, width)
 
     gate_up = []
@@ -125,28 +373,26 @@
     sine_part = jnp.sin(angles)[:, :, None, :]
     same = (segment[:, :, None] == segment[:, None, :])[:, None]
 
-    weight_parts = lax.optimization_barrier(
-        jnp.stack(
-            [
-                jnp.concatenate(
-                    [
-                        qkv_weight[:, g * width + d * part : g * width + (d + 1) * part]
-                        for g in range(3)
-                    ],
-                    axis=1,
-                )
-                for d in range(dps)
-            ]
-        )
-    )
+    mine = lax.dynamic_slice_in_dim(qkv_weight, my_ex * piece, piece, axis=0)
+    mine = jnp.stack(
+        [
+            jnp.concatenate(
+                [mine[:, g * width + d * part : g * width + (d + 1) * part] for g in range(3)],
+                axis=1,
+            )
+            for d in range(dps)
+        ]
+    )
+    mine = swap(mine, "dp").reshape(dps * piece, 3 * part)
+    weight_cols = gather_rows(mine, 1)
+    weight_cols = weight_cols.reshape(owners, dps, piece, 3 * part).transpose(1, 0, 2, 3)
+    weight_cols = weight_cols.reshape(width, 3 * part)
     tokens32 = dealt_tokens.astype(f32)
     attn_scale = rms_scale(tokens32)
     attn_normed = tokens32 * attn_scale
     attn_low = (attn_normed * attn_gain).astype(bf16)
-    attn_cols = swap(attn_low.reshape(rows, dps, part).transpose(1, 0, 2), "dp")
-    attn_cols = attn_cols.reshape(group, part)
-    qkv = jnp.einsum("tk,dkc->dtc", attn_cols, weight_parts, preferred_element_type=f32)
-    qkv = jnp.sum(swap(qkv.astype(bf16), "dp").astype(f32), axis=0)
+    attn_rows = spread(attn_low, "dp", dps).reshape(group, width)
+    qkv = dotf(attn_rows, weight_cols, ((1,), (0,)))
     queries, keys, values_low = (
         qkv[:, g * part : (g + 1) * part].reshape(dps, rows, heads, HD) for g in range(3)
     )
@@ -174,7 +420,7 @@
     ffn_scale = rms_scale(residual)
     ffn_normed = residual * ffn_scale
     feed_low = (ffn_normed * ffn_gain).astype(bf16)
-    feed = lax.all_gather(feed_low, "expert", axis=0, tiled=True)
+    feed = gather_rows(feed_low, 2)
     logits = dotf(feed, router_weight, ((1,), (0,)))
     table = group_routes[:, :, None] == jnp.arange(experts, dtype=jnp.int32)
     named = jnp.any(table, axis=1)
@@ -192,19 +438,18 @@
         inner.append((jax.nn.silu(g) * u * own_gates[:, e : e + 1]).astype(bf16))
     inner = jnp.concatenate(inner, axis=1)
     moe = dotf(inner, down, ((1,), (0,)))
-    moe = lax.psum_scatter(moe.astype(bf16), "expert", scatter_dimension=0, tiled=True)
-    result = residual + moe.astype(f32)
+    moe = reduce_rows(moe.astype(bf16), 3)
+    result = residual + moe
 
     keep = counted.astype(f32)[:, None]
     error_rows = result - dealt_teacher.astype(f32)
     part_square = jnp.sum(keep * error_rows * error_rows)
     grad_result = (2.0 * (rows * devices) / valid_total) * keep * error_rows
 
-    grad_rows = lax.all_gather(grad_result.astype(bf16), "expert", axis=0, tiled=True)
+    grad_rows = gather_rows(grad_result.astype(bf16), 4)
     grad_feed = 0.0
-    gate_grads, grad_gate_up_w = [], []
+    gate_grads, grad_gus = [], []
     grad_inner_raw = dotf(grad_rows, down, ((1,), (1,)))
-    grad_down_w = dotf(inner, grad_rows, ((0,), (0,)))
     for e in range(local):
         g, u = gate_rows[e], up_rows[e]
         sg = jax.nn.sigmoid(g)
@@ -215,11 +460,13 @@
         grad_g = grad_inner * u * sg * (1.0 + g * (1.0 - sg))
         grad_u = grad_inner * silu
         grad_gu = jnp.concatenate([grad_g, grad_u], axis=1).astype(bf16)
-        grad_gate_up_w.append(dotf(feed, grad_gu, ((0,), (0,))))
+        grad_gus.append(grad_gu)
         grad_feed = grad_feed + dotf(grad_gu, gate_up[e], ((1,), (1,)))
-    grad_feed = lax.psum_scatter(
-        grad_feed.astype(bf16), "expert", scatter_dimension=0, tiled=True
-    ).astype(f32)
+    grad_down_w = dotf(inner, grad_rows, ((0,), (0,))).astype(bf16)
+    grad_feed = reduce_rows(grad_feed.astype(bf16), 5)
+    grad_gate_up_w = []
+    for e in range(local):
+        grad_gate_up_w.append(dotf(feed, grad_gus[e], ((0,), (0,))).astype(bf16))
     gate_grad = swap(
         jnp.stack(gate_grads, axis=0).reshape(local, owners, rows).transpose(1, 0, 2), "expert"
     )
@@ -243,7 +490,8 @@
     grad_resid = grad_result + norm_back(grad_feed * ffn_gain, ffn_normed, ffn_scale)
 
     early = sum_small((part_square, grad_ffn_gain, grad_router), devices)
-    grad_attn = spread(grad_resid.astype(bf16), "dp", dps).reshape(group, width)
+    grad_attn = spread(grad_resid.astype(bf16), "dp", dps)
+    grad_attn = grad_attn.reshape(group, width)
     grad_out_w = dotf(mixed_low, grad_attn, ((0,), (0,)))
     grad_mixed = dotf(grad_attn, out_weight, ((1,), (1,)))
     grad_mixed = grad_mixed.reshape(dps, rows, heads, HD).astype(bf16)
@@ -271,35 +519,30 @@
         ],
         axis=1,
     )
-    grad_qkv = spread(grad_qkv, "dp", dps)
-    grad_qkv_w = [dotf(attn_cols, grad_qkv[d], ((0,), (0,))).astype(bf16) for d in range(dps)]
-    grad_qkv_w = jnp.concatenate(
-        [grad_qkv_w[d][:, g * part : (g + 1) * part] for g in range(3) for d in range(dps)], axis=1
-    )
-    grad_normed = jnp.einsum("dtc,dkc->tk", grad_qkv, weight_parts, preferred_element_type=f32)
-    grad_normed = swap(grad_normed.astype(bf16).reshape(dps, rows, part), "dp")
-    grad_normed = grad_normed.transpose(1, 0, 2).reshape(rows, width).astype(f32)
+    grad_normed = dotf(grad_qkv, weight_cols, ((1,), (1,))).astype(bf16)
+    grad_normed = swap(grad_normed.reshape(dps, rows, width), "dp")
+    grad_normed = jnp.sum(grad_normed.astype(f32), axis=0)
+    grad_qkv_w = dotf(attn_rows, grad_qkv, ((0,), (0,))).astype(bf16)
     grad_attn_gain = jnp.sum(grad_normed * attn_normed, axis=0)
     grad_tokens = grad_resid + norm_back(grad_normed * attn_gain, attn_normed, attn_scale)
 
-    qkv_out = lax.psum_scatter(
-        grad_qkv_w, "expert", scatter_dimension=0, tiled=True
+    grad_qkv_w = grad_qkv_w.reshape(dps, owners, piece, 3 * part).transpose(1, 0, 2, 3)
+    grad_qkv_w = reduce_rows(grad_qkv_w.reshape(-1, 3 * part), 6).astype(bf16)
+    grad_qkv_w = swap(grad_qkv_w.reshape(dps, piece, 3 * part), "dp")
+    qkv_out = jnp.concatenate(
+        [grad_qkv_w[d, :, g * part : (g + 1) * part] for g in range(3) for d in range(dps)], axis=1
     ).astype(f32)
-    out_out = lax.psum_scatter(
-        grad_out_w.astype(bf16), "expert", scatter_dimension=0, tiled=True
-    ).astype(f32)
-    gate_up_out = jnp.stack(
-        [
-            lax.psum_scatter(w.astype(bf16), "dp", scatter_dimension=0, tiled=True).astype(f32)
-            for w in grad_gate_up_w
-        ]
-    )
+    out_out = reduce_rows(grad_out_w.astype(bf16), 7)
     down_out = lax.psum_scatter(
-        grad_down_w.astype(bf16).reshape(local, hidden, width),
-        "dp",
-        scatter_dimension=1,
-        tiled=True,
-    ).astype(f32)
+        grad_down_w.reshape(local, hidden, width), "dp", scatter_dimension=1, tiled=True
+    )
+    down_out = down_out.astype(f32)
+    gate_up_out = []
+    for e in range(local):
+        gate_up_out.append(
+            lax.psum_scatter(grad_gate_up_w[e], "dp", scatter_dimension=0, tiled=True)
+        )
+    gate_up_out = jnp.stack([w.astype(f32) for w in gate_up_out])
     late = sum_small((grad_query_gain, grad_key_gain, grad_attn_gain), devices)
     mean_loss = early[0] / (valid_total * width)
 

time: 1270 us -> 943 us (0.74)
  waiting for transfers between devices: 682 us -> 140 us
  Pallas kernels: 0 us -> 321 us
  blocking collectives: 135 us -> 32.5 us
  other arithmetic: 89.9 us -> 76.7 us
    pallas_call x0 -> x7, Pallas kernels: none -> 321 us  [the longest x4 168 us: reduce_rows(): pl.pallas_call(functools.partial(reduce_kernel, count), out_shape=jax.Sha...]
    reduce_scatter x7 -> x3, waiting for transfers between devices: 193 us -> 0.01 us  [the longest x2 0.01 us: on_device(): lax.psum_scatter(grad_gate_up_w[e], 'dp', scatter_dimension=0, tiled=True)]
    all_gather x2, waiting for transfers between devices: 156 us -> 0.02 us  [on_device(): gate_up.append(lax.all_gather(gate_up_weight[e], 'dp', axis=0, tiled=True))]
    all_to_all x2, blocking collectives: 135 us -> 32.5 us  [swap(): return lax.all_to_all(pieces, axes, split_axis=0, concat_axis=0, tiled=True)]
    all_gather x2 -> x0, waiting for transfers between devices: 86.6 us -> none  [the longest x1 47.9 us: on_device(): lax.all_gather(grad_result.astype(bf16), 'expert', axis=0, tiled=True)]
    all_gather x1, waiting for transfers between devices: 71 us -> 0.01 us  [on_device(): down = lax.all_gather(down_weight, 'dp', axis=1, tiled=True)]
    all_to_all x14, waiting for transfers between devices: 174 us -> 138 us  [swap(): return lax.all_to_all(pieces, axes, split_axis=0, concat_axis=0, tiled=True)]
    dot_general x2 -> x0, matrix products: 17.4 us -> none  [the longest x1 9.24 us: on_device(): jnp.einsum('dtc,dkc->tk', grad_qkv, weight_parts, preferred_element_type=...]
  transfers between devices with their start and end apart: 26 -> 20, of which waited for: 22 -> 10; matrix products, arithmetic and copies ran while one was open for 17% -> 31% of each run, Pallas kernels for 0% -> 25%
where the time goes in v2:
time: 943 us; the launch traced here: 935 us
  Pallas kernels  321 us (34%)
  matrix products  171 us (18%)
  waiting for transfers between devices  140 us (15%)
  local copies, waits for them, and re-layouts  118 us (13%)
  other arithmetic  76.7 us (8%)
  starting transfers between devices  57.5 us (6%)
  blocking collectives  32.5 us (3%)
  between operations  18.2 us (2%)
    pallas_call x4, Pallas kernels, reduce_rows(): pl.pallas_call(functools.partial(reduce_kernel, count), out_shape=jax.Sha...  168 us
    dot_general x16, matrix products, dotf(): lax.dot_general(left, right, (dims, ((), ())), preferred_element_type=jnp...  155 us
    pallas_call x3, Pallas kernels, gather_rows(): pl.pallas_call(functools.partial(gather_kernel, count), out_shape=jax.Sha...  153 us
    all_to_all x14, waiting for transfers between devices, swap(): return lax.all_to_all(pieces, axes, split_axis=0, concat_axis=0, tiled=True)  138 us
    all_to_all x14, starting transfers between devices, swap(): return lax.all_to_all(pieces, axes, split_axis=0, concat_axis=0, tiled=True)  57.2 us
    unnamed x171, local copies, waits for them, and re-layouts  35.3 us
    all_to_all x2, blocking collectives, swap(): return lax.all_to_all(pieces, axes, split_axis=0, concat_axis=0, tiled=True)  32.5 us
  transfers between devices with their start and end apart: 20, of which 10 were waited for; matrix products, arithmetic and copies ran while one was open for 31% of the time, Pallas kernels for 25%

profile of v2, /device:TPU:0, one launch (start us, length us, event | category | flops | bytes accessed | tf_op | source)
XLA Modules:
  0.0 934.7 jit_solution(6542440817640504699)
XLA Ops:
  7.2 5.0 fusion.83
  15.2 7.3 all-to-all-start
  24.3 14.6 %all-to-all-done = bf16[32,4,2048]{2,1,0:T(4,128)(2,1)S(1)} async-done(((bf16[32,4,2048]{2,1,0:T(4,128)(2,1)}), bf16[32,4,2048]{2,1,0:T(4,128)(2,1)S(1)}, u32[]{:S(2)}, u32[]{:S(2)}) %all-to-all-start) | async-done | bytes 524320 | tf_op jit(solution)/shard_map/all_to_all | solution.py:37
  39.7 3.3 all-to-all-start.3
  44.4 7.2 all-to-all-done.3
  51.6 4.2 all-to-all-start.2
  58.7 13.9 %all-to-all-done.2 = bf16[4,64,1536]{2,1,0:T(8,128)(2,1)} async-done(((bf16[4,64,1536]{2,1,0:T(8,128)(2,1)}), bf16[4,64,1536]{2,1,0:T(8,128)(2,1)}, u32[]{:S(2)}, u32[]{:S(2)}) %all-to-all-start.2) | async-done | bytes 786464 | tf_op jit(solution)/shard_map/all_to_all | solution.py:37
  75.3 4.4 all-to-all-start.1
  87.4 61.2 %shard_map.238 = bf16[8,256,1536]{2,1,0:T(8,128)(2,1)} custom-call(bf16[256,1536]{1,0:T(8,128)(2,1)} %bitcast.5.block), custom_call_target="tpu_custom_call" | custom-call | bytes 94371840 | tf_op jit(solution)/shard_map/pallas_call | solution.py:135
  148.6 6.1 copy.194
  154.7 3.5 all-to-all-start.6
  158.2 6.2 fusion.87
  183.7 3.4 fusion.85
  187.1 3.2 fusion.23
  194.3 4.5 all-to-all-start.4
  204.4 42.9 %all-to-all-done.4 = bf16[4,128,2048]{2,1,0:T(8,128)(2,1)} async-done(((bf16[4,128,2048]{2,1,0:T(8,128)(2,1)}), bf16[4,128,2048]{2,1,0:T(8,128)(2,1)}, u32[]{:S(2)}, u32[]{:S(2)}) %all-to-all-start.4) | async-done | bytes 2097184 | tf_op jit(solution)/shard_map/all_to_all | solution.py:37
  247.4 3.0 convert_reduce_fusion.1
  257.4 44.9 %shard_map.239 = bf16[8,128,2048]{2,1,0:T(8,128)(2,1)} custom-call(bf16[128,2048]{1,0:T(8,128)(2,1)} %get-tuple-element.102.block), custom_call_target="tpu_custom_call" | custom-call | bytes 62914560 | tf_op jit(solution)/shard_map/pallas_call | solution.py:135
  302.3 3.4 fusion.86
  306.4 12.5 %fusion.7 = f32[1024,2048]{1,0:T(8,128)S(1)} fusion(bf16[1024,2048]{1,0:T(8,128)(2,1)} %bitcast.241, bf16[1,2048,2048]{2,1,0:T(8,128)(2,1)} %all-gather.8.cloned.1.call-done), kind=kOutput, calls=%fused_computation.12 | convolution fusion | flops 8589934592 | bytes 20971520 | tf_op jit(solution)/shard_map/dot_general | solution.py:33
  318.9 3.4 copy-done.1
  324.9 12.5 %fusion.3 = f32[1024,2048]{1,0:T(8,128)S(1)} fusion(bf16[1024,2048]{1,0:T(8,128)(2,1)} %bitcast.242, bf16[1,2048,2048]{2,1,0:T(8,128)(2,1)} %all-gather.10.cloned.1.call-done), kind=kOutput, calls=%fused_computation.8 | convolution fusion | flops 8589934592 | bytes 20971520 | tf_op jit(solution)/shard_map/dot_general | solution.py:33
  337.4 3.2 copy-done.2
  343.1 14.4 %convolution_convert_fusion.4 = bf16[1024,2048]{1,0:T(8,128)(2,1)} fusion(bf16[2048,2048]{1,0:T(8,128)(2,1)} %bitcast.290, bf16[1024,1024]{1,0:T(8,128)(2,1)} %multiply_convert_fusion.4, bf16[1024,1024]{1,0:T(8,128)(2,1)} %multiply_convert_fusion.5), kind=kOutput, calls=%fused_computation.41 | convolution fusion | flops 8600420352 | bytes 16777216 | tf_op jit(solution)/shard_map/dot_general | solution.py:33
  357.4 40.2 %shard_map.240 = f32[128,2048]{1,0:T(8,128)} custom-call(bf16[8,128,2048]{2,1,0:T(8,128)(2,1)} %bitcast.250), custom_call_target="tpu_custom_call" | custom-call | bytes 62914560 | tf_op jit(solution)/shard_map/pallas_call | solution.py:270
  397.6 3.2 multiply_convert_fusion.9
  400.9 46.6 %shard_map.241 = bf16[8,128,2048]{2,1,0:T(8,128)(2,1)} custom-call(bf16[128,2048]{1,0:T(8,128)(2,1)} %get-tuple-element.100.block), custom_call_target="tpu_custom_call" | custom-call | bytes 62914560 | tf_op jit(solution)/shard_map/pallas_call | solution.py:135
  447.5 12.6 %fusion.88 = f32[1024,2048]{1,0:T(8,128)S(1)} fusion(bf16[1024,2048]{1,0:T(8,128)(2,1)} %bitcast.251, bf16[2048,2048]{1,0:T(8,128)(2,1)} %bitcast.291), kind=kOutput, calls=%fused_computation.231 | convolution fusion | flops 8589934592 | bytes 20971520 | tf_op jit(solution)/shard_map/dot_general | solution.py:33
  460.1 10.5 %multiply_reduce_fusion.1 = (f32[1024]{0:T(1024)S(1)}, f32[1024]{0:T(1024)S(1)}, bf16[1024,1024]{1,0:T(8,128)(2,1)}, bf16[1024,1024]{1,0:T(8,128)(2,1)}, bf16[10...) fusion(f32[1024,2048]{1,0:T(8,128)S(1)} %fusion.88, f32[1024,2048]{1,0:T(8,128)} %copy-done.1, ...), kind=kLoop, calls=%fused_computation.25 | loop fusion | flops 35649536 | bytes 33570816 | tf_op jit(solution)/shard_map/reduce_sum | solution.py:458
  472.6 11.7 %convolution_convert_fusion.2 = bf16[2048,2048]{1,0:T(8,128)(2,1)} fusion(bf16[1024,2048]{1,0:T(8,128)(2,1)S(1)} %bitcast.244, bf16[1024,1024]{1,0:T(8,128)(2,1)S(1)} %get-tuple-element.110, bf16[1024,1024]{1,0:T(8,128)(2,1)S(1)} %get-tuple-element.111), kind=kOutput, calls=%fused_computation.17 | convolution fusion | flops 8602517504 | bytes 16777216 | tf_op jit(solution)/shard_map/dot_general | solution.py:33
  484.3 14.2 %convolution_convert_fusion.1 = bf16[2048,2048]{1,0:T(8,128)(2,1)} fusion(bf16[1024,2048]{1,0:T(8,128)(2,1)} %bitcast.243, bf16[1024,1024]{1,0:T(8,128)(2,1)} %get-tuple-element.108, bf16[1024,1024]{1,0:T(8,128)(2,1)} %get-tuple-element.109), kind=kOutput, calls=%fused_computation.16 | convolution fusion | flops 8602517504 | bytes 16777216 | tf_op jit(solution)/shard_map/dot_general | solution.py:33
  499.2 3.3 all-to-all-start.7
  502.5 14.4 %convolution_convert_fusion = bf16[2048,2048]{1,0:T(8,128)(2,1)} fusion(bf16[1024,2048]{1,0:T(8,128)(2,1)} %bitcast.252, bf16[1024,1024]{1,0:T(8,128)(2,1)} %multiply_convert_fusion.4, bf16[1024,1024]{1,0:T(8,128)(2,1)} %multiply_convert_fusion.5), kind=kOutput, calls=%fused_computation.15 | convolution fusion | flops 8602517504 | bytes 16777216 | tf_op jit(solution)/shard_map/dot_general | solution.py:33
  517.0 15.0 %fusion.1 = f32[1024,2048]{1,0:T(8,128)} fusion(bf16[1,2048,2048]{2,1,0:T(8,128)(2,1)} %all-gather.10.cloned.1.call-done, bf16[1024,1024]{1,0:T(8,128)(2,1)} %get-tuple-element.108, bf16[1024,1024]{1,0:T(8,128)(2,1)} %get-tuple-element.109), kind=kOutput, calls=%fused_computation.6 | convolution fusion | flops 8598323200 | bytes 20971520 | tf_op jit(solution)/shard_map/dot_general | solution.py:33
  531.9 14.6 %add_convert_fusion = bf16[1024,2048]{1,0:T(8,128)(2,1)} fusion(f32[1024,2048]{1,0:T(8,128)} %fusion.1, bf16[1,2048,2048]{2,1,0:T(8,128)(2,1)} %all-gather.8.cloned.1.call-done, bf16[1024,1024]{1,0:T(8,128)(2,1)S(1)} %copy-done.28, bf16[1024,1024]{1,0:T(8,128)(2,1)} %copy-done.29), kind=kOutput, calls=%fused_computation.14 | convolution fusion | flops 8602517504 | bytes 25165824 | tf_op jit(solution)/shard_map/dot_general | solution.py:33
  546.5 41.3 %shard_map.242 = f32[128,2048]{1,0:T(8,128)} custom-call(bf16[8,128,2048]{2,1,0:T(8,128)(2,1)} %bitcast.249), custom_call_target="tpu_custom_call" | custom-call | bytes 62914560 | tf_op jit(solution)/shard_map/pallas_call | solution.py:270
  588.6 2.7 fusion.61
  595.1 3.6 fusion.82
  599.5 13.8 %all_to_all.91 = f32[32,1,1152]{2,1,0:T(1,128)S(1)} all-to-all(f32[32,1,1152]{2,1,0:T(1,128)S(1)} %bitcast.266), channel_id=1, replica_groups=mesh['dp'=4,'expert'=8] {'dp','expert'}, dimensions={0} | all-to-all | bytes 294912 | tf_op jit(solution)/shard_map/all_to_all | solution.py:37
  618.0 7.1 all-to-all-done.9
  625.1 18.7 %all_to_all.92 = bf16[32,4,2048]{2,1,0:T(4,128)(2,1)} all-to-all(bf16[32,4,2048]{2,1,0:T(4,128)(2,1)S(1)} %reshape.371), channel_id=1, replica_groups=mesh['dp'=4,'expert'=8] {'dp','expert'}, dimensions={0} | all-to-all | bytes 1048576 | tf_op jit(solution)/shard_map/all_to_all | solution.py:37
  646.4 4.5 all-to-all-start.10
  660.3 23.2 %all-to-all-done.10 = bf16[4,128,2048]{2,1,0:T(8,128)(2,1)} async-done(((bf16[4,128,2048]{2,1,0:T(8,128)(2,1)}), bf16[4,128,2048]{2,1,0:T(8,128)(2,1)}, u32[]{:S(2)}, u32[]{:S(2)}) %all-to-all-start.10) | async-done | bytes 2097184 | tf_op jit(solution)/shard_map/all_to_all | solution.py:37
  683.5 2.9 fusion.20
  693.5 2.9 copy.217
  696.4 3.1 multiply_reduce_fusion.5
  700.4 3.0 copy.211
  703.4 3.7 fusion.24
  717.5 5.9 convolution_convert_fusion.3
  723.4 3.4 copy.222
  726.8 56.4 %shard_map.243 = f32[256,1536]{1,0:T(8,128)} custom-call(bf16[8,256,1536]{2,1,0:T(8,128)(2,1)} %bitcast.239), custom_call_target="tpu_custom_call" | custom-call | bytes 94371840 | tf_op jit(solution)/shard_map/pallas_call | solution.py:270
  785.6 3.5 all-to-all-start.13
  789.1 4.3 convolution_convert_fusion.5
  793.3 30.3 %shard_map.244 = f32[64,2048]{1,0:T(8,128)} custom-call(bf16[8,64,2048]{2,1,0:T(8,128)(2,1)} %bitcast.260), custom_call_target="tpu_custom_call" | custom-call | bytes 31457280 | tf_op jit(solution)/shard_map/pallas_call | solution.py:270
  823.7 7.9 convolution_convert_fusion.6
  832.5 4.5 all-to-all-start.11
  848.9 13.3 %all-to-all-done.11 = bf16[4,128,2048]{2,1,0:T(8,128)(2,1)} async-done(((bf16[4,128,2048]{2,1,0:T(8,128)(2,1)}), bf16[4,128,2048]{2,1,0:T(8,128)(2,1)}, u32[]{:S(2)}, u32[]{:S(2)}) %all-to-all-start.11) | async-done | bytes 2097184 | tf_op jit(solution)/shard_map/all_to_all | solution.py:37
  862.2 3.0 convert_reduce_fusion
  870.5 5.6 all-to-all-start.14
  876.3 7.0 all-to-all-done.14
  893.6 3.4 all-to-all-start.12
  906.4 6.8 all-to-all-done.12
  915.4 6.2 maximum_convert_fusion
  921.5 4.2 convert_element_type.209
  (312 shorter events, 146.1 us)
Async XLA Ops:
  7.2 184.5 %copy-start = (bf16[512,2048]{1,0:T(8,128)(2,1)S(1)}, bf16[512,2048]{1,0:T(8,128)(2,1)}, u32[]{:S(2)}) copy-start(bf16[512,2048]{1,0:T(8,128)(2,1)} %param.18) | copy-start | bytes 6291460
  7.2 299.2 %all-gather.8.cloned.1.call-start = ((), (), s32[]{:S(2)}) async-start(), calls=%async_computation.23 | async-start | bytes 10485760 | tf_op jit(solution)/shard_map/all_gather | solution.py:359
  12.2 10.4 %copy-start.70 = (s32[128,8]{0,1:T(8,128)S(1)}, s32[128,8]{0,1:T(8,128)}, u32[]{:S(2)}) copy-start(s32[128,8]{0,1:T(8,128)} %param.27) | copy-start | bytes 12292
  12.2 10.6 %copy-start.72 = (s32[1,4]{1,0:T(1,128)S(1)}, s32[1,4]{1,0:T(1,128)}, u32[]{:S(2)}) copy-start(s32[1,4]{1,0:T(1,128)} %param.29) | copy-start | bytes 52
  12.2 10.6 %copy-start.73 = (s32[128]{0:T(128)S(1)}, s32[128]{0:T(128)}, u32[]{:S(2)}) copy-start(s32[128]{0:T(128)} %param.28) | copy-start | bytes 1540
  12.2 312.6 %all-gather.10.cloned.1.call-start = ((), (), s32[]{:S(2)}) async-start(), calls=%async_computation.24 | async-start | bytes 10485760 | tf_op jit(solution)/shard_map/all_gather | solution.py:359
  13.5 10.9 %copy-start.71 = (s32[32]{0:T(128)}, s32[32]{0:T(128)S(1)}, u32[]{:S(2)}) copy-start(s32[32]{0:T(128)S(1)} %compare_select_fusion.1) | copy-start | bytes 388
  15.2 23.7 %all-to-all-start = ((bf16[32,4,2048]{2,1,0:T(4,128)(2,1)}), bf16[32,4,2048]{2,1,0:T(4,128)(2,1)S(1)}, u32[]{:S(2)}, u32[]{:S(2)}) async-start(bf16[32,4,2048]{2,1,0:T(4,128)(2,1)} %gather_fusion), calls=%async_computation | async-start | bytes 1048576 | tf_op jit(solution)/shard_map/all_to_all | solution.py:37
  22.8 34.8 %copy-start.53 = (f32[2048]{0:T(1024)S(1)}, f32[2048]{0:T(1024)}, u32[]{:S(2)}) copy-start(f32[2048]{0:T(1024)} %param.21) | copy-start | bytes 24580
  38.9 16.9 %copy-start.12 = (bf16[32,4,2048]{2,1,0:T(4,128)(2,1)}, bf16[32,4,2048]{2,1,0:T(4,128)(2,1)S(1)}, u32[]{:S(2)}) copy-start(bf16[32,4,2048]{2,1,0:T(4,128)(2,1)S(1)} %all-to-all-done) | copy-start | bytes 1572868
  39.7 11.8 %all-to-all-start.3 = ((s32[32,1,1280]{2,1,0:T(1,128)}), s32[32,1,1280]{2,1,0:T(1,128)}, u32[]{:S(2)}, u32[]{:S(2)}) async-start(s32[32,1,1280]{2,1,0:T(1,128)} %broadcast_in_dim.27), calls=%async_computation.3 | async-start | bytes 327680 | tf_op jit(solution)/shard_map/all_to_all | solution.py:37
  51.6 21.1 %all-to-all-start.2 = ((bf16[4,64,1536]{2,1,0:T(8,128)(2,1)}), bf16[4,64,1536]{2,1,0:T(8,128)(2,1)}, u32[]{:S(2)}, u32[]{:S(2)}) async-start(bf16[4,64,1536]{2,1,0:T(8,128)(2,1)} %pad_maximum_fusion.12), calls=%async_computation.2 | async-start | bytes 1572864 | tf_op jit(solution)/shard_map/all_to_all | solution.py:37
  56.5 18.8 %copy-start.68 = (f32[128]{0:T(128)}, f32[128]{0:T(128)S(1)}, u32[]{:S(2)}) copy-start(f32[128]{0:T(128)S(1)} %rsqrt.40) | copy-start | bytes 1540
  57.6 17.6 %copy-start.8 = (f32[128,2048]{1,0:T(8,128)}, f32[128,2048]{1,0:T(8,128)S(1)}, u32[]{:S(2)}) copy-start(f32[128,2048]{1,0:T(8,128)S(1)} %reshape.389) | copy-start | bytes 3145732
  75.3 79.4 %all-to-all-start.1 = ((bf16[4,128,2048]{2,1,0:T(8,128)(2,1)}), bf16[4,128,2048]{2,1,0:T(8,128)(2,1)}, u32[]{:S(2)}, u32[]{:S(2)}) async-start(bf16[4,128,2048]{2,1,0:T(8,128)(2,1)} %broadcast_in_dim.26), calls=%async_computation.1 | async-start | bytes 4194304 | tf_op jit(solution)/shard_map/all_to_all | solution.py:37
  79.7 263.4 %all-gather.6.cloned.1.call-start = ((), (), s32[]{:S(2)}) async-start(), calls=%async_computation.19 | async-start | bytes 10485760 | tf_op jit(solution)/shard_map/all_gather | solution.py:360
  85.5 101.6 %copy-start.55 = (pred[4,128,128]{1,2,0:T(8,128)(4,1)}, pred[4,128,128]{1,2,0:T(8,128)(4,1)S(1)}, u32[]{:S(2)}) copy-start(pred[4,128,128]{1,2,0:T(8,128)(4,1)S(1)} %broadcast_compare_fusion) | copy-start | bytes 196612
  87.4 89.9 %copy-start.18 = (f32[4,128,64]{2,1,0:T(8,128)}, f32[4,128,64]{2,1,0:T(8,128)S(1)}, u32[]{:S(2)}) copy-start(f32[4,128,64]{2,1,0:T(8,128)S(1)} %get-tuple-element.150) | copy-start | bytes 393220
  154.7 39.6 %all-to-all-start.6 = ((bf16[32,4,2048]{2,1,0:T(4,128)(2,1)}), bf16[32,4,2048]{2,1,0:T(4,128)(2,1)}, u32[]{:S(2)}, u32[]{:S(2)}) async-start(bf16[32,4,2048]{2,1,0:T(4,128)(2,1)} %gather_fusion.2), calls=%async_computation.6 | async-start | bytes 1048576 | tf_op jit(solution)/shard_map/all_to_all | solution.py:37
  166.7 8.6 copy-start.62
  168.3 8.6 copy-start.65
  172.3 7.1 copy-start.4
  187.1 7.2 copy-start.56
  194.3 53.1 %all-to-all-start.4 = ((bf16[4,128,2048]{2,1,0:T(8,128)(2,1)}), bf16[4,128,2048]{2,1,0:T(8,128)(2,1)}, u32[]{:S(2)}, u32[]{:S(2)}) async-start(bf16[4,128,2048]{2,1,0:T(8,128)(2,1)} %bitcast.261), calls=%async_computation.4 | async-start | bytes 4194304 | tf_op jit(solution)/shard_map/all_to_all | solution.py:37
  198.8 716.6 %reduce-scatter.4.cloned.1.call-start = ((), (), s32[]{:S(2)}) async-start(), calls=%async_computation.20 | async-start | bytes 10485760 | tf_op jit(solution)/shard_map/reduce_scatter | solution.py:543
  202.2 52.6 %copy-start.9 = (f32[128,2048]{1,0:T(8,128)S(1)}, f32[128,2048]{1,0:T(8,128)}, u32[]{:S(2)}) copy-start(f32[128,2048]{1,0:T(8,128)} %copy-done.8) | copy-start | bytes 3145732
  202.2 52.6 %copy-start.51 = (f32[2048]{0:T(1024)S(1)}, f32[2048]{0:T(1024)}, u32[]{:S(2)}) copy-start(f32[2048]{0:T(1024)} %param.22) | copy-start | bytes 24580
  254.8 47.5 %copy-start.60 = (f32[128]{0:T(128)}, f32[128]{0:T(128)S(1)}, u32[]{:S(2)}) copy-start(f32[128]{0:T(128)S(1)} %rsqrt.44) | copy-start | bytes 1540
  254.8 47.5 %copy-start.42 = (bf16[2048,16]{0,1:T(8,128)(2,1)S(1)}, bf16[2048,16]{0,1:T(8,128)(2,1)}, u32[]{:S(2)}) copy-start(bf16[2048,16]{0,1:T(8,128)(2,1)} %param.23) | copy-start | bytes 196612
  357.4 40.2 %copy-start.11 = (f32[128,2048]{1,0:T(8,128)S(1)}, f32[128,2048]{1,0:T(8,128)}, u32[]{:S(2)}) copy-start(f32[128,2048]{1,0:T(8,128)} %get-tuple-element.103) | copy-start | bytes 3145732
  460.0 12.5 %copy-start.3 = (bf16[8,128,2048]{2,1,0:T(8,128)(2,1)S(1)}, bf16[8,128,2048]{2,1,0:T(8,128)(2,1)}, u32[]{:S(2)}) copy-start(bf16[8,128,2048]{2,1,0:T(8,128)(2,1)} %shard_map.239) | copy-start | bytes 12582916
  484.3 431.1 %reduce-scatter.6.cloned.1.call-start = ((), (), s32[]{:S(2)}) async-start(), calls=%async_computation.21 | async-start | bytes 10485760 | tf_op jit(solution)/shard_map/reduce_scatter | solution.py:543
  499.2 88.7 %all-to-all-start.7 = ((f32[8,2,128]{2,1,0:T(2,128)}), f32[8,2,128]{2,1,0:T(2,128)S(1)}, u32[]{:S(2)}, u32[]{:S(2)}) async-start(f32[8,2,128]{2,1,0:T(2,128)} %maximum_bitcast_fusion.4), calls=%async_computation.7 | async-start | bytes 16384 | tf_op jit(solution)/shard_map/all_to_all | solution.py:37
  502.5 419.0 %reduce-scatter.8.cloned.1.call-start = ((), (), s32[]{:S(2)}) async-start(), calls=%async_computation.22 | async-start | bytes 10485760 | tf_op jit(solution)/shard_map/reduce_scatter | solution.py:536
  517.0 15.0 %copy-start.28 = (bf16[1024,1024]{1,0:T(8,128)(2,1)S(1)}, bf16[1024,1024]{1,0:T(8,128)(2,1)}, u32[]{:S(2)}) copy-start(bf16[1024,1024]{1,0:T(8,128)(2,1)} %copy-done.27) | copy-start | bytes 6291460
  546.5 46.3 %copy-start.43 = (bf16[2048,16]{0,1:T(8,128)(2,1)S(1)}, bf16[2048,16]{0,1:T(8,128)(2,1)}, u32[]{:S(2)}) copy-start(bf16[2048,16]{0,1:T(8,128)(2,1)} %param.23) | copy-start | bytes 196612
  546.5 46.3 %copy-start.52 = (f32[2048]{0:T(1024)S(1)}, f32[2048]{0:T(1024)}, u32[]{:S(2)}) copy-start(f32[2048]{0:T(1024)} %param.22) | copy-start | bytes 24580
  546.5 46.3 %copy-start.61 = (f32[128]{0:T(128)S(1)}, f32[128]{0:T(128)}, u32[]{:S(2)}) copy-start(f32[128]{0:T(128)} %copy-done.60) | copy-start | bytes 1540
  614.1 11.0 %all-to-all-start.9 = ((f32[32,1,1152]{2,1,0:T(1,128)}), f32[32,1,1152]{2,1,0:T(1,128)S(1)}, u32[]{:S(2)}, u32[]{:S(2)}) async-start(f32[32,1,1152]{2,1,0:T(1,128)} %broadcast_in_dim.36), calls=%async_computation.9 | async-start | bytes 294912 | tf_op jit(solution)/shard_map/all_to_all | solution.py:37
  617.9 34.4 %copy-start.63 = (f32[128]{0:T(128)S(1)}, f32[128]{0:T(128)}, u32[]{:S(2)}) copy-start(f32[128]{0:T(128)} %param.20) | copy-start | bytes 1540
  618.0 34.4 %copy-start.66 = (f32[128]{0:T(128)S(1)}, f32[128]{0:T(128)}, u32[]{:S(2)}) copy-start(f32[128]{0:T(128)} %param.19) | copy-start | bytes 1540
  618.0 35.0 %copy-start.48 = (f32[4,128,4]{1,2,0:T(4,128)S(1)}, f32[4,128,4]{1,2,0:T(4,128)}, u32[]{:S(2)}) copy-start(f32[4,128,4]{1,2,0:T(4,128)} %copy-done.47) | copy-start | bytes 24580
  618.0 35.9 %copy-start.50 = (f32[4,128,4]{1,2,0:T(4,128)S(1)}, f32[4,128,4]{1,2,0:T(4,128)}, u32[]{:S(2)}) copy-start(f32[4,128,4]{1,2,0:T(4,128)} %copy-done.49) | copy-start | bytes 24580
  646.4 37.1 %all-to-all-start.10 = ((bf16[4,128,2048]{2,1,0:T(8,128)(2,1)}), bf16[4,128,2048]{2,1,0:T(8,128)(2,1)}, u32[]{:S(2)}, u32[]{:S(2)}) async-start(bf16[4,128,2048]{2,1,0:T(8,128)(2,1)} %broadcast_in_dim.37), calls=%async_computation.10 | async-start | bytes 4194304 | tf_op jit(solution)/shard_map/all_to_all | solution.py:37
  659.4 27.1 %copy-start.57 = (f32[4,4,128]{2,1,0:T(4,128)S(1)}, f32[4,4,128]{2,1,0:T(4,128)}, u32[]{:S(2)}) copy-start(f32[4,4,128]{2,1,0:T(4,128)} %copy-done.56) | copy-start | bytes 24580
  660.3 26.2 %copy-start.30 = (f32[4,4,128,128]{2,3,1,0:T(8,128)S(1)}, f32[4,4,128,128]{2,3,1,0:T(8,128)}, u32[]{:S(2)}) copy-start(f32[4,4,128,128]{2,3,1,0:T(8,128)} %get-tuple-element.152) | copy-start | bytes 3145732
  707.0 9.1 copy-start.15
  707.0 9.1 copy-start.58
  707.0 9.2 copy-start.59
  709.2 7.0 copy-start.14
  709.2 7.0 copy-start.16
  710.5 7.0 copy-start.37
  717.5 5.9 copy-start.40
  726.8 62.3 %copy-start.35 = (bf16[4,128,4,128]{3,2,1,0:T(4,128)(2,1)S(1)}, bf16[4,128,4,128]{3,2,1,0:T(4,128)(2,1)}, u32[]{:S(2)}) copy-start(bf16[4,128,4,128]{3,2,1,0:T(4,128)(2,1)} %copy-done.34) | copy-start | bytes 1572868
  785.6 46.0 %all-to-all-start.13 = ((bf16[4,64,1536]{2,1,0:T(8,128)(2,1)}), bf16[4,64,1536]{2,1,0:T(8,128)(2,1)S(1)}, u32[]{:S(2)}, u32[]{:S(2)}) async-start(bf16[4,64,1536]{2,1,0:T(8,128)(2,1)} %bitcast.259), calls=%async_computation.13 | async-start | bytes 1572864 | tf_op jit(solution)/shard_map/all_to_all | solution.py:37
  789.1 34.6 %copy-start.38 = (bf16[64,8,4,128]{3,1,2,0:T(8,128)(2,1)S(1)}, bf16[64,8,4,128]{3,1,2,0:T(8,128)(2,1)}, u32[]{:S(2)}) copy-start(bf16[64,8,4,128]{3,1,2,0:T(8,128)(2,1)} %copy-done.37) | copy-start | bytes 1572868
  832.5 29.8 %all-to-all-start.11 = ((bf16[4,128,2048]{2,1,0:T(8,128)(2,1)}), bf16[4,128,2048]{2,1,0:T(8,128)(2,1)}, u32[]{:S(2)}, u32[]{:S(2)}) async-start(bf16[4,128,2048]{2,1,0:T(8,128)(2,1)} %bitcast.262), calls=%async_computation.11 | async-start | bytes 4194304 | tf_op jit(solution)/shard_map/all_to_all | solution.py:37
  836.9 30.8 %copy-start.45 = (f32[32,4]{1,0:T(8,128)S(1)}, f32[32,4]{1,0:T(8,128)}, u32[]{:S(2)}) copy-start(f32[32,4]{1,0:T(8,128)} %copy-done.44) | copy-start | bytes 1540
  837.0 30.8 %copy-start.54 = (f32[2048]{0:T(1024)S(1)}, f32[2048]{0:T(1024)}, u32[]{:S(2)}) copy-start(f32[2048]{0:T(1024)} %param.21) | copy-start | bytes 24580
  837.0 49.5 %copy-start.10 = (f32[128,2048]{1,0:T(8,128)S(1)}, f32[128,2048]{1,0:T(8,128)}, u32[]{:S(2)}) copy-start(f32[128,2048]{1,0:T(8,128)} %copy-done.8) | copy-start | bytes 3145732
  837.0 49.5 %copy-start.69 = (f32[128]{0:T(128)S(1)}, f32[128]{0:T(128)}, u32[]{:S(2)}) copy-start(f32[128]{0:T(128)} %copy-done.68) | copy-start | bytes 1540
  870.5 12.7 %all-to-all-start.14 = ((f32[32,1,128]{2,1,0:T(1,128)}), f32[32,1,128]{2,1,0:T(1,128)S(1)}, u32[]{:S(2)}, u32[]{:S(2)}) async-start(f32[32,1,128]{2,1,0:T(1,128)} %bitcast.63), calls=%async_computation.14 | async-start | bytes 32768 | tf_op jit(solution)/shard_map/all_to_all | solution.py:37
  883.9 9.6 %all-to-all-start.15 = ((f32[32,1,128]{2,1,0:T(1,128)}), f32[32,1,128]{2,1,0:T(1,128)S(1)}, u32[]{:S(2)}, u32[]{:S(2)}) async-start(f32[32,1,128]{2,1,0:T(1,128)} %broadcast_in_dim.38), calls=%async_computation.15 | async-start | bytes 32768 | tf_op jit(solution)/shard_map/all_to_all | solution.py:37
  893.6 19.7 %all-to-all-start.12 = ((bf16[32,4,2048]{2,1,0:T(4,128)(2,1)}), bf16[32,4,2048]{2,1,0:T(4,128)(2,1)S(1)}, u32[]{:S(2)}, u32[]{:S(2)}) async-start(bf16[32,4,2048]{2,1,0:T(4,128)(2,1)} %reshape.382), calls=%async_computation.12 | async-start | bytes 1048576 | tf_op jit(solution)/shard_map/all_to_all | solution.py:37
  (32 other events, 78.2 us)
Sparse Core Ops, SparseCore 0:
  12.4 122.8 all-gather.7
  137.1 113.2 all-gather.9
  252.2 87.4 all-gather.5
  484.4 83.5 reduce-scatter.3
  570.9 109.7 reduce-scatter.5
  683.6 87.5 reduce-scatter.7

commit v3 on v2

--- a/solution.py
+++ b/solution.py
@@ -447,6 +447,8 @@
     grad_result = (2.0 * (rows * devices) / valid_total) * keep * error_rows
 
     grad_rows = gather_rows(grad_result.astype(bf16), 4)
+    output_rows, grad_rows = lax.optimization_barrier((result.astype(bf16), grad_rows))
+    back_output = swap(output_rows.reshape(devices, stripe, width), BOTH)
     grad_feed = 0.0
     gate_grads, grad_gus = [], []
     grad_inner_raw = dotf(grad_rows, down, ((1,), (1,)))
@@ -489,10 +491,9 @@
     grad_ffn_gain = jnp.sum(grad_feed * ffn_normed, axis=0)
     grad_resid = grad_result + norm_back(grad_feed * ffn_gain, ffn_normed, ffn_scale)
 
-    early = sum_small((part_square, grad_ffn_gain, grad_router), devices)
     grad_attn = spread(grad_resid.astype(bf16), "dp", dps)
     grad_attn = grad_attn.reshape(group, width)
-    grad_out_w = dotf(mixed_low, grad_attn, ((0,), (0,)))
+    grad_out_w = dotf(mixed_low, grad_attn, ((0,), (0,))).astype(bf16)
     grad_mixed = dotf(grad_attn, out_weight, ((1,), (1,)))
     grad_mixed = grad_mixed.reshape(dps, rows, heads, HD).astype(bf16)
     grad_probs = jnp.einsum("bthd,bshd->bhts", grad_mixed, values_low, preferred_element_type=f32)
@@ -526,13 +527,21 @@
     grad_attn_gain = jnp.sum(grad_normed * attn_normed, axis=0)
     grad_tokens = grad_resid + norm_back(grad_normed * attn_gain, attn_normed, attn_scale)
 
-    grad_qkv_w = grad_qkv_w.reshape(dps, owners, piece, 3 * part).transpose(1, 0, 2, 3)
-    grad_qkv_w = reduce_rows(grad_qkv_w.reshape(-1, 3 * part), 6).astype(bf16)
-    grad_qkv_w = swap(grad_qkv_w.reshape(dps, piece, 3 * part), "dp")
+    grad_qkv_w = grad_qkv_w.reshape(dps, owners, piece, 3, part).transpose(1, 3, 2, 0, 4)
+    attn_grads = jnp.concatenate(
+        [
+            grad_qkv_w.reshape(owners, 3 * piece, width),
+            grad_out_w.reshape(owners, piece, width),
+        ],
+        axis=1,
+    )
+    attn_grads = reduce_rows(attn_grads.reshape(-1, width), 6)
+    out_out = attn_grads[3 * piece :]
+    grad_qkv_w = attn_grads[: 3 * piece].astype(bf16).reshape(3 * piece, dps, part)
+    grad_qkv_w = swap(grad_qkv_w.transpose(1, 0, 2), "dp")
     qkv_out = jnp.concatenate(
-        [grad_qkv_w[d, :, g * part : (g + 1) * part] for g in range(3) for d in range(dps)], axis=1
+        [grad_qkv_w[d, g * piece : (g + 1) * piece] for g in range(3) for d in range(dps)], axis=1
     ).astype(f32)
-    out_out = reduce_rows(grad_out_w.astype(bf16), 7)
     down_out = lax.psum_scatter(
         grad_down_w.reshape(local, hidden, width), "dp", scatter_dimension=1, tiled=True
     )
@@ -543,13 +552,15 @@
             lax.psum_scatter(grad_gate_up_w[e], "dp", scatter_dimension=0, tiled=True)
         )
     gate_up_out = jnp.stack([w.astype(f32) for w in gate_up_out])
-    late = sum_small((grad_query_gain, grad_key_gain, grad_attn_gain), devices)
-    mean_loss = early[0] / (valid_total * width)
+    sums = sum_small(
+        (part_square, grad_query_gain, grad_key_gain, grad_attn_gain, grad_ffn_gain, grad_router),
+        devices,
+    )
+    mean_loss = sums[0] / (valid_total * width)
 
     inverse_deal = (
         jnp.zeros((devices,), jnp.int32).at[deal].set(jnp.arange(devices, dtype=jnp.int32))
     )
-    back_output = swap(result.astype(bf16).reshape(devices, stripe, width), BOTH)
     back_grad = swap(grad_tokens.astype(bf16).reshape(devices, stripe, width), BOTH)
     output = back_output[inverse_deal].reshape(rows, width)
     given_grad = back_grad[inverse_deal].reshape(rows, width).astype(f32)
@@ -559,11 +570,11 @@
         given_grad,
         qkv_out,
         out_out,
-        late[0],
-        late[1],
-        late[2],
-        early[1],
-        early[2],
+        sums[1],
+        sums[2],
+        sums[3],
+        sums[4],
+        sums[5],
         gate_up_out,
         down_out,
     )

time: 943 us -> 955 us (1.013)
  local copies, waits for them, and re-layouts: 118 us -> 152 us
  blocking collectives: 32.5 us -> 0 us
  Pallas kernels: 321 us -> 306 us
  waiting for transfers between devices: 140 us -> 150 us
    all_to_all x2 -> x0, blocking collectives: 32.5 us -> none  [swap(): return lax.all_to_all(pieces, axes, split_axis=0, concat_axis=0, tiled=True)]
    reshape x2 -> x4, local copies, waits for them, and re-layouts: 4.63 us -> 33.1 us  [the longest x1 18.8 us: on_device(): grad_qkv_w.reshape(dps, owners, piece, 3, part).transpose(1, 3, 2, 0, 4)]
    pallas_call x4 -> x3, Pallas kernels: 168 us -> 153 us  [reduce_rows(): pl.pallas_call(functools.partial(reduce_kernel, count), out_shape=jax.Sha...]
    transpose x0 -> x1, local copies, waits for them, and re-layouts: none -> 13.5 us  [on_device(): grad_qkv_w.reshape(dps, owners, piece, 3, part).transpose(1, 3, 2, 0, 4)]
    all_to_all x14, waiting for transfers between devices: 138 us -> 149 us  [swap(): return lax.all_to_all(pieces, axes, split_axis=0, concat_axis=0, tiled=True)]
    unnamed x171 -> x168, local copies, waits for them, and re-layouts: 35.3 us -> 27.6 us
  transfers between devices with their start and end apart: 20 -> 20, of which waited for: 10 -> 10; matrix products, arithmetic and copies ran while one was open for 31% -> 35% of each run, Pallas kernels for 25% -> 23%
where the time goes in v3:
time: 955 us; the launch traced here: 946 us
  Pallas kernels  306 us (32%)
  matrix products  175 us (18%)
  local copies, waits for them, and re-layouts  152 us (16%)
  waiting for transfers between devices  150 us (16%)
  other arithmetic  83 us (9%)
  starting transfers between devices  61.4 us (6%)
  between operations  18.3 us (2%)
    dot_general x16, matrix products, dotf(): lax.dot_general(left, right, (dims, ((), ())), preferred_element_type=jnp...  157 us
    pallas_call x3, Pallas kernels, reduce_rows(): pl.pallas_call(functools.partial(reduce_kernel, count), out_shape=jax.Sha...  153 us
    pallas_call x3, Pallas kernels, gather_rows(): pl.pallas_call(functools.partial(gather_kernel, count), out_shape=jax.Sha...  153 us
    all_to_all x14, waiting for transfers between devices, swap(): return lax.all_to_all(pieces, axes, split_axis=0, concat_axis=0, tiled=True)  149 us
    all_to_all x14, starting transfers between devices, swap(): return lax.all_to_all(pieces, axes, split_axis=0, concat_axis=0, tiled=True)  61.2 us
    unnamed x168, local copies, waits for them, and re-layouts  27.6 us
  transfers between devices with their start and end apart: 20, of which 10 were waited for; matrix products, arithmetic and copies ran while one was open for 35% of the time, Pallas kernels for 23%

profile of v3, /device:TPU:0, one launch (start us, length us, event | category | flops | bytes accessed | tf_op | source)
XLA Modules:
  0.0 946.2 jit_solution(5225085352219350701)
XLA Ops:
  7.2 4.9 fusion.83
  15.2 7.3 all-to-all-start
  24.3 14.6 %all-to-all-done = bf16[32,4,2048]{2,1,0:T(4,128)(2,1)S(1)} async-done(((bf16[32,4,2048]{2,1,0:T(4,128)(2,1)}), bf16[32,4,2048]{2,1,0:T(4,128)(2,1)S(1)}, u32[]{:S(2)}, u32[]{:S(2)}) %all-to-all-start) | async-done | bytes 524320 | tf_op jit(solution)/shard_map/all_to_all | solution.py:37
  39.7 3.3 all-to-all-start.3
  44.4 7.2 all-to-all-done.3
  51.5 4.2 all-to-all-start.2
  58.7 13.9 %all-to-all-done.2 = bf16[4,64,1536]{2,1,0:T(8,128)(2,1)} async-done(((bf16[4,64,1536]{2,1,0:T(8,128)(2,1)}), bf16[4,64,1536]{2,1,0:T(8,128)(2,1)}, u32[]{:S(2)}, u32[]{:S(2)}) %all-to-all-start.2) | async-done | bytes 786464 | tf_op jit(solution)/shard_map/all_to_all | solution.py:37
  75.3 4.4 all-to-all-start.1
  87.4 61.2 %shard_map.238 = bf16[8,256,1536]{2,1,0:T(8,128)(2,1)} custom-call(bf16[256,1536]{1,0:T(8,128)(2,1)} %bitcast.5.block), custom_call_target="tpu_custom_call" | custom-call | bytes 94371840 | tf_op jit(solution)/shard_map/pallas_call | solution.py:135
  148.6 6.1 copy.199
  154.7 3.6 all-to-all-start.5
  158.3 6.2 fusion.89
  184.1 3.2 fusion.87
  187.4 3.4 fusion.23
  194.7 4.5 all-to-all-start.4
  204.9 42.9 %all-to-all-done.4 = bf16[4,128,2048]{2,1,0:T(8,128)(2,1)} async-done(((bf16[4,128,2048]{2,1,0:T(8,128)(2,1)}), bf16[4,128,2048]{2,1,0:T(8,128)(2,1)}, u32[]{:S(2)}, u32[]{:S(2)}) %all-to-all-start.4) | async-done | bytes 2097184 | tf_op jit(solution)/shard_map/all_to_all | solution.py:37
  247.8 3.0 convert_reduce_fusion.1
  257.8 44.9 %shard_map.239 = bf16[8,128,2048]{2,1,0:T(8,128)(2,1)} custom-call(bf16[128,2048]{1,0:T(8,128)(2,1)} %get-tuple-element.106.block), custom_call_target="tpu_custom_call" | custom-call | bytes 62914560 | tf_op jit(solution)/shard_map/pallas_call | solution.py:135
  302.8 3.4 fusion.88
  306.9 12.5 %fusion.7 = f32[1024,2048]{1,0:T(8,128)S(1)} fusion(bf16[1024,2048]{1,0:T(8,128)(2,1)} %bitcast.237, bf16[1,2048,2048]{2,1,0:T(8,128)(2,1)} %all-gather.8.cloned.1.call-done), kind=kOutput, calls=%fused_computation.13 | convolution fusion | flops 8589934592 | bytes 20971520 | tf_op jit(solution)/shard_map/dot_general | solution.py:33
  319.4 3.4 copy-done.1
  325.4 12.5 %fusion.3 = f32[1024,2048]{1,0:T(8,128)S(1)} fusion(bf16[1024,2048]{1,0:T(8,128)(2,1)} %bitcast.238, bf16[1,2048,2048]{2,1,0:T(8,128)(2,1)} %all-gather.10.cloned.1.call-done), kind=kOutput, calls=%fused_computation.9 | convolution fusion | flops 8589934592 | bytes 20971520 | tf_op jit(solution)/shard_map/dot_general | solution.py:33
  337.9 3.2 copy-done.2
  343.6 14.4 %convolution_convert_fusion.4 = bf16[1024,2048]{1,0:T(8,128)(2,1)} fusion(bf16[2048,2048]{1,0:T(8,128)(2,1)} %bitcast.284, bf16[1024,1024]{1,0:T(8,128)(2,1)} %multiply_convert_fusion.4, bf16[1024,1024]{1,0:T(8,128)(2,1)} %multiply_convert_fusion.5), kind=kOutput, calls=%fused_computation.42 | convolution fusion | flops 8600420352 | bytes 16777216 | tf_op jit(solution)/shard_map/dot_general | solution.py:33
  358.0 40.2 %shard_map.240 = f32[128,2048]{1,0:T(8,128)} custom-call(bf16[8,128,2048]{2,1,0:T(8,128)(2,1)} %bitcast.245), custom_call_target="tpu_custom_call" | custom-call | bytes 62914560 | tf_op jit(solution)/shard_map/pallas_call | solution.py:270
  398.2 3.3 fusion.25
  403.4 46.6 %shard_map.241 = bf16[8,128,2048]{2,1,0:T(8,128)(2,1)} custom-call(bf16[128,2048]{1,0:T(8,128)(2,1)} %multiply_convert_fusion.9.block), custom_call_target="tpu_custom_call" | custom-call | bytes 62914560 | tf_op jit(solution)/shard_map/pallas_call | solution.py:135
  450.0 12.6 %fusion.90 = f32[1024,2048]{1,0:T(8,128)S(1)} fusion(bf16[1024,2048]{1,0:T(8,128)(2,1)} %bitcast.246, bf16[2048,2048]{1,0:T(8,128)(2,1)} %bitcast.285), kind=kOutput, calls=%fused_computation.231 | convolution fusion | flops 8589934592 | bytes 20971520 | tf_op jit(solution)/shard_map/dot_general | solution.py:33
  462.6 10.5 %multiply_reduce_fusion.1 = (f32[1024]{0:T(1024)S(1)}, f32[1024]{0:T(1024)S(1)}, bf16[1024,1024]{1,0:T(8,128)(2,1)}, bf16[1024,1024]{1,0:T(8,128)(2,1)}, bf16[10...) fusion(f32[1024,2048]{1,0:T(8,128)S(1)} %fusion.90, f32[1024,2048]{1,0:T(8,128)} %copy-done.1, ...), kind=kLoop, calls=%fused_computation.26 | loop fusion | flops 35649536 | bytes 33570816 | tf_op jit(solution)/shard_map/reduce_sum | solution.py:460
  475.1 11.6 %convolution_convert_fusion.2 = bf16[2048,2048]{1,0:T(8,128)(2,1)} fusion(bf16[1024,2048]{1,0:T(8,128)(2,1)S(1)} %bitcast.240, bf16[1024,1024]{1,0:T(8,128)(2,1)S(1)} %get-tuple-element.114, bf16[1024,1024]{1,0:T(8,128)(2,1)S(1)} %get-tuple-element.115), kind=kOutput, calls=%fused_computation.18 | convolution fusion | flops 8602517504 | bytes 16777216 | tf_op jit(solution)/shard_map/dot_general | solution.py:33
  486.8 14.4 %convolution_convert_fusion.1 = bf16[2048,2048]{1,0:T(8,128)(2,1)} fusion(bf16[1024,2048]{1,0:T(8,128)(2,1)} %bitcast.239, bf16[1024,1024]{1,0:T(8,128)(2,1)} %get-tuple-element.112, bf16[1024,1024]{1,0:T(8,128)(2,1)} %get-tuple-element.113), kind=kOutput, calls=%fused_computation.17 | convolution fusion | flops 8602517504 | bytes 16777216 | tf_op jit(solution)/shard_map/dot_general | solution.py:33
  501.8 3.3 all-to-all-start.7
  505.2 14.3 %convolution_convert_fusion = bf16[2048,2048]{1,0:T(8,128)(2,1)} fusion(bf16[1024,2048]{1,0:T(8,128)(2,1)} %bitcast.247, bf16[1024,1024]{1,0:T(8,128)(2,1)} %multiply_convert_fusion.4, bf16[1024,1024]{1,0:T(8,128)(2,1)} %multiply_convert_fusion.5), kind=kOutput, calls=%fused_computation.16 | convolution fusion | flops 8602517504 | bytes 16777216 | tf_op jit(solution)/shard_map/dot_general | solution.py:33
  519.5 15.0 %fusion.1 = f32[1024,2048]{1,0:T(8,128)} fusion(bf16[1,2048,2048]{2,1,0:T(8,128)(2,1)} %all-gather.10.cloned.1.call-done, bf16[1024,1024]{1,0:T(8,128)(2,1)} %get-tuple-element.112, bf16[1024,1024]{1,0:T(8,128)(2,1)} %get-tuple-element.113), kind=kOutput, calls=%fused_computation.7 | convolution fusion | flops 8598323200 | bytes 20971520 | tf_op jit(solution)/shard_map/dot_general | solution.py:33
  534.5 14.6 %add_convert_fusion = bf16[1024,2048]{1,0:T(8,128)(2,1)} fusion(f32[1024,2048]{1,0:T(8,128)} %fusion.1, bf16[1,2048,2048]{2,1,0:T(8,128)(2,1)} %all-gather.8.cloned.1.call-done, bf16[1024,1024]{1,0:T(8,128)(2,1)S(1)} %copy-done.27, bf16[1024,1024]{1,0:T(8,128)(2,1)} %copy-done.28), kind=kOutput, calls=%fused_computation.15 | convolution fusion | flops 8602517504 | bytes 25165824 | tf_op jit(solution)/shard_map/dot_general | solution.py:33
  549.1 41.1 %shard_map.242 = f32[128,2048]{1,0:T(8,128)} custom-call(bf16[8,128,2048]{2,1,0:T(8,128)(2,1)} %bitcast.244), custom_call_target="tpu_custom_call" | custom-call | bytes 62914560 | tf_op jit(solution)/shard_map/pallas_call | solution.py:270
  592.2 5.7 all-to-all-start.6
  598.6 2.8 multiply_reduce_fusion.3
  604.1 10.0 %all-to-all-done.6 = bf16[32,4,2048]{2,1,0:T(4,128)(2,1)} async-done(((bf16[32,4,2048]{2,1,0:T(4,128)(2,1)}), bf16[32,4,2048]{2,1,0:T(4,128)(2,1)}, u32[]{:S(2)}, u32[]{:S(2)}) %all-to-all-start.6) | async-done | bytes 524320 | tf_op jit(solution)/shard_map/all_to_all | solution.py:37
  616.8 4.5 all-to-all-start.8
  630.7 24.4 %all-to-all-done.8 = bf16[4,128,2048]{2,1,0:T(8,128)(2,1)} async-done(((bf16[4,128,2048]{2,1,0:T(8,128)(2,1)}), bf16[4,128,2048]{2,1,0:T(8,128)(2,1)}, u32[]{:S(2)}, u32[]{:S(2)}) %all-to-all-start.8) | async-done | bytes 2097184 | tf_op jit(solution)/shard_map/all_to_all | solution.py:37
  655.1 3.7 fusion.20
  658.8 3.3 fusion.24
  672.3 2.9 copy.213
  675.2 3.1 multiply_reduce_fusion.5
  688.1 7.3 convolution_convert_fusion.3
  695.3 18.8 %reshape.366 = bf16[4,8,64,3,512]{4,3,2,1,0:T(4,128)(2,1)} reshape(bf16[2048,1536]{1,0:T(8,128)(2,1)} %convolution_convert_fusion.3) | data formatting | bytes 12582912 | tf_op jit(solution)/shard_map/reshape | solution.py:530
  714.1 13.5 %copy.227 = bf16[8,3,64,4,512]{4,3,2,1,0:T(4,128)(2,1)} copy(bf16[8,3,64,4,512]{4,1,2,0,3:T(4,128)(2,1)} %bitcast.234) | data formatting | bytes 12582912 | tf_op jit(solution)/shard_map/transpose | solution.py:530
  727.6 11.3 %reshape.367 = bf16[8,192,2048]{2,1,0:T(8,128)(2,1)} reshape(bf16[8,3,64,4,512]{4,3,2,1,0:T(4,128)(2,1)} %copy.227) | data formatting | bytes 12582912 | tf_op jit(solution)/shard_map/reshape | solution.py:533
  738.9 4.2 convolution_convert_fusion.5
  743.1 8.7 pad_maximum_fusion.parts
  751.8 72.2 %shard_map.243 = f32[256,2048]{1,0:T(8,128)} custom-call(bf16[8,256,2048]{2,1,0:T(8,128)(2,1)} %pad_maximum_fusion.parts), custom_call_target="tpu_custom_call" | custom-call | bytes 125829120 | tf_op jit(solution)/shard_map/pallas_call | solution.py:270
  828.4 3.7 all-to-all-start.13
  832.2 7.9 convolution_convert_fusion.6
  840.1 4.5 all-to-all-start.9
  849.7 19.1 %all-to-all-done.9 = bf16[4,128,2048]{2,1,0:T(8,128)(2,1)} async-done(((bf16[4,128,2048]{2,1,0:T(8,128)(2,1)}), bf16[4,128,2048]{2,1,0:T(8,128)(2,1)}, u32[]{:S(2)}, u32[]{:S(2)}) %all-to-all-start.9) | async-done | bytes 2097184 | tf_op jit(solution)/shard_map/all_to_all | solution.py:37
  868.8 3.0 convert_reduce_fusion
  877.9 6.4 all-to-all-start.10
  885.9 6.9 all-to-all-done.10
  900.9 3.9 all-to-all-done.11
  904.8 3.3 all-to-all-start.12
  918.7 5.6 all-to-all-done.12
  927.5 6.2 maximum_convert_fusion
  933.7 4.1 convert_element_type.204
  (308 shorter events, 141.5 us)
Async XLA Ops:
  7.2 184.9 %copy-start = (bf16[512,2048]{1,0:T(8,128)(2,1)S(1)}, bf16[512,2048]{1,0:T(8,128)(2,1)}, u32[]{:S(2)}) copy-start(bf16[512,2048]{1,0:T(8,128)(2,1)} %param.18) | copy-start | bytes 6291460
  7.2 299.7 %all-gather.8.cloned.1.call-start = ((), (), s32[]{:S(2)}) async-start(), calls=%async_computation.21 | async-start | bytes 10485760 | tf_op jit(solution)/shard_map/all_gather | solution.py:359
  12.2 10.4 %copy-start.70 = (s32[128,8]{0,1:T(8,128)S(1)}, s32[128,8]{0,1:T(8,128)}, u32[]{:S(2)}) copy-start(s32[128,8]{0,1:T(8,128)} %param.27) | copy-start | bytes 12292
  12.2 10.6 %copy-start.72 = (s32[1,4]{1,0:T(1,128)S(1)}, s32[1,4]{1,0:T(1,128)}, u32[]{:S(2)}) copy-start(s32[1,4]{1,0:T(1,128)} %param.29) | copy-start | bytes 52
  12.2 10.6 %copy-start.73 = (s32[128]{0:T(128)S(1)}, s32[128]{0:T(128)}, u32[]{:S(2)}) copy-start(s32[128]{0:T(128)} %param.28) | copy-start | bytes 1540
  12.2 313.2 %all-gather.10.cloned.1.call-start = ((), (), s32[]{:S(2)}) async-start(), calls=%async_computation.22 | async-start | bytes 10485760 | tf_op jit(solution)/shard_map/all_gather | solution.py:359
  13.4 10.9 %copy-start.71 = (s32[32]{0:T(128)}, s32[32]{0:T(128)S(1)}, u32[]{:S(2)}) copy-start(s32[32]{0:T(128)S(1)} %compare_select_fusion.1) | copy-start | bytes 388
  15.2 23.7 %all-to-all-start = ((bf16[32,4,2048]{2,1,0:T(4,128)(2,1)}), bf16[32,4,2048]{2,1,0:T(4,128)(2,1)S(1)}, u32[]{:S(2)}, u32[]{:S(2)}) async-start(bf16[32,4,2048]{2,1,0:T(4,128)(2,1)} %gather_fusion), calls=%async_computation | async-start | bytes 1048576 | tf_op jit(solution)/shard_map/all_to_all | solution.py:37
  22.8 34.8 %copy-start.52 = (f32[2048]{0:T(1024)S(1)}, f32[2048]{0:T(1024)}, u32[]{:S(2)}) copy-start(f32[2048]{0:T(1024)} %param.21) | copy-start | bytes 24580
  38.9 16.9 %copy-start.11 = (bf16[32,4,2048]{2,1,0:T(4,128)(2,1)}, bf16[32,4,2048]{2,1,0:T(4,128)(2,1)S(1)}, u32[]{:S(2)}) copy-start(bf16[32,4,2048]{2,1,0:T(4,128)(2,1)S(1)} %all-to-all-done) | copy-start | bytes 1572868
  39.7 11.8 %all-to-all-start.3 = ((s32[32,1,1280]{2,1,0:T(1,128)}), s32[32,1,1280]{2,1,0:T(1,128)}, u32[]{:S(2)}, u32[]{:S(2)}) async-start(s32[32,1,1280]{2,1,0:T(1,128)} %broadcast_in_dim.25), calls=%async_computation.3 | async-start | bytes 327680 | tf_op jit(solution)/shard_map/all_to_all | solution.py:37
  51.5 21.1 %all-to-all-start.2 = ((bf16[4,64,1536]{2,1,0:T(8,128)(2,1)}), bf16[4,64,1536]{2,1,0:T(8,128)(2,1)}, u32[]{:S(2)}, u32[]{:S(2)}) async-start(bf16[4,64,1536]{2,1,0:T(8,128)(2,1)} %pad_maximum_fusion.13), calls=%async_computation.2 | async-start | bytes 1572864 | tf_op jit(solution)/shard_map/all_to_all | solution.py:37
  56.5 18.8 %copy-start.68 = (f32[128]{0:T(128)}, f32[128]{0:T(128)S(1)}, u32[]{:S(2)}) copy-start(f32[128]{0:T(128)S(1)} %rsqrt.40) | copy-start | bytes 1540
  57.6 17.7 %copy-start.7 = (f32[128,2048]{1,0:T(8,128)}, f32[128,2048]{1,0:T(8,128)S(1)}, u32[]{:S(2)}) copy-start(f32[128,2048]{1,0:T(8,128)S(1)} %reshape.373) | copy-start | bytes 3145732
  75.3 79.4 %all-to-all-start.1 = ((bf16[4,128,2048]{2,1,0:T(8,128)(2,1)}), bf16[4,128,2048]{2,1,0:T(8,128)(2,1)}, u32[]{:S(2)}, u32[]{:S(2)}) async-start(bf16[4,128,2048]{2,1,0:T(8,128)(2,1)} %broadcast_in_dim.24), calls=%async_computation.1 | async-start | bytes 4194304 | tf_op jit(solution)/shard_map/all_to_all | solution.py:37
  79.7 263.9 %all-gather.6.cloned.1.call-start = ((), (), s32[]{:S(2)}) async-start(), calls=%async_computation.17 | async-start | bytes 10485760 | tf_op jit(solution)/shard_map/all_gather | solution.py:360
  85.5 101.8 %copy-start.54 = (pred[4,128,128]{1,2,0:T(8,128)(4,1)}, pred[4,128,128]{1,2,0:T(8,128)(4,1)S(1)}, u32[]{:S(2)}) copy-start(pred[4,128,128]{1,2,0:T(8,128)(4,1)S(1)} %broadcast_compare_fusion) | copy-start | bytes 196612
  87.4 92.1 %copy-start.18 = (f32[4,128,64]{2,1,0:T(8,128)}, f32[4,128,64]{2,1,0:T(8,128)S(1)}, u32[]{:S(2)}) copy-start(f32[4,128,64]{2,1,0:T(8,128)S(1)} %get-tuple-element.155) | copy-start | bytes 393220
  154.7 40.0 %all-to-all-start.5 = ((bf16[32,4,2048]{2,1,0:T(4,128)(2,1)}), bf16[32,4,2048]{2,1,0:T(4,128)(2,1)}, u32[]{:S(2)}, u32[]{:S(2)}) async-start(bf16[32,4,2048]{2,1,0:T(4,128)(2,1)} %gather_fusion.1), calls=%async_computation.5 | async-start | bytes 1048576 | tf_op jit(solution)/shard_map/all_to_all | solution.py:37
  166.8 10.8 %copy-start.66 = (f32[128]{0:T(128)S(1)}, f32[128]{0:T(128)}, u32[]{:S(2)}) copy-start(f32[128]{0:T(128)} %param.20) | copy-start | bytes 1540
  168.4 11.1 %copy-start.4 = (f32[4,128,4,128]{3,2,1,0:T(4,128)}, f32[4,128,4,128]{3,2,1,0:T(4,128)S(1)}, u32[]{:S(2)}) copy-start(f32[4,128,4,128]{3,2,1,0:T(4,128)S(1)} %reshape.349) | copy-start | bytes 3145732
  168.4 9.5 %copy-start.63 = (f32[128]{0:T(128)S(1)}, f32[128]{0:T(128)}, u32[]{:S(2)}) copy-start(f32[128]{0:T(128)} %param.19) | copy-start | bytes 1540
  181.5 9.3 copy-start.20
  187.4 7.3 copy-start.56
  194.7 53.1 %all-to-all-start.4 = ((bf16[4,128,2048]{2,1,0:T(8,128)(2,1)}), bf16[4,128,2048]{2,1,0:T(8,128)(2,1)}, u32[]{:S(2)}, u32[]{:S(2)}) async-start(bf16[4,128,2048]{2,1,0:T(8,128)(2,1)} %bitcast.256), calls=%async_computation.4 | async-start | bytes 4194304 | tf_op jit(solution)/shard_map/all_to_all | solution.py:37
  199.2 728.3 %reduce-scatter.4.cloned.1.call-start = ((), (), s32[]{:S(2)}) async-start(), calls=%async_computation.18 | async-start | bytes 10485760 | tf_op jit(solution)/shard_map/reduce_scatter | solution.py:552
  202.7 52.5 %copy-start.8 = (f32[128,2048]{1,0:T(8,128)S(1)}, f32[128,2048]{1,0:T(8,128)}, u32[]{:S(2)}) copy-start(f32[128,2048]{1,0:T(8,128)} %copy-done.7) | copy-start | bytes 3145732
  202.7 52.5 %copy-start.50 = (f32[2048]{0:T(1024)S(1)}, f32[2048]{0:T(1024)}, u32[]{:S(2)}) copy-start(f32[2048]{0:T(1024)} %param.22) | copy-start | bytes 24580
  255.2 47.5 %copy-start.60 = (f32[128]{0:T(128)}, f32[128]{0:T(128)S(1)}, u32[]{:S(2)}) copy-start(f32[128]{0:T(128)S(1)} %rsqrt.44) | copy-start | bytes 1540
  255.2 47.5 %copy-start.41 = (bf16[2048,16]{0,1:T(8,128)(2,1)S(1)}, bf16[2048,16]{0,1:T(8,128)(2,1)}, u32[]{:S(2)}) copy-start(bf16[2048,16]{0,1:T(8,128)(2,1)} %param.23) | copy-start | bytes 196612
  358.0 40.2 %copy-start.10 = (f32[128,2048]{1,0:T(8,128)S(1)}, f32[128,2048]{1,0:T(8,128)}, u32[]{:S(2)}) copy-start(f32[128,2048]{1,0:T(8,128)} %get-tuple-element.107) | copy-start | bytes 3145732
  462.6 12.5 %copy-start.3 = (bf16[8,128,2048]{2,1,0:T(8,128)(2,1)S(1)}, bf16[8,128,2048]{2,1,0:T(8,128)(2,1)}, u32[]{:S(2)}) copy-start(bf16[8,128,2048]{2,1,0:T(8,128)(2,1)} %shard_map.239) | copy-start | bytes 12582916
  486.8 440.8 %reduce-scatter.6.cloned.1.call-start = ((), (), s32[]{:S(2)}) async-start(), calls=%async_computation.19 | async-start | bytes 10485760 | tf_op jit(solution)/shard_map/reduce_scatter | solution.py:552
  501.8 90.3 %all-to-all-start.7 = ((f32[8,2,128]{2,1,0:T(2,128)}), f32[8,2,128]{2,1,0:T(2,128)S(1)}, u32[]{:S(2)}, u32[]{:S(2)}) async-start(f32[8,2,128]{2,1,0:T(2,128)} %maximum_bitcast_fusion.4), calls=%async_computation.7 | async-start | bytes 16384 | tf_op jit(solution)/shard_map/all_to_all | solution.py:37
  505.1 428.6 %reduce-scatter.8.cloned.1.call-start = ((), (), s32[]{:S(2)}) async-start(), calls=%async_computation.20 | async-start | bytes 10485760 | tf_op jit(solution)/shard_map/reduce_scatter | solution.py:545
  519.5 15.0 %copy-start.27 = (bf16[1024,1024]{1,0:T(8,128)(2,1)S(1)}, bf16[1024,1024]{1,0:T(8,128)(2,1)}, u32[]{:S(2)}) copy-start(bf16[1024,1024]{1,0:T(8,128)(2,1)} %copy-done.26) | copy-start | bytes 6291460
  549.1 49.5 %copy-start.42 = (bf16[2048,16]{0,1:T(8,128)(2,1)S(1)}, bf16[2048,16]{0,1:T(8,128)(2,1)}, u32[]{:S(2)}) copy-start(bf16[2048,16]{0,1:T(8,128)(2,1)} %param.23) | copy-start | bytes 196612
  549.1 49.5 %copy-start.51 = (f32[2048]{0:T(1024)S(1)}, f32[2048]{0:T(1024)}, u32[]{:S(2)}) copy-start(f32[2048]{0:T(1024)} %param.22) | copy-start | bytes 24580
  549.1 49.5 %copy-start.61 = (f32[128]{0:T(128)S(1)}, f32[128]{0:T(128)}, u32[]{:S(2)}) copy-start(f32[128]{0:T(128)} %copy-done.60) | copy-start | bytes 1540
  592.2 22.0 %all-to-all-start.6 = ((bf16[32,4,2048]{2,1,0:T(4,128)(2,1)}), bf16[32,4,2048]{2,1,0:T(4,128)(2,1)}, u32[]{:S(2)}, u32[]{:S(2)}) async-start(bf16[32,4,2048]{2,1,0:T(4,128)(2,1)} %reshape.356), calls=%async_computation.6 | async-start | bytes 1048576 | tf_op jit(solution)/shard_map/all_to_all | solution.py:37
  604.1 18.2 %copy-start.64 = (f32[128]{0:T(128)S(1)}, f32[128]{0:T(128)}, u32[]{:S(2)}) copy-start(f32[128]{0:T(128)} %param.19) | copy-start | bytes 1540
  604.1 18.2 %copy-start.67 = (f32[128]{0:T(128)S(1)}, f32[128]{0:T(128)}, u32[]{:S(2)}) copy-start(f32[128]{0:T(128)} %param.20) | copy-start | bytes 1540
  604.1 18.7 %copy-start.49 = (f32[4,128,4]{1,2,0:T(4,128)S(1)}, f32[4,128,4]{1,2,0:T(4,128)}, u32[]{:S(2)}) copy-start(f32[4,128,4]{1,2,0:T(4,128)} %copy-done.48) | copy-start | bytes 24580
  604.1 19.6 %copy-start.47 = (f32[4,128,4]{1,2,0:T(4,128)S(1)}, f32[4,128,4]{1,2,0:T(4,128)}, u32[]{:S(2)}) copy-start(f32[4,128,4]{1,2,0:T(4,128)} %copy-done.46) | copy-start | bytes 24580
  604.1 19.8 %copy-start.15 = (bf16[128,2048]{1,0:T(8,128)(2,1)S(1)}, bf16[128,2048]{1,0:T(8,128)(2,1)}, u32[]{:S(2)}) copy-start(bf16[128,2048]{1,0:T(8,128)(2,1)} %get-tuple-element.106.block) | copy-start | bytes 1572868
  616.8 38.3 %all-to-all-start.8 = ((bf16[4,128,2048]{2,1,0:T(8,128)(2,1)}), bf16[4,128,2048]{2,1,0:T(8,128)(2,1)}, u32[]{:S(2)}, u32[]{:S(2)}) async-start(bf16[4,128,2048]{2,1,0:T(8,128)(2,1)} %broadcast_in_dim.30), calls=%async_computation.8 | async-start | bytes 4194304 | tf_op jit(solution)/shard_map/all_to_all | solution.py:37
  629.8 29.0 %copy-start.21 = (bf16[4,128,4,64]{3,1,2,0:T(8,128)(2,1)S(1)}, bf16[4,128,4,64]{3,1,2,0:T(8,128)(2,1)}, u32[]{:S(2)}) copy-start(bf16[4,128,4,64]{3,1,2,0:T(8,128)(2,1)} %copy-done.20) | copy-start | bytes 786436
  630.7 28.0 %copy-start.22 = (bf16[4,128,4,64]{3,1,2,0:T(8,128)(2,1)S(1)}, bf16[4,128,4,64]{3,1,2,0:T(8,128)(2,1)}, u32[]{:S(2)}) copy-start(bf16[4,128,4,64]{3,1,2,0:T(8,128)(2,1)} %get-tuple-element.146) | copy-start | bytes 786436
  678.4 7.3 copy-start.16
  678.4 7.3 copy-start.58
  678.4 7.3 copy-start.59
  727.6 11.3 %copy-start.35 = (bf16[4,128,4,128]{3,2,1,0:T(4,128)(2,1)S(1)}, bf16[4,128,4,128]{3,2,1,0:T(4,128)(2,1)}, u32[]{:S(2)}) copy-start(bf16[4,128,4,128]{3,2,1,0:T(4,128)(2,1)} %copy-done.34) | copy-start | bytes 1572868
  824.0 8.2 copy-start.37
  828.4 11.7 %all-to-all-start.13 = ((bf16[4,192,512]{2,1,0:T(8,128)(2,1)}), bf16[4,192,512]{2,1,0:T(8,128)(2,1)S(1)}, u32[]{:S(2)}, u32[]{:S(2)}) async-start(bf16[4,192,512]{2,1,0:T(8,128)(2,1)} %bitcast.254), calls=%async_computation.13 | async-start | bytes 1572864 | tf_op jit(solution)/shard_map/all_to_all | solution.py:37
  840.1 8.9 copy-start.17
  840.1 28.7 %all-to-all-start.9 = ((bf16[4,128,2048]{2,1,0:T(8,128)(2,1)}), bf16[4,128,2048]{2,1,0:T(8,128)(2,1)}, u32[]{:S(2)}, u32[]{:S(2)}) async-start(bf16[4,128,2048]{2,1,0:T(8,128)(2,1)} %bitcast.257), calls=%async_computation.9 | async-start | bytes 4194304 | tf_op jit(solution)/shard_map/all_to_all | solution.py:37
  844.6 29.7 %copy-start.44 = (f32[32,4]{1,0:T(8,128)S(1)}, f32[32,4]{1,0:T(8,128)}, u32[]{:S(2)}) copy-start(f32[32,4]{1,0:T(8,128)} %copy-done.43) | copy-start | bytes 1540
  844.6 29.7 %copy-start.53 = (f32[2048]{0:T(1024)S(1)}, f32[2048]{0:T(1024)}, u32[]{:S(2)}) copy-start(f32[2048]{0:T(1024)} %param.21) | copy-start | bytes 24580
  844.6 31.8 %copy-start.55 = (f32[2048]{0:T(1024)S(1)}, f32[2048]{0:T(1024)}, u32[]{:S(2)}) copy-start(f32[2048]{0:T(1024)} %get-tuple-element.92) | copy-start | bytes 24580
  849.7 46.6 %copy-start.9 = (f32[128,2048]{1,0:T(8,128)S(1)}, f32[128,2048]{1,0:T(8,128)}, u32[]{:S(2)}) copy-start(f32[128,2048]{1,0:T(8,128)} %copy-done.7) | copy-start | bytes 3145732
  849.7 46.6 %copy-start.69 = (f32[128]{0:T(128)S(1)}, f32[128]{0:T(128)}, u32[]{:S(2)}) copy-start(f32[128]{0:T(128)} %copy-done.68) | copy-start | bytes 1540
  877.9 14.9 %all-to-all-start.10 = ((f32[32,1,1280]{2,1,0:T(1,128)}), f32[32,1,1280]{2,1,0:T(1,128)S(1)}, u32[]{:S(2)}, u32[]{:S(2)}) async-start(f32[32,1,1280]{2,1,0:T(1,128)} %bitcast.42), calls=%async_computation.10 | async-start | bytes 327680 | tf_op jit(solution)/shard_map/all_to_all | solution.py:37
  893.7 11.1 %all-to-all-start.11 = ((f32[32,1,1280]{2,1,0:T(1,128)}), f32[32,1,1280]{2,1,0:T(1,128)S(1)}, u32[]{:S(2)}, u32[]{:S(2)}) async-start(f32[32,1,1280]{2,1,0:T(1,128)} %broadcast_in_dim.35), calls=%async_computation.11 | async-start | bytes 327680 | tf_op jit(solution)/shard_map/all_to_all | solution.py:37
  904.8 19.6 %all-to-all-start.12 = ((bf16[32,4,2048]{2,1,0:T(4,128)(2,1)}), bf16[32,4,2048]{2,1,0:T(4,128)(2,1)}, u32[]{:S(2)}, u32[]{:S(2)}) async-start(bf16[32,4,2048]{2,1,0:T(4,128)(2,1)} %reshape.365), calls=%async_computation.12 | async-start | bytes 1048576 | tf_op jit(solution)/shard_map/all_to_all | solution.py:37
  (31 other events, 74.0 us)
Sparse Core Ops, SparseCore 0:
  12.4 122.8 all-gather.7
  137.1 113.1 all-gather.9
  252.2 87.4 all-gather.5
  486.9 83.5 reduce-scatter.3
  573.4 114.3 reduce-scatter.5
  690.7 86.3 reduce-scatter.7

commit v4 on v3

--- a/solution.py
+++ b/solution.py
@@ -262,6 +262,58 @@
         return carry
 
     lax.fori_loop(0, count, drain, 0)
+
+
+def attn_reduce_kernel(count, qkv_grad, out_grad, out, parts, loads, *rest):
+    dps, _, piece, _ = qkv_grad.shape
+    part = out_grad.shape[-1] // dps
+    moves = [
+        pltpu.make_async_copy(
+            qkv_grad.at[i, :, :, pl.ds(g * part, part)],
+            parts.at[:, pl.ds(g * piece, piece), pl.ds(i * part, part)],
+            loads.at[g * dps + i],
+        )
+        for g in range(3)
+        for i in range(dps)
+    ]
+    moves.append(
+        pltpu.make_async_copy(
+            out_grad, parts.at[:, pl.ds(3 * piece, piece), :], loads.at[3 * dps]
+        )
+    )
+    for move in moves:
+        move.start()
+    for move in moves:
+        move.wait()
+    reduce_kernel(count, parts, out, *rest)
+
+
+def reduce_attn(qkv_grad, out_grad, number):
+    count = lax.axis_size("expert")
+    dps = lax.axis_size("dp")
+    width = out_grad.shape[1]
+    piece = out_grad.shape[0] // count
+    qkv_grad = qkv_grad.reshape(dps, count, piece, qkv_grad.shape[1])
+    out_grad = out_grad.reshape(count, piece, width)
+    shape = (count, 4 * piece, width)
+    return pl.pallas_call(
+        functools.partial(attn_reduce_kernel, count),
+        out_shape=jax.ShapeDtypeStruct(shape[1:], jnp.float32),
+        in_specs=[pl.BlockSpec(memory_space=pl.ANY)] * 2,
+        out_specs=pl.BlockSpec(memory_space=pltpu.VMEM),
+        scratch_shapes=[
+            pltpu.VMEM(shape, out_grad.dtype),
+            pltpu.SemaphoreType.DMA((3 * dps + 1,)),
+        ]
+        + [pltpu.VMEM(shape, out_grad.dtype)] * 2
+        + [pltpu.SemaphoreType.DMA((count,))] * 4,
+        compiler_params=pltpu.CompilerParams(
+            collective_id=number, has_side_effects=True, vmem_limit_bytes=LIMIT
+        ),
+        cost_estimate=pl.CostEstimate(
+            flops=0, bytes_accessed=30 * math.prod(shape), transcendentals=0
+        ),
+    )(qkv_grad, out_grad)
 
 
 def reduce_rows(parts, number):
@@ -288,8 +340,8 @@
     size = flat.shape[0]
     chunk = -(-size // (devices * 128)) * 128
     flat = jnp.pad(flat, (0, devices * chunk - size)).reshape(devices, chunk)
-    total = jnp.sum(swap(flat, BOTH), axis=0)
-    total = spread(total, BOTH, devices).reshape(-1)
+    flat = swap(flat, BOTH)
+    total = spread(jnp.sum(flat, axis=0), BOTH, devices).reshape(-1)
     out, at = [], 0
     for v in values:
         out.append(total[at : at + v.size].reshape(v.shape))
@@ -431,8 +483,8 @@
     my_gates = lax.dynamic_slice_in_dim(gates, my_ex * rows, rows, axis=0)
     gate_rows, up_rows, inner = [], [], []
     for e in range(local):
-        gu = dotf(feed, gate_up[e], ((1,), (0,)))
-        g, u = gu[:, :hidden], gu[:, hidden:]
+        gu = dotf(feed, gate_up[e], ((1,), (0,))).astype(bf16)
+        g, u = gu[:, :hidden].astype(f32), gu[:, hidden:].astype(f32)
         gate_rows.append(g)
         up_rows.append(u)
         inner.append((jax.nn.silu(g) * u * own_gates[:, e : e + 1]).astype(bf16))
@@ -451,12 +503,12 @@
     back_output = swap(output_rows.reshape(devices, stripe, width), BOTH)
     grad_feed = 0.0
     gate_grads, grad_gus = [], []
-    grad_inner_raw = dotf(grad_rows, down, ((1,), (1,)))
+    grad_inner_raw = dotf(grad_rows, down, ((1,), (1,))).astype(bf16)
     for e in range(local):
         g, u = gate_rows[e], up_rows[e]
         sg = jax.nn.sigmoid(g)
         silu = g * sg
-        raw = grad_inner_raw[:, e * hidden : (e + 1) * hidden]
+        raw = grad_inner_raw[:, e * hidden : (e + 1) * hidden].astype(f32)
         gate_grads.append(jnp.sum(raw * (silu * u), axis=1))
         grad_inner = raw * own_gates[:, e : e + 1]
         grad_g = grad_inner * u * sg * (1.0 + g * (1.0 - sg))
@@ -520,22 +572,15 @@
         ],
         axis=1,
     )
-    grad_normed = dotf(grad_qkv, weight_cols, ((1,), (1,))).astype(bf16)
+    grad_normed = dotf(grad_qkv, weight_cols, ((1,), (1,)))
+    grad_attn_gain = jnp.sum(grad_normed * attn_rows.astype(f32), axis=0) / attn_gain
+    grad_normed = grad_normed.astype(bf16)
     grad_normed = swap(grad_normed.reshape(dps, rows, width), "dp")
     grad_normed = jnp.sum(grad_normed.astype(f32), axis=0)
     grad_qkv_w = dotf(attn_rows, grad_qkv, ((0,), (0,))).astype(bf16)
-    grad_attn_gain = jnp.sum(grad_normed * attn_normed, axis=0)
     grad_tokens = grad_resid + norm_back(grad_normed * attn_gain, attn_normed, attn_scale)
 
-    grad_qkv_w = grad_qkv_w.reshape(dps, owners, piece, 3, part).transpose(1, 3, 2, 0, 4)
-    attn_grads = jnp.concatenate(
-        [
-            grad_qkv_w.reshape(owners, 3 * piece, width),
-            grad_out_w.reshape(owners, piece, width),
-        ],
-        axis=1,
-    )
-    attn_grads = reduce_rows(attn_grads.reshape(-1, width), 6)
+    attn_grads = reduce_attn(grad_qkv_w, grad_out_w, 6)
     out_out = attn_grads[3 * piece :]
     grad_qkv_w = attn_grads[: 3 * piece].astype(bf16).reshape(3 * piece, dps, part)
     grad_qkv_w = swap(grad_qkv_w.transpose(1, 0, 2), "dp")

time: 955 us -> 890 us (0.932)
  local copies, waits for them, and re-layouts: 152 us -> 109 us
  other arithmetic: 83 us -> 69.6 us
  waiting for transfers between devices: 150 us -> 140 us
    pallas_call x0 -> x1, Pallas kernels: none -> 73 us  [reduce_attn(): pl.pallas_call(functools.partial(attn_reduce_kernel, count), out_shape=ja...]
    pallas_call x3 -> x2, Pallas kernels: 153 us -> 81.6 us  [reduce_rows(): pl.pallas_call(functools.partial(reduce_kernel, count), out_shape=jax.Sha...]
    reshape x2 -> x0, local copies, waits for them, and re-layouts: 30.1 us -> none  [the longest x1 18.8 us: on_device(): grad_qkv_w.reshape(dps, owners, piece, 3, part).transpose(1, 3, 2, 0, 4)]
    transpose x1 -> x0, local copies, waits for them, and re-layouts: 13.5 us -> none  [on_device(): grad_qkv_w.reshape(dps, owners, piece, 3, part).transpose(1, 3, 2, 0, 4)]
    all_to_all x14, waiting for transfers between devices: 149 us -> 138 us  [swap(): return lax.all_to_all(pieces, axes, split_axis=0, concat_axis=0, tiled=True)]
    unnamed x168 -> x180, local copies, waits for them, and re-layouts: 27.6 us -> 30.7 us
  transfers between devices with their start and end apart: 20 -> 20, of which waited for: 10 -> 8; matrix products, arithmetic and copies ran while one was open for 35% -> 32% of each run, Pallas kernels for 23% -> 25%
where the time goes in v4:
time: 890 us; the launch traced here: 882 us
  Pallas kernels  307 us (34%)
  matrix products  174 us (20%)
  waiting for transfers between devices  140 us (16%)
  local copies, waits for them, and re-layouts  109 us (12%)
  other arithmetic  69.6 us (8%)
  starting transfers between devices  64.9 us (7%)
  between operations  18.2 us (2%)
    dot_general x16, matrix products, dotf(): lax.dot_general(left, right, (dims, ((), ())), preferred_element_type=jnp...  157 us
    pallas_call x3, Pallas kernels, gather_rows(): pl.pallas_call(functools.partial(gather_kernel, count), out_shape=jax.Sha...  153 us
    all_to_all x14, waiting for transfers between devices, swap(): return lax.all_to_all(pieces, axes, split_axis=0, concat_axis=0, tiled=True)  138 us
    pallas_call x2, Pallas kernels, reduce_rows(): pl.pallas_call(functools.partial(reduce_kernel, count), out_shape=jax.Sha...  81.6 us
    pallas_call x1, Pallas kernels, reduce_attn(): pl.pallas_call(functools.partial(attn_reduce_kernel, count), out_shape=ja...  73 us
    all_to_all x14, starting transfers between devices, swap(): return lax.all_to_all(pieces, axes, split_axis=0, concat_axis=0, tiled=True)  64.6 us
    unnamed x180, local copies, waits for them, and re-layouts  30.7 us
  transfers between devices with their start and end apart: 20, of which 8 were waited for; matrix products, arithmetic and copies ran while one was open for 32% of the time, Pallas kernels for 25%

profile of v4, /device:TPU:0, one launch (start us, length us, event | category | flops | bytes accessed | tf_op | source)
XLA Modules:
  0.0 881.9 jit_solution(10498164171285832002)
XLA Ops:
  7.2 5.0 fusion.109
  15.3 7.3 all-to-all-start
  24.4 14.6 %all-to-all-done = bf16[32,4,2048]{2,1,0:T(4,128)(2,1)S(1)} async-done(((bf16[32,4,2048]{2,1,0:T(4,128)(2,1)}), bf16[32,4,2048]{2,1,0:T(4,128)(2,1)S(1)}, u32[]{:S(2)}, u32[]{:S(2)}) %all-to-all-start) | async-done | bytes 524320 | tf_op jit(solution)/shard_map/all_to_all | solution.py:37
  39.8 3.3 all-to-all-start.3
  44.4 7.2 all-to-all-done.3
  51.6 4.2 all-to-all-start.2
  58.8 13.9 %all-to-all-done.2 = bf16[4,64,1536]{2,1,0:T(8,128)(2,1)} async-done(((bf16[4,64,1536]{2,1,0:T(8,128)(2,1)}), bf16[4,64,1536]{2,1,0:T(8,128)(2,1)}, u32[]{:S(2)}, u32[]{:S(2)}) %all-to-all-start.2) | async-done | bytes 786464 | tf_op jit(solution)/shard_map/all_to_all | solution.py:37
  72.7 2.6 broadcast_in_dim.24
  75.3 4.4 all-to-all-start.1
  87.4 61.1 %shard_map.238 = bf16[8,256,1536]{2,1,0:T(8,128)(2,1)} custom-call(bf16[256,1536]{1,0:T(8,128)(2,1)} %bitcast.5.block), custom_call_target="tpu_custom_call" | custom-call | bytes 94371840 | tf_op jit(solution)/shard_map/pallas_call | solution.py:135
  148.6 6.1 copy.193
  154.7 3.5 all-to-all-start.5
  158.2 6.2 fusion.115
  170.7 2.6 reshape.340
  173.3 2.6 multiply_reduce_fusion.8
  184.1 3.2 fusion.113
  187.3 3.4 fusion.47
  192.0 2.6 convolution_convert_fusion.7
  194.6 4.5 all-to-all-start.4
  204.8 42.9 %all-to-all-done.4 = bf16[4,128,2048]{2,1,0:T(8,128)(2,1)} async-done(((bf16[4,128,2048]{2,1,0:T(8,128)(2,1)}), bf16[4,128,2048]{2,1,0:T(8,128)(2,1)}, u32[]{:S(2)}, u32[]{:S(2)}) %all-to-all-start.4) | async-done | bytes 2097184 | tf_op jit(solution)/shard_map/all_to_all | solution.py:37
  247.7 3.0 convert_reduce_fusion.1
  250.7 2.5 reduce_sum.250
  255.2 2.6 multiply_convert_fusion.3
  257.8 45.0 %shard_map.239 = bf16[8,128,2048]{2,1,0:T(8,128)(2,1)} custom-call(bf16[128,2048]{1,0:T(8,128)(2,1)} %get-tuple-element.104.block), custom_call_target="tpu_custom_call" | custom-call | bytes 62914560 | tf_op jit(solution)/shard_map/pallas_call | solution.py:135
  302.8 3.4 fusion.114
  306.9 12.5 %fusion.34 = bf16[1024,2048]{1,0:T(8,128)(2,1)S(1)} fusion(bf16[1024,2048]{1,0:T(8,128)(2,1)} %bitcast.241, bf16[1,2048,2048]{2,1,0:T(8,128)(2,1)} %all-gather.10.cloned.1.call-done), kind=kOutput, calls=%fused_computation.63 | convolution fusion | flops 8592031744 | bytes 16777216 | tf_op jit(solution)/shard_map/dot_general | solution.py:33
  321.4 2.7 multiply_convert_fusion
  324.1 12.5 %fusion.31 = bf16[1024,2048]{1,0:T(8,128)(2,1)S(1)} fusion(bf16[1024,2048]{1,0:T(8,128)(2,1)} %bitcast.242, bf16[1,2048,2048]{2,1,0:T(8,128)(2,1)} %all-gather.8.cloned.1.call-done), kind=kOutput, calls=%fused_computation.62 | convolution fusion | flops 8592031744 | bytes 16777216 | tf_op jit(solution)/shard_map/dot_general | solution.py:33
  338.6 2.7 multiply_convert_fusion.1
  341.4 14.4 %convolution_convert_fusion.5 = bf16[1024,2048]{1,0:T(8,128)(2,1)} fusion(bf16[2048,2048]{1,0:T(8,128)(2,1)} %bitcast.291, bf16[1024,1024]{1,0:T(8,128)(2,1)} %multiply_convert_fusion, bf16[1024,1024]{1,0:T(8,128)(2,1)} %multiply_convert_fusion.1), kind=kOutput, calls=%fused_computation.65 | convolution fusion | flops 8600420352 | bytes 16777216 | tf_op jit(solution)/shard_map/dot_general | solution.py:33
  355.7 40.2 %shard_map.240 = f32[128,2048]{1,0:T(8,128)} custom-call(bf16[8,128,2048]{2,1,0:T(8,128)(2,1)} %bitcast.252), custom_call_target="tpu_custom_call" | custom-call | bytes 62914560 | tf_op jit(solution)/shard_map/pallas_call | solution.py:322
  395.9 3.3 fusion.49
  401.1 46.6 %shard_map.241 = bf16[8,128,2048]{2,1,0:T(8,128)(2,1)} custom-call(bf16[128,2048]{1,0:T(8,128)(2,1)} %multiply_convert_fusion.5.block), custom_call_target="tpu_custom_call" | custom-call | bytes 62914560 | tf_op jit(solution)/shard_map/pallas_call | solution.py:135
  447.7 12.7 %convolution_convert_fusion.4 = bf16[1024,2048]{1,0:T(8,128)(2,1)S(1)} fusion(bf16[1024,2048]{1,0:T(8,128)(2,1)} %bitcast.253, bf16[2048,2048]{1,0:T(8,128)(2,1)} %bitcast.292), kind=kOutput, calls=%fused_computation.64 | convolution fusion | flops 8592031744 | bytes 16777216 | tf_op jit(solution)/shard_map/dot_general | solution.py:33
  460.5 8.3 fusion.21
  470.1 12.9 %convolution_convert_fusion.1 = bf16[2048,2048]{1,0:T(8,128)(2,1)} fusion(bf16[1024,2048]{1,0:T(8,128)(2,1)S(1)} %bitcast.244, bf16[1024,1024]{1,0:T(8,128)(2,1)S(1)} %get-tuple-element.110, bf16[1024,1024]{1,0:T(8,128)(2,1)} %get-tuple-element.111), kind=kOutput, calls=%fused_computation.16 | convolution fusion | flops 8602517504 | bytes 16777216 | tf_op jit(solution)/shard_map/dot_general | solution.py:33
  483.1 14.3 %convolution_convert_fusion.2 = bf16[2048,2048]{1,0:T(8,128)(2,1)} fusion(bf16[1024,2048]{1,0:T(8,128)(2,1)} %bitcast.243, bf16[1024,1024]{1,0:T(8,128)(2,1)} %get-tuple-element.112, bf16[1024,1024]{1,0:T(8,128)(2,1)} %get-tuple-element.113), kind=kOutput, calls=%fused_computation.17 | convolution fusion | flops 8602517504 | bytes 16777216 | tf_op jit(solution)/shard_map/dot_general | solution.py:33
  498.0 3.3 all-to-all-start.7
  501.4 14.3 %convolution_convert_fusion = bf16[2048,2048]{1,0:T(8,128)(2,1)} fusion(bf16[1024,2048]{1,0:T(8,128)(2,1)} %bitcast.254, bf16[1024,1024]{1,0:T(8,128)(2,1)} %multiply_convert_fusion, bf16[1024,1024]{1,0:T(8,128)(2,1)} %multiply_convert_fusion.1), kind=kOutput, calls=%fused_computation.15 | convolution fusion | flops 8602517504 | bytes 16777216 | tf_op jit(solution)/shard_map/dot_general | solution.py:33
  515.7 15.0 %fusion.1 = f32[1024,2048]{1,0:T(8,128)} fusion(bf16[1,2048,2048]{2,1,0:T(8,128)(2,1)} %all-gather.10.cloned.1.call-done, bf16[1024,1024]{1,0:T(8,128)(2,1)} %copy-done.23, bf16[1024,1024]{1,0:T(8,128)(2,1)} %get-tuple-element.111), kind=kOutput, calls=%fused_computation.6 | convolution fusion | flops 8598323200 | bytes 20971520 | tf_op jit(solution)/shard_map/dot_general | solution.py:33
  530.7 14.6 %add_convert_fusion = bf16[1024,2048]{1,0:T(8,128)(2,1)} fusion(f32[1024,2048]{1,0:T(8,128)} %fusion.1, bf16[1,2048,2048]{2,1,0:T(8,128)(2,1)} %all-gather.8.cloned.1.call-done, bf16[1024,1024]{1,0:T(8,128)(2,1)S(1)} %copy-done.22, bf16[1024,1024]{1,0:T(8,128)(2,1)} %get-tuple-element.113), kind=kOutput, calls=%fused_computation.14 | convolution fusion | flops 8602517504 | bytes 25165824 | tf_op jit(solution)/shard_map/dot_general | solution.py:33
  545.3 41.4 %shard_map.242 = f32[128,2048]{1,0:T(8,128)} custom-call(bf16[8,128,2048]{2,1,0:T(8,128)(2,1)} %bitcast.251), custom_call_target="tpu_custom_call" | custom-call | bytes 62914560 | tf_op jit(solution)/shard_map/pallas_call | solution.py:322
  587.5 2.9 multiply_reduce_fusion.2
  590.3 2.7 fusion.107
  594.6 4.5 all-to-all-start.8
  605.7 39.1 %all-to-all-done.8 = bf16[4,128,2048]{2,1,0:T(8,128)(2,1)} async-done(((bf16[4,128,2048]{2,1,0:T(8,128)(2,1)}), bf16[4,128,2048]{2,1,0:T(8,128)(2,1)}, u32[]{:S(2)}, u32[]{:S(2)}) %all-to-all-start.8) | async-done | bytes 2097184 | tf_op jit(solution)/shard_map/all_to_all | solution.py:37
  644.8 5.1 all-to-all-start.6
  650.0 2.9 fusion.44
  663.1 3.6 fusion.48
  677.1 6.1 fusion.108
  684.7 8.3 convolution_convert_fusion.3
  693.0 6.2 all-to-all-start.9
  699.2 4.2 convolution_convert_fusion.6
  703.4 73.0 %shard_map.243 = f32[256,2048]{1,0:T(8,128)} custom-call(bf16[4,8,64,1536]{3,2,1,0:T(8,128)(2,1)} %bitcast.250, bf16[8,64,2048]{2,1,0:T(8,128)(2,1)} %bitcast.263), custom_call_target="tpu_custom_call" | custom-call | bytes 125829120 | tf_op jit(solution)/shard_map/pallas_call | solution.py:299
  779.5 3.5 all-to-all-start.13
  791.1 4.5 all-to-all-start.11
  807.2 13.6 %all-to-all-done.11 = bf16[4,128,2048]{2,1,0:T(8,128)(2,1)} async-done(((bf16[4,128,2048]{2,1,0:T(8,128)(2,1)}), bf16[4,128,2048]{2,1,0:T(8,128)(2,1)}, u32[]{:S(2)}, u32[]{:S(2)}) %all-to-all-start.11) | async-done | bytes 2097184 | tf_op jit(solution)/shard_map/all_to_all | solution.py:37
  821.6 4.3 all-to-all-start.10
  825.9 3.0 convert_reduce_fusion
  833.5 2.6 add_convert_fusion.1
  838.2 6.0 all-to-all-start.12
  854.7 5.6 all-to-all-done.12
  863.4 6.2 maximum_convert_fusion
  869.6 4.1 convert_element_type.243
  (318 shorter events, 122.4 us)
Async XLA Ops:
  7.2 184.8 %copy-start = (bf16[512,2048]{1,0:T(8,128)(2,1)S(1)}, bf16[512,2048]{1,0:T(8,128)(2,1)}, u32[]{:S(2)}) copy-start(bf16[512,2048]{1,0:T(8,128)(2,1)} %param.18) | copy-start | bytes 6291460
  7.2 299.7 %all-gather.10.cloned.1.call-start = ((), (), s32[]{:S(2)}) async-start(), calls=%async_computation.22 | async-start | bytes 10485760 | tf_op jit(solution)/shard_map/all_gather | solution.py:411
  12.3 10.4 %copy-start.73 = (s32[128,8]{0,1:T(8,128)S(1)}, s32[128,8]{0,1:T(8,128)}, u32[]{:S(2)}) copy-start(s32[128,8]{0,1:T(8,128)} %param.27) | copy-start | bytes 12292
  12.3 10.6 %copy-start.75 = (s32[1,4]{1,0:T(1,128)S(1)}, s32[1,4]{1,0:T(1,128)}, u32[]{:S(2)}) copy-start(s32[1,4]{1,0:T(1,128)} %param.29) | copy-start | bytes 52
  12.3 10.6 %copy-start.76 = (s32[128]{0:T(128)S(1)}, s32[128]{0:T(128)}, u32[]{:S(2)}) copy-start(s32[128]{0:T(128)} %param.28) | copy-start | bytes 1540
  12.3 311.8 %all-gather.8.cloned.1.call-start = ((), (), s32[]{:S(2)}) async-start(), calls=%async_computation.21 | async-start | bytes 10485760 | tf_op jit(solution)/shard_map/all_gather | solution.py:411
  13.5 10.9 %copy-start.74 = (s32[32]{0:T(128)}, s32[32]{0:T(128)S(1)}, u32[]{:S(2)}) copy-start(s32[32]{0:T(128)S(1)} %compare_select_fusion.1) | copy-start | bytes 388
  15.3 23.7 %all-to-all-start = ((bf16[32,4,2048]{2,1,0:T(4,128)(2,1)}), bf16[32,4,2048]{2,1,0:T(4,128)(2,1)S(1)}, u32[]{:S(2)}, u32[]{:S(2)}) async-start(bf16[32,4,2048]{2,1,0:T(4,128)(2,1)} %gather_fusion), calls=%async_computation | async-start | bytes 1048576 | tf_op jit(solution)/shard_map/all_to_all | solution.py:37
  22.9 34.8 %copy-start.48 = (f32[2048]{0:T(1024)S(1)}, f32[2048]{0:T(1024)}, u32[]{:S(2)}) copy-start(f32[2048]{0:T(1024)} %param.21) | copy-start | bytes 24580
  39.0 16.9 %copy-start.13 = (bf16[32,4,2048]{2,1,0:T(4,128)(2,1)}, bf16[32,4,2048]{2,1,0:T(4,128)(2,1)S(1)}, u32[]{:S(2)}) copy-start(bf16[32,4,2048]{2,1,0:T(4,128)(2,1)S(1)} %all-to-all-done) | copy-start | bytes 1572868
  39.8 11.8 %all-to-all-start.3 = ((s32[32,1,1280]{2,1,0:T(1,128)}), s32[32,1,1280]{2,1,0:T(1,128)}, u32[]{:S(2)}, u32[]{:S(2)}) async-start(s32[32,1,1280]{2,1,0:T(1,128)} %broadcast_in_dim.25), calls=%async_computation.3 | async-start | bytes 327680 | tf_op jit(solution)/shard_map/all_to_all | solution.py:37
  51.6 21.1 %all-to-all-start.2 = ((bf16[4,64,1536]{2,1,0:T(8,128)(2,1)}), bf16[4,64,1536]{2,1,0:T(8,128)(2,1)}, u32[]{:S(2)}, u32[]{:S(2)}) async-start(bf16[4,64,1536]{2,1,0:T(8,128)(2,1)} %pad_maximum_fusion.12), calls=%async_computation.2 | async-start | bytes 1572864 | tf_op jit(solution)/shard_map/all_to_all | solution.py:37
  56.6 18.8 %copy-start.71 = (f32[128]{0:T(128)}, f32[128]{0:T(128)S(1)}, u32[]{:S(2)}) copy-start(f32[128]{0:T(128)S(1)} %rsqrt.40) | copy-start | bytes 1540
  57.7 17.6 %copy-start.9 = (f32[128,2048]{1,0:T(8,128)}, f32[128,2048]{1,0:T(8,128)S(1)}, u32[]{:S(2)}) copy-start(f32[128,2048]{1,0:T(8,128)S(1)} %reshape.363) | copy-start | bytes 3145732
  75.3 79.4 %all-to-all-start.1 = ((bf16[4,128,2048]{2,1,0:T(8,128)(2,1)}), bf16[4,128,2048]{2,1,0:T(8,128)(2,1)}, u32[]{:S(2)}, u32[]{:S(2)}) async-start(bf16[4,128,2048]{2,1,0:T(8,128)(2,1)} %broadcast_in_dim.24), calls=%async_computation.1 | async-start | bytes 4194304 | tf_op jit(solution)/shard_map/all_to_all | solution.py:37
  79.8 261.6 %all-gather.6.cloned.1.call-start = ((), (), s32[]{:S(2)}) async-start(), calls=%async_computation.17 | async-start | bytes 10485760 | tf_op jit(solution)/shard_map/all_gather | solution.py:412
  87.3 92.2 %copy-start.20 = (f32[4,128,64]{2,1,0:T(8,128)}, f32[4,128,64]{2,1,0:T(8,128)S(1)}, u32[]{:S(2)}) copy-start(f32[4,128,64]{2,1,0:T(8,128)S(1)} %get-tuple-element.155) | copy-start | bytes 393220
  87.4 99.9 %copy-start.56 = (pred[4,128,128]{1,2,0:T(8,128)(4,1)}, pred[4,128,128]{1,2,0:T(8,128)(4,1)S(1)}, u32[]{:S(2)}) copy-start(pred[4,128,128]{1,2,0:T(8,128)(4,1)S(1)} %broadcast_compare_fusion) | copy-start | bytes 196612
  154.7 39.9 %all-to-all-start.5 = ((bf16[32,4,2048]{2,1,0:T(4,128)(2,1)}), bf16[32,4,2048]{2,1,0:T(4,128)(2,1)}, u32[]{:S(2)}, u32[]{:S(2)}) async-start(bf16[32,4,2048]{2,1,0:T(4,128)(2,1)} %gather_fusion.1), calls=%async_computation.5 | async-start | bytes 1048576 | tf_op jit(solution)/shard_map/all_to_all | solution.py:37
  166.7 10.8 %copy-start.68 = (f32[128]{0:T(128)S(1)}, f32[128]{0:T(128)}, u32[]{:S(2)}) copy-start(f32[128]{0:T(128)} %param.19) | copy-start | bytes 1540
  168.3 11.1 %copy-start.2 = (f32[4,128,4,128]{3,2,1,0:T(4,128)}, f32[4,128,4,128]{3,2,1,0:T(4,128)S(1)}, u32[]{:S(2)}) copy-start(f32[4,128,4,128]{3,2,1,0:T(4,128)S(1)} %reshape.339) | copy-start | bytes 3145732
  168.3 9.6 %copy-start.65 = (f32[128]{0:T(128)S(1)}, f32[128]{0:T(128)}, u32[]{:S(2)}) copy-start(f32[128]{0:T(128)} %param.20) | copy-start | bytes 1540
  181.4 9.2 %copy-start.25 = (bf16[4,128,4,64]{3,1,2,0:T(8,128)(2,1)}, bf16[4,128,4,64]{3,1,2,0:T(8,128)(2,1)S(1)}, u32[]{:S(2)}) copy-start(bf16[4,128,4,64]{3,1,2,0:T(8,128)(2,1)S(1)} %get-tuple-element.139) | copy-start | bytes 786436
  187.3 7.3 copy-start.59
  194.6 53.1 %all-to-all-start.4 = ((bf16[4,128,2048]{2,1,0:T(8,128)(2,1)}), bf16[4,128,2048]{2,1,0:T(8,128)(2,1)}, u32[]{:S(2)}, u32[]{:S(2)}) async-start(bf16[4,128,2048]{2,1,0:T(8,128)(2,1)} %bitcast.265), calls=%async_computation.4 | async-start | bytes 4194304 | tf_op jit(solution)/shard_map/all_to_all | solution.py:37
  199.1 664.3 %reduce-scatter.6.cloned.1.call-start = ((), (), s32[]{:S(2)}) async-start(), calls=%async_computation.19 | async-start | bytes 10485760 | tf_op jit(solution)/shard_map/reduce_scatter | solution.py:597
  202.6 52.6 %copy-start.10 = (f32[128,2048]{1,0:T(8,128)S(1)}, f32[128,2048]{1,0:T(8,128)}, u32[]{:S(2)}) copy-start(f32[128,2048]{1,0:T(8,128)} %copy-done.9) | copy-start | bytes 3145732
  202.6 52.6 %copy-start.54 = (f32[2048]{0:T(1024)S(1)}, f32[2048]{0:T(1024)}, u32[]{:S(2)}) copy-start(f32[2048]{0:T(1024)} %param.22) | copy-start | bytes 24580
  255.2 47.6 %copy-start.63 = (f32[128]{0:T(128)}, f32[128]{0:T(128)S(1)}, u32[]{:S(2)}) copy-start(f32[128]{0:T(128)S(1)} %rsqrt.44) | copy-start | bytes 1540
  255.2 47.6 %copy-start.43 = (bf16[2048,16]{0,1:T(8,128)(2,1)S(1)}, bf16[2048,16]{0,1:T(8,128)(2,1)}, u32[]{:S(2)}) copy-start(bf16[2048,16]{0,1:T(8,128)(2,1)} %param.23) | copy-start | bytes 196612
  355.7 40.2 %copy-start.12 = (f32[128,2048]{1,0:T(8,128)S(1)}, f32[128,2048]{1,0:T(8,128)}, u32[]{:S(2)}) copy-start(f32[128,2048]{1,0:T(8,128)} %get-tuple-element.105) | copy-start | bytes 3145732
  447.7 12.7 %copy-start.6 = (bf16[1024,2048]{1,0:T(8,128)(2,1)S(1)}, bf16[1024,2048]{1,0:T(8,128)(2,1)}, u32[]{:S(2)}) copy-start(bf16[1024,2048]{1,0:T(8,128)(2,1)} %copy-done.5) | copy-start | bytes 12582916
  447.7 12.7 %copy-start.8 = (bf16[1024,2048]{1,0:T(8,128)(2,1)S(1)}, bf16[1024,2048]{1,0:T(8,128)(2,1)}, u32[]{:S(2)}) copy-start(bf16[1024,2048]{1,0:T(8,128)(2,1)} %copy-done.7) | copy-start | bytes 12582916
  460.5 9.7 %copy-start.1 = (bf16[8,128,2048]{2,1,0:T(8,128)(2,1)S(1)}, bf16[8,128,2048]{2,1,0:T(8,128)(2,1)}, u32[]{:S(2)}) copy-start(bf16[8,128,2048]{2,1,0:T(8,128)(2,1)} %shard_map.239) | copy-start | bytes 12582916
  483.0 380.4 %reduce-scatter.4.cloned.1.call-start = ((), (), s32[]{:S(2)}) async-start(), calls=%async_computation.18 | async-start | bytes 10485760 | tf_op jit(solution)/shard_map/reduce_scatter | solution.py:597
  498.0 88.7 %all-to-all-start.7 = ((f32[8,2,128]{2,1,0:T(2,128)}), f32[8,2,128]{2,1,0:T(2,128)S(1)}, u32[]{:S(2)}, u32[]{:S(2)}) async-start(f32[8,2,128]{2,1,0:T(2,128)} %maximum_bitcast_fusion.4), calls=%async_computation.7 | async-start | bytes 16384 | tf_op jit(solution)/shard_map/all_to_all | solution.py:37
  501.3 368.2 %reduce-scatter.8.cloned.1.call-start = ((), (), s32[]{:S(2)}) async-start(), calls=%async_computation.20 | async-start | bytes 10485760 | tf_op jit(solution)/shard_map/reduce_scatter | solution.py:590
  515.7 15.0 %copy-start.22 = (bf16[1024,1024]{1,0:T(8,128)(2,1)S(1)}, bf16[1024,1024]{1,0:T(8,128)(2,1)}, u32[]{:S(2)}) copy-start(bf16[1024,1024]{1,0:T(8,128)(2,1)} %get-tuple-element.112) | copy-start | bytes 6291460
  545.3 42.2 %copy-start.44 = (bf16[2048,16]{0,1:T(8,128)(2,1)S(1)}, bf16[2048,16]{0,1:T(8,128)(2,1)}, u32[]{:S(2)}) copy-start(bf16[2048,16]{0,1:T(8,128)(2,1)} %param.23) | copy-start | bytes 196612
  545.3 42.2 %copy-start.55 = (f32[2048]{0:T(1024)S(1)}, f32[2048]{0:T(1024)}, u32[]{:S(2)}) copy-start(f32[2048]{0:T(1024)} %param.22) | copy-start | bytes 24580
  545.3 42.2 %copy-start.64 = (f32[128]{0:T(128)S(1)}, f32[128]{0:T(128)}, u32[]{:S(2)}) copy-start(f32[128]{0:T(128)} %copy-done.63) | copy-start | bytes 1540
  593.0 6.8 copy-start.53
  593.0 7.6 copy-start.51
  593.0 7.8 copy-start.24
  593.0 8.8 copy-start.17
  594.6 50.2 %all-to-all-start.8 = ((bf16[4,128,2048]{2,1,0:T(8,128)(2,1)}), bf16[4,128,2048]{2,1,0:T(8,128)(2,1)}, u32[]{:S(2)}, u32[]{:S(2)}) async-start(bf16[4,128,2048]{2,1,0:T(8,128)(2,1)} %broadcast_in_dim.30), calls=%async_computation.8 | async-start | bytes 4194304 | tf_op jit(solution)/shard_map/all_to_all | solution.py:37
  605.7 47.2 %copy-start.31 = (f32[4,4,128,128]{2,3,1,0:T(8,128)S(1)}, f32[4,4,128,128]{2,3,1,0:T(8,128)}, u32[]{:S(2)}) copy-start(f32[4,4,128,128]{2,3,1,0:T(8,128)} %get-tuple-element.157) | copy-start | bytes 3145732
  644.8 48.2 %all-to-all-start.6 = ((bf16[32,4,2048]{2,1,0:T(4,128)(2,1)}), bf16[32,4,2048]{2,1,0:T(4,128)(2,1)}, u32[]{:S(2)}, u32[]{:S(2)}) async-start(bf16[32,4,2048]{2,1,0:T(4,128)(2,1)} %reshape.347), calls=%async_computation.6 | async-start | bytes 1048576 | tf_op jit(solution)/shard_map/all_to_all | solution.py:37
  666.7 8.7 copy-start.61
  666.7 8.7 copy-start.62
  668.8 6.6 copy-start.16
  668.8 6.6 copy-start.18
  668.8 7.8 slice-start
  670.1 6.5 copy-start.39
  676.6 6.5 copy-start.40
  684.7 14.5 %copy-start.37 = (bf16[4,128,4,128]{3,2,1,0:T(4,128)(2,1)S(1)}, bf16[4,128,4,128]{3,2,1,0:T(4,128)(2,1)}, u32[]{:S(2)}) copy-start(bf16[4,128,4,128]{3,2,1,0:T(4,128)(2,1)} %copy-done.36) | copy-start | bytes 1572868
  693.0 85.9 %all-to-all-start.9 = ((f32[32,1,1280]{2,1,0:T(1,128)}), f32[32,1,1280]{2,1,0:T(1,128)S(1)}, u32[]{:S(2)}, u32[]{:S(2)}) async-start(f32[32,1,1280]{2,1,0:T(1,128)} %bitcast.41), calls=%async_computation.9 | async-start | bytes 327680 | tf_op jit(solution)/shard_map/all_to_all | solution.py:37
  779.5 11.5 %all-to-all-start.13 = ((bf16[4,192,512]{2,1,0:T(8,128)(2,1)}), bf16[4,192,512]{2,1,0:T(8,128)(2,1)S(1)}, u32[]{:S(2)}, u32[]{:S(2)}) async-start(bf16[4,192,512]{2,1,0:T(8,128)(2,1)} %bitcast.261), calls=%async_computation.13 | async-start | bytes 1572864 | tf_op jit(solution)/shard_map/all_to_all | solution.py:37
  791.1 29.8 %all-to-all-start.11 = ((bf16[4,128,2048]{2,1,0:T(8,128)(2,1)}), bf16[4,128,2048]{2,1,0:T(8,128)(2,1)}, u32[]{:S(2)}, u32[]{:S(2)}) async-start(bf16[4,128,2048]{2,1,0:T(8,128)(2,1)} %bitcast.264), calls=%async_computation.11 | async-start | bytes 4194304 | tf_op jit(solution)/shard_map/all_to_all | solution.py:37
  795.5 35.9 %copy-start.46 = (f32[32,4]{1,0:T(8,128)S(1)}, f32[32,4]{1,0:T(8,128)}, u32[]{:S(2)}) copy-start(f32[32,4]{1,0:T(8,128)} %copy-done.45) | copy-start | bytes 1540
  796.8 36.7 %copy-start.11 = (f32[128,2048]{1,0:T(8,128)S(1)}, f32[128,2048]{1,0:T(8,128)}, u32[]{:S(2)}) copy-start(f32[128,2048]{1,0:T(8,128)} %copy-done.9) | copy-start | bytes 3145732
  796.8 36.7 %copy-start.72 = (f32[128]{0:T(128)S(1)}, f32[128]{0:T(128)}, u32[]{:S(2)}) copy-start(f32[128]{0:T(128)} %copy-done.71) | copy-start | bytes 1540
  821.6 16.6 %all-to-all-start.10 = ((f32[32,1,1280]{2,1,0:T(1,128)}), f32[32,1,1280]{2,1,0:T(1,128)S(1)}, u32[]{:S(2)}, u32[]{:S(2)}) async-start(f32[32,1,1280]{2,1,0:T(1,128)} %broadcast_in_dim.35), calls=%async_computation.10 | async-start | bytes 327680 | tf_op jit(solution)/shard_map/all_to_all | solution.py:37
  838.2 22.2 %all-to-all-start.12 = ((bf16[32,4,2048]{2,1,0:T(4,128)(2,1)}), bf16[32,4,2048]{2,1,0:T(4,128)(2,1)}, u32[]{:S(2)}, u32[]{:S(2)}) async-start(bf16[32,4,2048]{2,1,0:T(4,128)(2,1)} %reshape.356), calls=%async_computation.12 | async-start | bytes 1048576 | tf_op jit(solution)/shard_map/all_to_all | solution.py:37
  (37 other events, 94.5 us)
Sparse Core Ops, SparseCore 0:
  12.4 122.8 all-gather.9
  137.7 113.1 all-gather.7
  252.8 87.4 all-gather.5
  483.2 83.5 reduce-scatter.5
  569.7 113.1 reduce-scatter.3
  685.8 87.5 reduce-scatter.7

commit v5 on v4

--- a/solution.py
+++ b/solution.py
@@ -339,7 +339,7 @@
     flat = jnp.concatenate([v.reshape(-1) for v in values])
     size = flat.shape[0]
     chunk = -(-size // (devices * 128)) * 128
-    flat = jnp.pad(flat, (0, devices * chunk - size)).reshape(devices, chunk)
+    flat = jnp.pad(flat, (0, devices * chunk - size)).reshape(devices, chunk // 128, 128)
     flat = swap(flat, BOTH)
     total = spread(jnp.sum(flat, axis=0), BOTH, devices).reshape(-1)
     out, at = [], 0
@@ -393,7 +393,7 @@
             jnp.pad(lengths[0], (0, lanes - lengths.shape[1])),
         ]
     )
-    packed = spread(packed, BOTH, devices)
+    packed = spread(packed.reshape(-1, lanes), BOTH, devices)
     packed = packed.reshape(dps, owners, -1)
     total_count = jnp.sum(packed[:, :, rows * slots : rows * slots + rows]).astype(f32)
     valid_total = jnp.maximum(total_count, 1.0)
@@ -406,9 +406,12 @@
     dealt_tokens = dealt_tokens.reshape(rows, width)
     dealt_teacher = swap(teacher.reshape(devices, stripe, width)[deal], BOTH).reshape(rows, width)
 
-    gate_up = []
-    for e in range(local):
-        gate_up.append(lax.all_gather(gate_up_weight[e], "dp", axis=0, tiled=True))
+    gate_up = lax.all_gather(
+        jnp.concatenate([gate_up_weight[e] for e in range(local)], axis=1),
+        "dp",
+        axis=0,
+        tiled=True,
+    )
     down = lax.all_gather(down_weight, "dp", axis=1, tiled=True)
     down = down.reshape(local * hidden, width)
 
@@ -481,10 +484,12 @@
     gates = gates / jnp.sum(gates, axis=1, keepdims=True)
     own_gates = lax.dynamic_slice_in_dim(gates, my_ex * local, local, axis=1)
     my_gates = lax.dynamic_slice_in_dim(gates, my_ex * rows, rows, axis=0)
+    gate_up_rows = dotf(feed, gate_up, ((1,), (0,))).astype(bf16)
     gate_rows, up_rows, inner = [], [], []
     for e in range(local):
-        gu = dotf(feed, gate_up[e], ((1,), (0,))).astype(bf16)
-        g, u = gu[:, :hidden].astype(f32), gu[:, hidden:].astype(f32)
+        at = 2 * e * hidden
+        g = gate_up_rows[:, at : at + hidden].astype(f32)
+        u = gate_up_rows[:, at + hidden : at + 2 * hidden].astype(f32)
         gate_rows.append(g)
         up_rows.append(u)
         inner.append((jax.nn.silu(g) * u * own_gates[:, e : e + 1]).astype(bf16))
@@ -501,7 +506,6 @@
     grad_rows = gather_rows(grad_result.astype(bf16), 4)
     output_rows, grad_rows = lax.optimization_barrier((result.astype(bf16), grad_rows))
     back_output = swap(output_rows.reshape(devices, stripe, width), BOTH)
-    grad_feed = 0.0
     gate_grads, grad_gus = [], []
     grad_inner_raw = dotf(grad_rows, down, ((1,), (1,))).astype(bf16)
     for e in range(local):
@@ -513,14 +517,18 @@
         grad_inner = raw * own_gates[:, e : e + 1]
         grad_g = grad_inner * u * sg * (1.0 + g * (1.0 - sg))
         grad_u = grad_inner * silu
-        grad_gu = jnp.concatenate([grad_g, grad_u], axis=1).astype(bf16)
-        grad_gus.append(grad_gu)
-        grad_feed = grad_feed + dotf(grad_gu, gate_up[e], ((1,), (1,)))
+        grad_gus += [grad_g.astype(bf16), grad_u.astype(bf16)]
+    grad_gus = jnp.concatenate(grad_gus, axis=1)
+    grad_feed = dotf(grad_gus, gate_up, ((1,), (1,))).astype(bf16)
     grad_down_w = dotf(inner, grad_rows, ((0,), (0,))).astype(bf16)
-    grad_feed = reduce_rows(grad_feed.astype(bf16), 5)
     grad_gate_up_w = []
     for e in range(local):
-        grad_gate_up_w.append(dotf(feed, grad_gus[e], ((0,), (0,))).astype(bf16))
+        at = 2 * e * hidden
+        grad_gate_up_w.append(
+            dotf(feed, grad_gus[:, at : at + 2 * hidden], ((0,), (0,))).astype(bf16)
+        )
+    grad_feed, grad_gate_up_w[0] = lax.optimization_barrier((grad_feed, grad_gate_up_w[0]))
+    grad_feed = reduce_rows(grad_feed, 5)
     gate_grad = swap(
         jnp.stack(gate_grads, axis=0).reshape(local, owners, rows).transpose(1, 0, 2), "expert"
     )

time: 890 us -> 868 us (0.975)
  waiting for transfers between devices: 140 us -> 108 us
    all_to_all x14, waiting for transfers between devices: 138 us -> 107 us  [swap(): return lax.all_to_all(pieces, axes, split_axis=0, concat_axis=0, tiled=True)]
    dot_general x16 -> x14, matrix products: 157 us -> 165 us  [dotf(): lax.dot_general(left, right, (dims, ((), ())), preferred_element_type=jnp...]
    unnamed x180 -> x175, local copies, waits for them, and re-layouts: 30.7 us -> 28.5 us
  transfers between devices with their start and end apart: 20 -> 19, of which waited for: 8 -> 8; matrix products, arithmetic and copies ran while one was open for 32% -> 33% of each run, Pallas kernels for 25% -> 26%
where the time goes in v5:
time: 868 us; the launch traced here: 860 us
  Pallas kernels  307 us (35%)
  matrix products  182 us (21%)
  waiting for transfers between devices  108 us (12%)
  local copies, waits for them, and re-layouts  106 us (12%)
  other arithmetic  74.3 us (9%)
  starting transfers between devices  64.6 us (7%)
  between operations  17.8 us (2%)
    dot_general x14, matrix products, dotf(): lax.dot_general(left, right, (dims, ((), ())), preferred_element_type=jnp...  165 us
    pallas_call x3, Pallas kernels, gather_rows(): pl.pallas_call(functools.partial(gather_kernel, count), out_shape=jax.Sha...  153 us
    all_to_all x14, waiting for transfers between devices, swap(): return lax.all_to_all(pieces, axes, split_axis=0, concat_axis=0, tiled=True)  107 us
    pallas_call x2, Pallas kernels, reduce_rows(): pl.pallas_call(functools.partial(reduce_kernel, count), out_shape=jax.Sha...  80.9 us
    pallas_call x1, Pallas kernels, reduce_attn(): pl.pallas_call(functools.partial(attn_reduce_kernel, count), out_shape=ja...  73 us
    all_to_all x14, starting transfers between devices, swap(): return lax.all_to_all(pieces, axes, split_axis=0, concat_axis=0, tiled=True)  64 us
    unnamed x175, local copies, waits for them, and re-layouts  28.5 us
  transfers between devices with their start and end apart: 19, of which 8 were waited for; matrix products, arithmetic and copies ran while one was open for 33% of the time, Pallas kernels for 26%

profile of v5, /device:TPU:0, one launch (start us, length us, event | category | flops | bytes accessed | tf_op | source)
XLA Modules:
  0.0 860.0 jit_solution(11555757279972914905)
XLA Ops:
  7.2 2.9 slice_bitcast_fusion.1
  10.2 2.5 pad_maximum_fusion
  15.7 7.3 all-to-all-start
  25.7 13.7 %all-to-all-done = bf16[32,4,2048]{2,1,0:T(4,128)(2,1)S(1)} async-done(((bf16[32,4,2048]{2,1,0:T(4,128)(2,1)}), bf16[32,4,2048]{2,1,0:T(4,128)(2,1)S(1)}, u32[]{:S(2)}, u32[]{:S(2)}) %all-to-all-start) | async-done | bytes 524320 | tf_op jit(solution)/shard_map/all_to_all | solution.py:37
  40.2 2.6 all-to-all-start.3
  45.1 7.7 all-to-all-done.3
  52.8 4.2 all-to-all-start.2
  60.0 17.7 %all-to-all-done.2 = bf16[4,64,1536]{2,1,0:T(8,128)(2,1)} async-done(((bf16[4,64,1536]{2,1,0:T(8,128)(2,1)}), bf16[4,64,1536]{2,1,0:T(8,128)(2,1)}, u32[]{:S(2)}, u32[]{:S(2)}) %all-to-all-start.2) | async-done | bytes 786464 | tf_op jit(solution)/shard_map/all_to_all | solution.py:37
  77.7 2.6 broadcast_in_dim.26
  80.3 4.4 all-to-all-start.1
  90.9 61.8 %shard_map.238 = bf16[8,256,1536]{2,1,0:T(8,128)(2,1)} custom-call(bf16[256,1536]{1,0:T(8,128)(2,1)} %bitcast.5.block), custom_call_target="tpu_custom_call" | custom-call | bytes 94371840 | tf_op jit(solution)/shard_map/pallas_call | solution.py:135
  152.7 6.2 copy.161
  158.9 3.5 all-to-all-start.5
  162.4 6.2 fusion.115
  174.9 2.6 reshape.327
  177.4 2.6 multiply_reduce_fusion.8
  188.0 3.2 fusion.113
  191.2 3.4 fusion.48
  195.9 2.6 convolution_convert_fusion.8
  198.5 4.5 all-to-all-start.4
  208.7 21.0 %all-to-all-done.4 = bf16[4,128,2048]{2,1,0:T(8,128)(2,1)} async-done(((bf16[4,128,2048]{2,1,0:T(8,128)(2,1)}), bf16[4,128,2048]{2,1,0:T(8,128)(2,1)}, u32[]{:S(2)}, u32[]{:S(2)}) %all-to-all-start.4) | async-done | bytes 2097184 | tf_op jit(solution)/shard_map/all_to_all | solution.py:37
  229.7 3.4 convert_reduce_fusion.1
  233.0 2.5 reduce_sum.250
  237.5 2.6 multiply_convert_fusion.3
  240.1 44.6 %shard_map.239 = bf16[8,128,2048]{2,1,0:T(8,128)(2,1)} custom-call(bf16[128,2048]{1,0:T(8,128)(2,1)} %get-tuple-element.96.block), custom_call_target="tpu_custom_call" | custom-call | bytes 62914560 | tf_op jit(solution)/shard_map/pallas_call | solution.py:135
  284.7 3.4 fusion.114
  288.9 21.5 %convolution_convert_fusion.4 = bf16[1024,4096]{1,0:T(8,128)(2,1)S(1)} fusion(bf16[1024,2048]{1,0:T(8,128)(2,1)} %bitcast.227, bf16[2048,4096]{1,0:T(8,128)(2,1)} %all-gather.3.cloned.1.call-done), kind=kOutput, calls=%fused_computation.18 | convolution fusion | flops 17184063488 | bytes 29360128 | tf_op jit(solution)/shard_map/dot_general | solution.py:33
  310.4 3.4 copy-done.1
  313.8 4.2 multiply_convert_fusion.1
  318.0 14.4 %convolution_convert_fusion.6 = bf16[1024,2048]{1,0:T(8,128)(2,1)} fusion(bf16[2048,2048]{1,0:T(8,128)(2,1)} %bitcast.269, bf16[1024,1024]{1,0:T(8,128)(2,1)} %get-tuple-element.107, bf16[1024,1024]{1,0:T(8,128)(2,1)} %get-tuple-element.106), kind=kOutput, calls=%fused_computation.69 | convolution fusion | flops 8600420352 | bytes 16777216 | tf_op jit(solution)/shard_map/dot_general | solution.py:33
  332.3 40.1 %shard_map.240 = f32[128,2048]{1,0:T(8,128)} custom-call(bf16[8,128,2048]{2,1,0:T(8,128)(2,1)} %bitcast.237), custom_call_target="tpu_custom_call" | custom-call | bytes 62914560 | tf_op jit(solution)/shard_map/pallas_call | solution.py:322
  372.5 3.3 fusion.50
  377.7 47.0 %shard_map.241 = bf16[8,128,2048]{2,1,0:T(8,128)(2,1)} custom-call(bf16[128,2048]{1,0:T(8,128)(2,1)} %multiply_convert_fusion.5.block), custom_call_target="tpu_custom_call" | custom-call | bytes 62914560 | tf_op jit(solution)/shard_map/pallas_call | solution.py:135
  424.7 12.6 %convolution_convert_fusion.5 = bf16[1024,2048]{1,0:T(8,128)(2,1)S(1)} fusion(bf16[1024,2048]{1,0:T(8,128)(2,1)} %bitcast.238, bf16[2048,2048]{1,0:T(8,128)(2,1)} %bitcast.270), kind=kOutput, calls=%fused_computation.68 | convolution fusion | flops 8592031744 | bytes 16777216 | tf_op jit(solution)/shard_map/dot_general | solution.py:33
  437.3 9.8 %fusion.19 = (f32[1024]{0:T(1024)S(1)}, f32[1024]{0:T(1024)S(1)}, bf16[1024,1024]{1,0:T(8,128)(2,1)S(1)}, bf16[1024,1024]{1,0:T(8,128)(2,1)S(1)}, bf16[1024,1024]{1,0:T(8,128)(2,1)}, /*index=5*/bf16[1024,1024]{1,0:T(8,128)(2,1)}) fusion(bf16[1024,2048]{1,0:T(8,128)(2,1)S(1)} %convolution_convert_fusion.5, bf16[1024,4096]{1,0:T(8,128)(2,1)} %copy-done.1, ...), kind=kLoop, calls=%fused_computation.43 | loop fusion | flops 41940992 | bytes 20987904 | tf_op jit(solution)/shard_map/reduce_sum | solution.py:516
  449.1 11.6 %convolution_convert_fusion.1 = bf16[2048,2048]{1,0:T(8,128)(2,1)} fusion(bf16[1024,2048]{1,0:T(8,128)(2,1)S(1)} %bitcast.229, bf16[1024,1024]{1,0:T(8,128)(2,1)S(1)} %get-tuple-element.102, bf16[1024,1024]{1,0:T(8,128)(2,1)S(1)} %get-tuple-element.103), kind=kOutput, calls=%fused_computation.15 | convolution fusion | flops 8602517504 | bytes 16777216 | tf_op jit(solution)/shard_map/dot_general | solution.py:33
  460.9 14.1 %convolution_convert_fusion.3 = bf16[2048,2048]{1,0:T(8,128)(2,1)} fusion(bf16[1024,2048]{1,0:T(8,128)(2,1)} %bitcast.228, bf16[1024,1024]{1,0:T(8,128)(2,1)} %get-tuple-element.104, bf16[1024,1024]{1,0:T(8,128)(2,1)} %get-tuple-element.105), kind=kOutput, calls=%fused_computation.17 | convolution fusion | flops 8602517504 | bytes 16777216 | tf_op jit(solution)/shard_map/dot_general | solution.py:33
  475.0 42.0 %fusion.35 = bf16[1024,2048]{1,0:T(8,128)(2,1)} fusion(bf16[2048,4096]{1,0:T(8,128)(2,1)} %all-gather.3.cloned.1.call-done, bf16[1024,1024]{1,0:T(8,128)(2,1)} %copy-done.19, bf16[1024,1024]{1,0:T(8,128)(2,1)} %copy-done.20, bf16[1024,1024]{1,0:T(8,128)(2,1)} %get-tuple-element.104, bf16[1024,1024]{1,0:T(8,128)(2,1)} %get-tuple-element.105), kind=kOutput, calls=%fused_computation.67 | convolution fusion | flops 17215520768 | bytes 29360128 | tf_op jit(solution)/shard_map/dot_general | solution.py:33
  517.3 14.8 %convolution_convert_fusion = bf16[2048,2048]{1,0:T(8,128)(2,1)} fusion(bf16[1024,2048]{1,0:T(8,128)(2,1)} %bitcast.239, bf16[1024,1024]{1,0:T(8,128)(2,1)} %get-tuple-element.107, bf16[1024,1024]{1,0:T(8,128)(2,1)} %get-tuple-element.106), kind=kOutput, calls=%fused_computation.14 | convolution fusion | flops 8602517504 | bytes 16777216 | tf_op jit(solution)/shard_map/dot_general | solution.py:33
  532.8 3.3 all-to-all-start.7
  536.1 40.8 %shard_map.242 = f32[128,2048]{1,0:T(8,128)} custom-call(bf16[8,128,2048]{2,1,0:T(8,128)(2,1)} %bitcast.236), custom_call_target="tpu_custom_call" | custom-call | bytes 62914560 | tf_op jit(solution)/shard_map/pallas_call | solution.py:322
  577.7 2.8 multiply_reduce_fusion.2
  580.5 2.6 fusion.108
  584.6 4.5 all-to-all-start.8
  595.7 26.9 %all-to-all-done.8 = bf16[4,128,2048]{2,1,0:T(8,128)(2,1)} async-done(((bf16[4,128,2048]{2,1,0:T(8,128)(2,1)}), bf16[4,128,2048]{2,1,0:T(8,128)(2,1)}, u32[]{:S(2)}, u32[]{:S(2)}) %all-to-all-start.8) | async-done | bytes 2097184 | tf_op jit(solution)/shard_map/all_to_all | solution.py:37
  622.6 5.9 all-to-all-start.6
  628.5 3.4 fusion.45
  642.2 3.8 fusion.49
  656.1 6.1 fusion.109
  663.8 8.3 convolution_convert_fusion.2
  672.1 5.6 all-to-all-start.9
  677.7 4.3 convolution_convert_fusion.7
  682.0 73.0 %shard_map.243 = f32[256,2048]{1,0:T(8,128)} custom-call(bf16[4,8,64,1536]{3,2,1,0:T(8,128)(2,1)} %bitcast.235, bf16[8,64,2048]{2,1,0:T(8,128)(2,1)} %bitcast.248), custom_call_target="tpu_custom_call" | custom-call | bytes 125829120 | tf_op jit(solution)/shard_map/pallas_call | solution.py:299
  758.2 3.7 all-to-all-start.13
  769.9 4.5 all-to-all-start.11
  784.5 15.3 %all-to-all-done.11 = bf16[4,128,2048]{2,1,0:T(8,128)(2,1)} async-done(((bf16[4,128,2048]{2,1,0:T(8,128)(2,1)}), bf16[4,128,2048]{2,1,0:T(8,128)(2,1)}, u32[]{:S(2)}, u32[]{:S(2)}) %all-to-all-start.11) | async-done | bytes 2097184 | tf_op jit(solution)/shard_map/all_to_all | solution.py:37
  800.5 3.9 all-to-all-start.10
  804.3 3.0 convert_reduce_fusion
  807.4 2.5 reduce_sum.272
  812.0 2.6 add_convert_fusion
  816.6 6.0 all-to-all-start.12
  835.0 3.9 all-to-all-done.12
  841.9 6.2 maximum_convert_fusion
  848.1 4.1 convert_element_type.253
  (311 shorter events, 117.0 us)
Async XLA Ops:
  7.2 188.7 %copy-start = (bf16[512,2048]{1,0:T(8,128)(2,1)S(1)}, bf16[512,2048]{1,0:T(8,128)(2,1)}, u32[]{:S(2)}) copy-start(bf16[512,2048]{1,0:T(8,128)(2,1)} %param.18) | copy-start | bytes 6291460
  7.2 281.7 %all-gather.3.cloned.1.call-start = ((), (), s32[]{:S(2)}) async-start(), calls=%async_computation.17 | async-start | bytes 20971520 | tf_op jit(solution)/shard_map/all_gather | solution.py:409
  12.7 10.4 %copy-start.71 = (s32[128,8]{0,1:T(8,128)S(1)}, s32[128,8]{0,1:T(8,128)}, u32[]{:S(2)}) copy-start(s32[128,8]{0,1:T(8,128)} %param.27) | copy-start | bytes 12292
  12.7 10.6 %copy-start.73 = (s32[1,4]{1,0:T(1,128)S(1)}, s32[1,4]{1,0:T(1,128)}, u32[]{:S(2)}) copy-start(s32[1,4]{1,0:T(1,128)} %param.29) | copy-start | bytes 52
  12.7 10.6 %copy-start.74 = (s32[128]{0:T(128)S(1)}, s32[128]{0:T(128)}, u32[]{:S(2)}) copy-start(s32[128]{0:T(128)} %param.28) | copy-start | bytes 1540
  14.0 26.2 %copy-start.72 = (s32[32]{0:T(128)}, s32[32]{0:T(128)S(1)}, u32[]{:S(2)}) copy-start(s32[32]{0:T(128)S(1)} %compare_select_fusion.1) | copy-start | bytes 388
  15.7 23.7 %all-to-all-start = ((bf16[32,4,2048]{2,1,0:T(4,128)(2,1)}), bf16[32,4,2048]{2,1,0:T(4,128)(2,1)S(1)}, u32[]{:S(2)}, u32[]{:S(2)}) async-start(bf16[32,4,2048]{2,1,0:T(4,128)(2,1)} %gather_fusion), calls=%async_computation | async-start | bytes 1048576 | tf_op jit(solution)/shard_map/all_to_all | solution.py:37
  24.9 34.0 %copy-start.46 = (f32[2048]{0:T(1024)S(1)}, f32[2048]{0:T(1024)}, u32[]{:S(2)}) copy-start(f32[2048]{0:T(1024)} %param.21) | copy-start | bytes 24580
  39.4 17.6 %copy-start.10 = (bf16[32,4,2048]{2,1,0:T(4,128)(2,1)}, bf16[32,4,2048]{2,1,0:T(4,128)(2,1)S(1)}, u32[]{:S(2)}) copy-start(bf16[32,4,2048]{2,1,0:T(4,128)(2,1)S(1)} %all-to-all-done) | copy-start | bytes 1572868
  40.2 12.6 %all-to-all-start.3 = ((s32[32,10,128]{2,1,0:T(8,128)}), s32[32,10,128]{2,1,0:T(8,128)S(1)}, u32[]{:S(2)}, u32[]{:S(2)}) async-start(s32[32,10,128]{2,1,0:T(8,128)} %broadcast_in_dim.28), calls=%async_computation.3 | async-start | bytes 524288 | tf_op jit(solution)/shard_map/all_to_all | solution.py:37
  52.8 24.9 %all-to-all-start.2 = ((bf16[4,64,1536]{2,1,0:T(8,128)(2,1)}), bf16[4,64,1536]{2,1,0:T(8,128)(2,1)}, u32[]{:S(2)}, u32[]{:S(2)}) async-start(bf16[4,64,1536]{2,1,0:T(8,128)(2,1)} %pad_maximum_fusion.7), calls=%async_computation.2 | async-start | bytes 1572864 | tf_op jit(solution)/shard_map/all_to_all | solution.py:37
  57.7 22.5 %copy-start.69 = (f32[128]{0:T(128)}, f32[128]{0:T(128)S(1)}, u32[]{:S(2)}) copy-start(f32[128]{0:T(128)S(1)} %rsqrt.40) | copy-start | bytes 1540
  58.9 21.4 %copy-start.6 = (f32[128,2048]{1,0:T(8,128)}, f32[128,2048]{1,0:T(8,128)S(1)}, u32[]{:S(2)}) copy-start(f32[128,2048]{1,0:T(8,128)S(1)} %reshape.351) | copy-start | bytes 3145732
  80.3 78.6 %all-to-all-start.1 = ((bf16[4,128,2048]{2,1,0:T(8,128)(2,1)}), bf16[4,128,2048]{2,1,0:T(8,128)(2,1)}, u32[]{:S(2)}, u32[]{:S(2)}) async-start(bf16[4,128,2048]{2,1,0:T(8,128)(2,1)} %broadcast_in_dim.26), calls=%async_computation.1 | async-start | bytes 4194304 | tf_op jit(solution)/shard_map/all_to_all | solution.py:37
  84.7 233.2 %all-gather.5.cloned.1.call-start = ((), (), s32[]{:S(2)}) async-start(), calls=%async_computation.18 | async-start | bytes 10485760 | tf_op jit(solution)/shard_map/all_gather | solution.py:415
  88.5 70.3 %copy-start.40 = (s32[4,8,1280]{2,1,0:T(8,128)}, s32[4,8,1280]{2,1,0:T(8,128)S(1)}, u32[]{:S(2)}) copy-start(s32[4,8,1280]{2,1,0:T(8,128)S(1)} %reshape.325) | copy-start | bytes 491524
  89.0 102.2 %copy-start.54 = (pred[4,128,128]{1,2,0:T(8,128)(4,1)}, pred[4,128,128]{1,2,0:T(8,128)(4,1)S(1)}, u32[]{:S(2)}) copy-start(pred[4,128,128]{1,2,0:T(8,128)(4,1)S(1)} %broadcast_compare_fusion) | copy-start | bytes 196612
  90.9 92.7 %copy-start.17 = (f32[4,128,64]{2,1,0:T(8,128)}, f32[4,128,64]{2,1,0:T(8,128)S(1)}, u32[]{:S(2)}) copy-start(f32[4,128,64]{2,1,0:T(8,128)S(1)} %get-tuple-element.149) | copy-start | bytes 393220
  158.9 39.7 %all-to-all-start.5 = ((bf16[32,4,2048]{2,1,0:T(4,128)(2,1)}), bf16[32,4,2048]{2,1,0:T(4,128)(2,1)}, u32[]{:S(2)}, u32[]{:S(2)}) async-start(bf16[32,4,2048]{2,1,0:T(4,128)(2,1)} %gather_fusion.1), calls=%async_computation.5 | async-start | bytes 1048576 | tf_op jit(solution)/shard_map/all_to_all | solution.py:37
  170.9 10.8 %copy-start.66 = (f32[128]{0:T(128)S(1)}, f32[128]{0:T(128)}, u32[]{:S(2)}) copy-start(f32[128]{0:T(128)} %param.19) | copy-start | bytes 1540
  172.5 11.1 %copy-start.3 = (f32[4,128,4,128]{3,2,1,0:T(4,128)}, f32[4,128,4,128]{3,2,1,0:T(4,128)S(1)}, u32[]{:S(2)}) copy-start(f32[4,128,4,128]{3,2,1,0:T(4,128)S(1)} %reshape.326) | copy-start | bytes 3145732
  172.5 9.5 %copy-start.63 = (f32[128]{0:T(128)S(1)}, f32[128]{0:T(128)}, u32[]{:S(2)}) copy-start(f32[128]{0:T(128)} %param.20) | copy-start | bytes 1540
  185.6 8.9 %copy-start.22 = (bf16[4,128,4,64]{3,1,2,0:T(8,128)(2,1)}, bf16[4,128,4,64]{3,1,2,0:T(8,128)(2,1)S(1)}, u32[]{:S(2)}) copy-start(bf16[4,128,4,64]{3,1,2,0:T(8,128)(2,1)S(1)} %get-tuple-element.133) | copy-start | bytes 786436
  191.2 7.3 copy-start.57
  198.5 31.2 %all-to-all-start.4 = ((bf16[4,128,2048]{2,1,0:T(8,128)(2,1)}), bf16[4,128,2048]{2,1,0:T(8,128)(2,1)}, u32[]{:S(2)}, u32[]{:S(2)}) async-start(bf16[4,128,2048]{2,1,0:T(8,128)(2,1)} %bitcast.250), calls=%async_computation.4 | async-start | bytes 4194304 | tf_op jit(solution)/shard_map/all_to_all | solution.py:37
  203.0 638.9 %reduce-scatter.6.cloned.1.call-start = ((), (), s32[]{:S(2)}) async-start(), calls=%async_computation.20 | async-start | bytes 10485760 | tf_op jit(solution)/shard_map/reduce_scatter | solution.py:605
  206.5 30.9 %copy-start.7 = (f32[128,2048]{1,0:T(8,128)S(1)}, f32[128,2048]{1,0:T(8,128)}, u32[]{:S(2)}) copy-start(f32[128,2048]{1,0:T(8,128)} %copy-done.6) | copy-start | bytes 3145732
  206.5 30.9 %copy-start.52 = (f32[2048]{0:T(1024)S(1)}, f32[2048]{0:T(1024)}, u32[]{:S(2)}) copy-start(f32[2048]{0:T(1024)} %param.22) | copy-start | bytes 24580
  237.5 47.2 %copy-start.61 = (f32[128]{0:T(128)}, f32[128]{0:T(128)S(1)}, u32[]{:S(2)}) copy-start(f32[128]{0:T(128)S(1)} %rsqrt.44) | copy-start | bytes 1540
  237.5 47.2 %copy-start.41 = (bf16[2048,16]{0,1:T(8,128)(2,1)S(1)}, bf16[2048,16]{0,1:T(8,128)(2,1)}, u32[]{:S(2)}) copy-start(bf16[2048,16]{0,1:T(8,128)(2,1)} %param.23) | copy-start | bytes 196612
  332.3 40.1 %copy-start.9 = (f32[128,2048]{1,0:T(8,128)S(1)}, f32[128,2048]{1,0:T(8,128)}, u32[]{:S(2)}) copy-start(f32[128,2048]{1,0:T(8,128)} %get-tuple-element.97) | copy-start | bytes 3145732
  437.3 11.8 %copy-start.2 = (bf16[8,128,2048]{2,1,0:T(8,128)(2,1)S(1)}, bf16[8,128,2048]{2,1,0:T(8,128)(2,1)}, u32[]{:S(2)}) copy-start(bf16[8,128,2048]{2,1,0:T(8,128)(2,1)} %shard_map.239) | copy-start | bytes 12582916
  460.7 381.2 %reduce-scatter.4.cloned.1.call-start = ((), (), s32[]{:S(2)}) async-start(), calls=%async_computation.19 | async-start | bytes 10485760 | tf_op jit(solution)/shard_map/reduce_scatter | solution.py:605
  517.0 331.0 %reduce-scatter.8.cloned.1.call-start = ((), (), s32[]{:S(2)}) async-start(), calls=%async_computation.21 | async-start | bytes 10485760 | tf_op jit(solution)/shard_map/reduce_scatter | solution.py:598
  532.1 45.5 %copy-start.42 = (bf16[2048,16]{0,1:T(8,128)(2,1)S(1)}, bf16[2048,16]{0,1:T(8,128)(2,1)}, u32[]{:S(2)}) copy-start(bf16[2048,16]{0,1:T(8,128)(2,1)} %param.23) | copy-start | bytes 196612
  532.1 45.5 %copy-start.53 = (f32[2048]{0:T(1024)S(1)}, f32[2048]{0:T(1024)}, u32[]{:S(2)}) copy-start(f32[2048]{0:T(1024)} %param.22) | copy-start | bytes 24580
  532.2 45.5 %copy-start.62 = (f32[128]{0:T(128)S(1)}, f32[128]{0:T(128)}, u32[]{:S(2)}) copy-start(f32[128]{0:T(128)} %copy-done.61) | copy-start | bytes 1540
  532.8 44.1 %all-to-all-start.7 = ((f32[8,2,128]{2,1,0:T(2,128)}), f32[8,2,128]{2,1,0:T(2,128)S(1)}, u32[]{:S(2)}, u32[]{:S(2)}) async-start(f32[8,2,128]{2,1,0:T(2,128)} %maximum_bitcast_fusion.4), calls=%async_computation.7 | async-start | bytes 16384 | tf_op jit(solution)/shard_map/all_to_all | solution.py:37
  583.0 6.7 copy-start.51
  583.0 7.6 copy-start.49
  583.0 7.8 copy-start.21
  583.0 8.8 %copy-start.14 = (bf16[128,2048]{1,0:T(8,128)(2,1)S(1)}, bf16[128,2048]{1,0:T(8,128)(2,1)}, u32[]{:S(2)}) copy-start(bf16[128,2048]{1,0:T(8,128)(2,1)} %get-tuple-element.96.block) | copy-start | bytes 1572868
  584.6 37.9 %all-to-all-start.8 = ((bf16[4,128,2048]{2,1,0:T(8,128)(2,1)}), bf16[4,128,2048]{2,1,0:T(8,128)(2,1)}, u32[]{:S(2)}, u32[]{:S(2)}) async-start(bf16[4,128,2048]{2,1,0:T(8,128)(2,1)} %broadcast_in_dim.37), calls=%async_computation.8 | async-start | bytes 4194304 | tf_op jit(solution)/shard_map/all_to_all | solution.py:37
  595.7 36.3 %copy-start.28 = (f32[4,4,128,128]{2,3,1,0:T(8,128)S(1)}, f32[4,4,128,128]{2,3,1,0:T(8,128)}, u32[]{:S(2)}) copy-start(f32[4,4,128,128]{2,3,1,0:T(8,128)} %get-tuple-element.151) | copy-start | bytes 3145732
  622.6 49.5 %all-to-all-start.6 = ((bf16[32,4,2048]{2,1,0:T(4,128)(2,1)}), bf16[32,4,2048]{2,1,0:T(4,128)(2,1)}, u32[]{:S(2)}, u32[]{:S(2)}) async-start(bf16[32,4,2048]{2,1,0:T(4,128)(2,1)} %reshape.334), calls=%async_computation.6 | async-start | bytes 1048576 | tf_op jit(solution)/shard_map/all_to_all | solution.py:37
  646.0 8.4 copy-start.59
  646.0 8.4 copy-start.60
  648.2 6.3 copy-start.13
  648.2 6.3 copy-start.15
  649.4 6.2 copy-start.37
  649.5 6.2 slice-start
  655.6 6.6 copy-start.38
  655.6 6.6 copy-start.39
  656.1 6.1 copy-start.55
  663.8 13.9 %copy-start.35 = (bf16[4,128,4,128]{3,2,1,0:T(4,128)(2,1)S(1)}, bf16[4,128,4,128]{3,2,1,0:T(4,128)(2,1)}, u32[]{:S(2)}) copy-start(bf16[4,128,4,128]{3,2,1,0:T(4,128)(2,1)} %copy-done.34) | copy-start | bytes 1572868
  672.1 85.4 %all-to-all-start.9 = ((f32[32,10,128]{2,1,0:T(8,128)}), f32[32,10,128]{2,1,0:T(8,128)S(1)}, u32[]{:S(2)}, u32[]{:S(2)}) async-start(f32[32,10,128]{2,1,0:T(8,128)} %reshape.340), calls=%async_computation.9 | async-start | bytes 524288 | tf_op jit(solution)/shard_map/all_to_all | solution.py:37
  758.2 11.7 %all-to-all-start.13 = ((bf16[4,192,512]{2,1,0:T(8,128)(2,1)}), bf16[4,192,512]{2,1,0:T(8,128)(2,1)S(1)}, u32[]{:S(2)}, u32[]{:S(2)}) async-start(bf16[4,192,512]{2,1,0:T(8,128)(2,1)} %bitcast.246), calls=%async_computation.13 | async-start | bytes 1572864 | tf_op jit(solution)/shard_map/all_to_all | solution.py:37
  769.9 6.4 copy-start.16
  769.9 29.8 %all-to-all-start.11 = ((bf16[4,128,2048]{2,1,0:T(8,128)(2,1)}), bf16[4,128,2048]{2,1,0:T(8,128)(2,1)}, u32[]{:S(2)}, u32[]{:S(2)}) async-start(bf16[4,128,2048]{2,1,0:T(8,128)(2,1)} %bitcast.249), calls=%async_computation.11 | async-start | bytes 4194304 | tf_op jit(solution)/shard_map/all_to_all | solution.py:37
  774.4 35.4 %copy-start.44 = (f32[32,4]{1,0:T(8,128)S(1)}, f32[32,4]{1,0:T(8,128)}, u32[]{:S(2)}) copy-start(f32[32,4]{1,0:T(8,128)} %copy-done.43) | copy-start | bytes 1540
  777.0 34.9 %copy-start.8 = (f32[128,2048]{1,0:T(8,128)S(1)}, f32[128,2048]{1,0:T(8,128)}, u32[]{:S(2)}) copy-start(f32[128,2048]{1,0:T(8,128)} %copy-done.6) | copy-start | bytes 3145732
  777.0 34.9 %copy-start.70 = (f32[128]{0:T(128)S(1)}, f32[128]{0:T(128)}, u32[]{:S(2)}) copy-start(f32[128]{0:T(128)} %copy-done.69) | copy-start | bytes 1540
  800.5 16.2 %all-to-all-start.10 = ((f32[32,10,128]{2,1,0:T(8,128)}), f32[32,10,128]{2,1,0:T(8,128)S(1)}, u32[]{:S(2)}, u32[]{:S(2)}) async-start(f32[32,10,128]{2,1,0:T(8,128)} %broadcast_in_dim.38), calls=%async_computation.10 | async-start | bytes 524288 | tf_op jit(solution)/shard_map/all_to_all | solution.py:37
  816.6 22.2 %all-to-all-start.12 = ((bf16[32,4,2048]{2,1,0:T(4,128)(2,1)}), bf16[32,4,2048]{2,1,0:T(4,128)(2,1)}, u32[]{:S(2)}, u32[]{:S(2)}) async-start(bf16[32,4,2048]{2,1,0:T(4,128)(2,1)} %reshape.344), calls=%async_computation.12 | async-start | bytes 1048576 | tf_op jit(solution)/shard_map/all_to_all | solution.py:37
  (34 other events, 78.7 us)
Sparse Core Ops, SparseCore 0:
  12.9 206.4 all-gather.2
  221.2 85.2 all-gather.4
  460.8 83.5 reduce-scatter.5
  547.3 113.4 reduce-scatter.3
  663.7 89.0 reduce-scatter.7
